TPU v7x, 16 devices: a whole 2x2x2 slice. The times are simulated.
16 devices in a mesh: dp: 4 (over z, y), tp: 4 (over x, core).
Axes of the slice: x: 2, y: 2, z: 2, core: 2. Of those that a mesh axis runs over, the one named last changes fastest.
Arguments:
- latents: bfloat16 [32, 24, 24, 1280], P('dp', 'tp'), parts along dimension 0
- context: bfloat16 [32, 77, 1024], P('dp'), parts along dimension 0
- io_vecs: float32 [4, 1280], replicated
- w_proj: bfloat16 [2, 1280, 1280], replicated
- block_vecs: float32 [2, 9, 1280], replicated
- w_qkv: bfloat16 [2, 1280, 3, 20, 64], P(None, None, None, 'tp')
- w_o1: bfloat16 [2, 20, 64, 1280], P(None, 'tp')
- w_q2: bfloat16 [2, 1280, 20, 64], P(None, None, 'tp')
- w_kv2: bfloat16 [2, 1024, 2, 20, 64], P(None, None, None, 'tp')
- w_o2: bfloat16 [2, 20, 64, 1280], P(None, 'tp')
- w_ff1: bfloat16 [2, 1280, 2, 5120], P(None, None, None, 'tp')
- b_ff1: float32 [2, 2, 5120], P(None, None, 'tp')
- w_ff2: bfloat16 [2, 5120, 1280], P(None, 'tp')
Outputs:
- output: bfloat16 [32, 24, 24, 1280], P('dp', 'tp'), parts along dimension 0
There are 4 independent parts. A program takes and returns all parts, laid end to end along the dimension named above; an argument that names none is the same for every part.
All inputs are finite; a program needn't handle non-finite values.
Results may differ from a plain program's by a relative error of at most 0.0161513.
Values are sent between devices in bfloat16 or wider.
A program may use at most 1 GiB of HBM per device.

v0:
```python
import functools

import jax
import jax.numpy as jnp
from jax import lax
from jax.experimental import pallas as pl
from jax.experimental.pallas import tpu as pltpu
from jax.sharding import PartitionSpec as P


GROUPS = 32
GN_EPS = 1e-6
LN_EPS = 1e-5
SHARDS = 4
HEAD = 64
LOG2E = 1.4426950408889634
F32 = jnp.float32
BF16 = jnp.bfloat16
NT = (((1,), (1,)), ((), ()))
VMEM_LIMIT = 50 * 1024 * 1024


def layer_norm(hidden, ln_gain, ln_shift):
    average = jnp.mean(hidden, axis=-1, keepdims=True)
    centered = hidden - average
    variance = jnp.mean(centered * centered, axis=-1, keepdims=True)
    return (centered * lax.rsqrt(variance + LN_EPS) * ln_gain + ln_shift).astype(BF16)


def attend(q, k, v):
    scores = lax.dot_general(q, k, NT, preferred_element_type=F32)
    top = jnp.max(scores, axis=-1, keepdims=True)
    probs = jnp.exp2((scores - top) * (HEAD ** -0.5 * LOG2E)).astype(BF16)
    values = jnp.concatenate([v, jnp.ones_like(v)], axis=1)
    mixed = jnp.dot(probs, values, preferred_element_type=F32)
    return (mixed[:, :HEAD] / mixed[:, HEAD:]).astype(BF16)


def in_kernel(x0, x1, x2, x3, w_ref, io_ref, ln_ref, h_out, a_out):
    tok, channels = x0.shape[1:]
    parts = [ref[0].astype(F32) for ref in (x0, x1, x2, x3)]
    size = channels // GROUPS
    count = len(parts) * tok * size
    lanes = 128
    row = lax.broadcasted_iota(jnp.int32, (channels, lanes), 0)
    first = lax.broadcasted_iota(jnp.int32, (channels, lanes), 1) * size
    member = ((row >= first) & (row < first + size)).astype(F32)

    def group_average(columns):
        per_group = jnp.dot(jnp.broadcast_to(columns, (8, channels)), member,
                            precision=lax.Precision.HIGHEST, preferred_element_type=F32) / count
        return lax.dot_general(per_group, member, NT, precision=lax.Precision.HIGHEST,
                               preferred_element_type=F32)[0:1]

    mean = group_average(sum(jnp.sum(p, axis=0, keepdims=True) for p in parts))
    var = group_average(sum(jnp.sum((p - mean) * (p - mean), axis=0, keepdims=True) for p in parts))
    inverse = lax.rsqrt(var + GN_EPS)
    for i, p in enumerate(parts):
        normed = ((p - mean) * inverse * io_ref[0:1] + io_ref[1:2]).astype(BF16)
        h = jnp.dot(normed, w_ref[0], preferred_element_type=F32) + io_ref[2:3]
        h_out[0, i * tok:(i + 1) * tok, :] = h
        a_out[0, i * tok:(i + 1) * tok, :] = layer_norm(h, ln_ref[0:1], ln_ref[1:2])


def flat(ref):
    value = ref[...]
    return value.reshape(-1, value.shape[-1])


def self_kernel(a_ref, w_ref, o_ref):
    width = o_ref.shape[-1]
    qkv = lax.dot_general(a_ref[0], flat(w_ref), NT, preferred_element_type=F32).astype(BF16)
    for head in range(width // HEAD):
        lo = head * HEAD
        o_ref[0, :, lo:lo + HEAD] = attend(
            qkv[:, lo:lo + HEAD], qkv[:, width + lo:width + lo + HEAD],
            qkv[:, 2 * width + lo:2 * width + lo + HEAD])


def row_copies(own, sib, rest, rest_sib, layer, slot, dst, sem):
    width = own.shape[1]
    pieces = rest.shape[0]
    rows = width // pieces
    pairs = [(ref.at[layer], dst.at[pl.ds(i * width, width)]) for i, ref in enumerate((own, sib))]
    for i, ref in ((2, rest), (3, rest_sib)):
        pairs += [(ref.at[d, pl.ds(slot * rows, rows)], dst.at[pl.ds(i * width + d * rows, rows)]) for d in range(pieces)]
    return [pltpu.make_async_copy(src, to, sem) for src, to in pairs]


def mid_kernel(valid, layer, slot, h_ref, o0, o1, o2, o3, kv0, kv1, kv2, kv3, vec_ref,
               o1_own, o1_sib, q2_own, q2_sib, o2_own, o2_sib, rest, rest_sib,
               h_out, a_out, o_all, w_out1, w_q, w_out2, k_scr, v_scr, p_scr, sems):
    step = pl.program_id(0)
    width = o0.shape[-1]
    heads = width // HEAD
    keys = kv0.shape[2]
    lanes = 128
    group = k_scr.shape[2] // HEAD
    cols = group * HEAD
    copies = [row_copies(own, sib, rest, rest_sib, layer, slot + i, dst, sems.at[i]) for i, (own, sib, dst) in enumerate(
        ((o1_own, o1_sib, w_out1), (q2_own, q2_sib, w_q), (o2_own, o2_sib, w_out2)))]

    def wait(i):
        @pl.when(step == 0)
        def _():
            for copy in copies[i]:
                copy.wait()

    @pl.when(step == 0)
    def _():
        for some in copies:
            for copy in some:
                copy.start()
        k_scr[...] = jnp.zeros_like(k_scr)
        v_scr[...] = jnp.zeros_like(v_scr)

    @pl.when(step % 2 == 0)
    def _():
        live = lax.broadcasted_iota(jnp.int32, (keys, HEAD), 0) < valid
        for shard, ref in enumerate((kv0, kv1, kv2, kv3)):
            kv = ref[0, 0]
            for head in range(heads):
                place = shard * heads + head
                g, r = place // group, place % group
                rows = slice(r * lanes, r * lanes + keys)
                at = slice(r * HEAD, (r + 1) * HEAD)
                k_scr[g, rows, at] = kv[:, head * HEAD:(head + 1) * HEAD]
                v_scr[g, rows, at] = kv[:, width + head * HEAD:width + (head + 1) * HEAD]
                v_scr[g, rows, cols + r * HEAD:cols + (r + 1) * HEAD] = live.astype(BF16)

    for i, o_ref in enumerate((o0, o1, o2, o3)):
        o_all[:, i * width:(i + 1) * width] = o_ref[0]
    wait(0)
    h = h_ref[0] + jnp.dot(o_all[...], w_out1[...], preferred_element_type=F32) + vec_ref[0:1]
    act = layer_norm(h, vec_ref[1:2], vec_ref[2:3])
    wait(1)
    q = lax.dot_general(act, w_q[...], NT, preferred_element_type=F32).astype(BF16)
    live = lax.broadcasted_iota(jnp.int32, (q.shape[0], lanes), 1) < valid
    for g in range(k_scr.shape[0]):
        at = slice(g * cols, (g + 1) * cols)
        scores = lax.dot_general(q[:, at], k_scr[g], NT, preferred_element_type=F32)
        for r in range(group):
            sl = slice(r * lanes, (r + 1) * lanes)
            s = jnp.where(live, scores[:, sl], -jnp.inf)
            top = jnp.max(s, axis=-1, keepdims=True)
            p_scr[g, :, sl] = jnp.exp2((s - top) * (HEAD ** -0.5 * LOG2E)).astype(BF16)
        mixed = jnp.dot(p_scr[g], v_scr[g], preferred_element_type=F32)
        o_all[:, at] = (mixed[:, :cols] / mixed[:, cols:]).astype(BF16)
    wait(2)
    h = h + jnp.dot(o_all[...], w_out2[...], preferred_element_type=F32) + vec_ref[3:4]
    h_out[0] = h
    a_out[0] = layer_norm(h, vec_ref[4:5], vec_ref[5:6])


FF_COLS = 256


def ff_copies(layer, shards, w1, w2, sems):
    ff = w1.shape[3]
    chunks = ff // FF_COLS
    first, second = [], []
    for n, refs in enumerate(shards):
        for j in range(chunks):
            at = pl.ds(j * FF_COLS, FF_COLS)
            if len(refs) == 2:
                first.append([(refs[0].at[layer, :, :, at], w1.at[n, :, :, at])])
            else:
                rows = refs[0].shape[2]
                first.append([(refs[0].at[d, pl.ds(0, 2), :, at], w1.at[n, :, pl.ds(d * rows, rows), at])
                              for d in range(refs[0].shape[0])])
        if len(refs) == 2:
            second.append([(refs[1].at[layer], w2.at[pl.ds(n * ff, ff)])])
        else:
            rows = refs[0].shape[2]
            second.append([(refs[0].at[d, 2], w2.at[pl.ds(n * ff + d * rows, rows)]) for d in range(refs[0].shape[0])])
    return [[pltpu.make_async_copy(src, to, sems.at[i]) for src, to in pairs] for i, pairs in enumerate(first + second)]


def ff_steps(layer, a_ref, biases, shards, w1, w2, m_scr, sems, finish):
    step = pl.program_id(0)
    groups = ff_copies(layer, shards, w1, w2, sems)
    ff = w1.shape[3]
    chunks = ff // FF_COLS
    ahead = 2

    def start(i):
        for copy in groups[i] if i < len(groups) else ():
            copy.start()

    def run(first):
        if first:
            for i in range(ahead):
                start(i)
        a = a_ref[0]
        for n, b1_ref in enumerate(biases):
            for j in range(chunks):
                if first:
                    start(n * chunks + j + ahead)
                    for copy in groups[n * chunks + j]:
                        copy.wait()
                sl = slice(j * FF_COLS, (j + 1) * FF_COLS)
                u0 = jnp.dot(a, w1[n, 0, :, sl], preferred_element_type=F32) + b1_ref[0, 0:1, sl]
                u1 = jnp.dot(a, w1[n, 1, :, sl], preferred_element_type=F32) + b1_ref[0, 1:2, sl]
                gate = 0.5 * u1 * (1.0 + lax.erf(u1 * (0.5 ** 0.5)))
                m_scr[:, n * ff + j * FF_COLS:n * ff + (j + 1) * FF_COLS] = (u0 * gate).astype(BF16)
        if first:
            for some in groups[len(biases) * chunks:]:
                for copy in some:
                    copy.wait()
        finish(jnp.dot(m_scr[...], w2[...], preferred_element_type=F32), first)

    pl.when(step == 0)(functools.partial(run, True))
    pl.when(step > 0)(functools.partial(run, False))


def ff_pair_kernel(layer, h_ref, a_ref, b0_ref, b1_ref, own1, own2, sib1, sib2, h_out, w1, w2, m_scr, sems):
    def finish(update, first):
        h_out[0] = h_ref[0] + update

    ff_steps(layer, a_ref, (b0_ref, b1_ref), ((own1, own2), (sib1, sib2)), w1, w2, m_scr, sems, finish)


def ff_kernel(layer, h_ref, a_ref, b1_ref, w_ref, h_out, w1, w2, m_scr, sems):
    def finish(update, first):
        h_out[0] = h_ref[0] + update

    ff_steps(layer, a_ref, (b1_ref,), ((w_ref,),), w1, w2, m_scr, sems, finish)


def ff_last_kernel(layer, h_ref, a_ref, b1_ref, vec_ref, w_ref, h_out, a_out, w1, w2, m_scr, sems):
    def finish(update, first):
        h = h_ref[0] + update + vec_ref[0:1]
        h_out[0] = h
        a_out[0] = layer_norm(h, vec_ref[1:2], vec_ref[2:3])

    ff_steps(layer, a_ref, (b1_ref,), ((w_ref,),), w1, w2, m_scr, sems, finish)


def ff_end_kernel(layer, h_ref, a_ref, b1_ref, vec_ref, io_ref, x0, x1, x2, x3, wp_ref, w_ref, y_ref,
                  w1, w2, m_scr, wp, wp_sem, sems):
    tok = x0.shape[1]
    last = pltpu.make_async_copy(wp_ref.at[1], wp, wp_sem.at[0])

    @pl.when(pl.program_id(0) == 0)
    def _():
        last.start()

    def finish(update, first):
        h = h_ref[0] + update + vec_ref[0:1]
        if first:
            last.wait()
        y = jnp.dot(h.astype(BF16), wp[...], preferred_element_type=F32) + io_ref[3:4]
        for i, ref in enumerate((x0, x1) if first else (x2, x3)):
            y_ref[i, 0] = (y[i * tok:(i + 1) * tok] + ref[0].astype(F32)).astype(BF16)

    ff_steps(layer, a_ref, (b1_ref,), ((w_ref,),), w1, w2, m_scr, sems, finish)


def rows_spec(shape):
    return pl.BlockSpec((1,) + shape, lambda i: (i, 0, 0))


def fixed_spec(shape, layer):
    return pl.BlockSpec((1,) + shape, lambda i: (layer,) + (0,) * len(shape))


def vec_spec(rows, cols):
    return pl.BlockSpec((rows, cols), lambda i: (0, 0))


def call(kernel, grid, in_specs, out_specs, out_shape, flops, scratch=(), aliases=None):
    return pl.pallas_call(
        kernel, grid=grid, in_specs=in_specs, out_specs=out_specs, out_shape=out_shape,
        scratch_shapes=scratch, input_output_aliases=aliases or {},
        cost_estimate=pl.CostEstimate(flops=flops, bytes_accessed=16 << 20, transcendentals=0),
        compiler_params=pltpu.CompilerParams(vmem_limit_bytes=VMEM_LIMIT))


def tie(*values):
    return lax.optimization_barrier(values)


def solution(mesh):
    tp_size = mesh.shape["tp"]
    dp_size = mesh.shape["dp"]

    def swap(value, mask):
        return lax.ppermute(value, "tp", [(i, i ^ mask) for i in range(tp_size)])

    def body(latents, context, io_vecs, w_proj, block_vecs, w_qkv, w_o1, w_q2, w_kv2, w_o2, w_ff1, b_ff1, w_ff2):
        batch, rows_loc, side, channels = latents.shape
        tok = rows_loc * side
        layers = w_qkv.shape[0]
        width = w_o1.shape[1] * HEAD
        ff = w_ff2.shape[1]
        ctx_len = context.shape[1]
        ctx_pad = -(-ctx_len // 16) * 16
        mine = batch // tp_size
        n_tok = tp_size * tok
        me = lax.axis_index("tp")
        dp_me = lax.axis_index("dp")

        def piece_of(value, layer, axis):
            rows = value.shape[axis] // dp_size
            start = [0] * value.ndim
            start[0], start[axis] = layer, dp_me * rows
            size = list(value.shape)
            size[0], size[axis] = 1, rows
            return lax.dynamic_slice(value, start, size)

        def gather(piece):
            return lax.all_gather(piece, "dp", axis=0, tiled=True)

        qkv_t = w_qkv.transpose(0, 2, 3, 4, 1).reshape(layers, 3 * width, channels)
        q2_t = w_q2.transpose(0, 2, 3, 1).reshape(layers, width, channels)
        o1_t = w_o1.reshape(layers, width, channels)
        o2_t = w_o2.reshape(layers, width, channels)
        ff1_t = w_ff1.transpose(0, 2, 1, 3)

        def ff_piece(ff1, ff2, layer):
            return jnp.concatenate([piece_of(ff1, layer, 2)[0], piece_of(ff2, layer, 1)])

        x_rows = latents.reshape(tp_size, mine, tok, channels)

        def group_of(array, index):
            return lax.dynamic_index_in_dim(array, index, 0, keepdims=False)

        x_parts = [group_of(x_rows, me)] + [swap(group_of(x_rows, me ^ m), m) for m in (1, 2, 3)]
        far_qkv = swap(piece_of(qkv_t, 0, 1)[0], 2)
        far_rest = swap(jnp.concatenate([piece_of(w, 0, 1)[0] for w in (o1_t, q2_t, o2_t)]), 2)
        sib_qkv, sib_o1, sib_q2, sib_o2 = (
            swap(w, 1) for w in (qkv_t, o1_t, q2_t, o2_t))
        bias = [b_ff1] + [swap(b_ff1, m) for m in (1, 2, 3)]

        kv = jnp.einsum("blc,rcjhd->rbljhd", context, w_kv2, preferred_element_type=F32).astype(BF16)
        kv = kv.reshape(layers, batch, ctx_len, 2 * width)
        kv = jnp.pad(kv, ((0, 0), (0, 0), (0, ctx_pad - ctx_len), (0, 0)))
        kv_out = [lax.dynamic_slice_in_dim(kv, (me ^ m) * mine, mine, 1) for m in range(tp_size)]
        kv_out[0], piece = tie(kv_out[0], far_qkv)
        full_qkv = gather(piece)
        kv_parts = [kv_out[0]] + [swap(kv_out[m], m) for m in (1, 2, 3)]
        ff_src = ff_piece(ff1_t, w_ff2, 0)
        far_ff = swap(ff_src, 2)
        sib_ff1, sib_ff2 = swap(ff1_t, 1), swap(w_ff2, 1)
        x_parts = list(tie(*x_parts, ff_src, *kv_out))[:tp_size]

        grid = (mine,)
        total = mine * n_tok
        a_shape = jax.ShapeDtypeStruct((mine, n_tok, channels), BF16)
        h_shape = jax.ShapeDtypeStruct((mine, n_tok, channels), F32)
        o_shape = jax.ShapeDtypeStruct((mine, n_tok, width), BF16)
        a_spec, o_spec = rows_spec((n_tok, channels)), rows_spec((n_tok, width))
        x_spec = rows_spec((tok, channels))

        hidden, act = call(
            in_kernel, grid,
            [x_spec] * 4 + [fixed_spec((channels, channels), 0), vec_spec(4, channels), vec_spec(2, channels)],
            [a_spec, a_spec], [h_shape, a_shape], 2 * total * channels * channels,
        )(*x_parts, w_proj, io_vecs, block_vecs[0, 0:2])

        def self_attn(act, weight, spec):
            return call(self_kernel, grid, [a_spec, spec], o_spec, o_shape,
                        2 * total * channels * 3 * width + 16 * total * n_tok * width)(act, weight)

        tile = n_tok // 2
        tiles = (2 * mine,)
        t_spec = pl.BlockSpec((1, tile, channels), lambda i: (i // 2, i % 2, 0))
        any_spec = pl.BlockSpec(memory_space=pl.ANY)
        group = 4
        cross_groups = SHARDS * width // (group * HEAD)

        def middle(hidden, mixed, vecs, layer, slot, rest, rest_sib):
            ot_spec = pl.BlockSpec((1, tile, width), lambda i: (i // 2, i % 2, 0))
            kv_spec = pl.BlockSpec((1, 1, ctx_pad, 2 * width), lambda i: (layer, i // 2, 0, 0))
            square = pltpu.VMEM((channels, channels), BF16)
            return call(
                functools.partial(mid_kernel, ctx_len, layer, slot), tiles,
                [t_spec] + [ot_spec] * 4 + [kv_spec] * 4 + [vec_spec(6, channels)] + [any_spec] * 8,
                [t_spec, t_spec], [h_shape, a_shape], 8 * total * channels * channels,
                [pltpu.VMEM((tile, channels), BF16), square, square, square,
                 pltpu.VMEM((cross_groups, group * 128, group * HEAD), BF16),
                 pltpu.VMEM((cross_groups, group * 128, 2 * group * HEAD), BF16),
                 pltpu.VMEM((cross_groups, tile, group * 128), BF16),
                 pltpu.SemaphoreType.DMA((3,))], {0: 0},
            )(hidden, *mixed, *kv_parts, vecs, o1_t, sib_o1, q2_t, sib_q2, o2_t, sib_o2, rest, rest_sib)

        chunks = ff // FF_COLS
        ff_flops = 6 * total * channels * ff

        def ff_scratch(n, *more):
            return [pltpu.VMEM((n, 2, channels, ff), BF16), pltpu.VMEM((n * ff, channels), BF16),
                    pltpu.VMEM((tile, n * ff), BF16), *more, pltpu.SemaphoreType.DMA((n * (chunks + 1),))]

        b_spec = [fixed_spec((2, ff), layer) for layer in range(layers)]

        def feed_forward_pair(hidden, act, layer):
            return call(functools.partial(ff_pair_kernel, layer), tiles,
                        [t_spec, t_spec] + [b_spec[layer]] * 2 + [any_spec] * 4, t_spec, h_shape,
                        2 * ff_flops, ff_scratch(2), {0: 0})(
                        hidden, act, bias[0], bias[1], ff1_t, w_ff2, sib_ff1, sib_ff2)

        def feed_forward(hidden, act, layer, shard, weight):
            return call(functools.partial(ff_kernel, layer), tiles,
                        [t_spec, t_spec, b_spec[layer], any_spec], t_spec, h_shape,
                        ff_flops, ff_scratch(1), {0: 0})(hidden, act, bias[shard], weight)

        def far_spec(rows, slot):
            return pl.BlockSpec((dp_size, rows // dp_size, channels), lambda i: (0, slot, 0))

        act, piece = tie(act, far_rest)
        full_rest = gather(piece)
        for layer in range(layers):
            vecs = block_vecs[layer]
            specs = [fixed_spec((3 * width, channels), layer)] * 2 + [far_spec(3 * width, 0)] * 2
            m0 = self_attn(act, qkv_t, specs[0])
            act, m0 = tie(act, m0)
            m1 = self_attn(act, sib_qkv, specs[1])
            act, m1, full = tie(act, m1, full_qkv)
            rem = full.reshape(dp_size, -1, channels)
            rem_sib = swap(rem, 1)
            if layer == 0:
                act, src_a, src_b, src_c = tie(act, qkv_t, ff1_t, w_ff2)
                far_qkv = swap(piece_of(src_a, 1, 1)[0], 2)
                far_ff1 = swap(ff_piece(src_b, src_c, 1), 2)
            m2 = self_attn(act, rem, specs[2])
            if layer == 0:
                act, m2, rest = tie(act, m2, full_rest)
                rest = rest.reshape(dp_size, -1, channels)
            rest_sib = swap(rest, 1)
            if layer == 0:
                act, *src = tie(act, o1_t, q2_t, o2_t)
                next_rest = swap(jnp.concatenate([w[1].reshape(dp_size, -1, channels) for w in src], axis=1), 2)
            m3 = self_attn(act, rem_sib, specs[3])
            if layer == 0:
                act, m3, piece = tie(act, m3, far_ff)
                full_ff = gather(piece)
            hidden, act = middle(hidden, [m0, m1, m2, m3], jnp.stack([vecs[i] for i in (6, 2, 3, 7, 4, 5)]),
                                 layer, 0, rest, rest_sib)
            if layer == 0:
                act, piece = tie(act, far_qkv)
                full_qkv = gather(piece)
            hidden = feed_forward_pair(hidden, act, layer)
            hidden, act, full = tie(hidden, act, full_ff)
            rem = full.reshape(dp_size, 3, ff // dp_size, channels)
            rem_sib = swap(rem, 1)
            hidden = feed_forward(hidden, act, layer, 2, rem)
            if layer == 0:
                hidden, piece, rest = tie(hidden, far_ff1, next_rest)
                next_ff = gather(piece)
            if layer < layers - 1:
                full_ff = next_ff
                after = block_vecs[layer + 1]
                hidden, act = call(
                    functools.partial(ff_last_kernel, layer), tiles,
                    [t_spec, t_spec, b_spec[layer], vec_spec(3, channels), any_spec],
                    [t_spec, t_spec], [h_shape, a_shape], ff_flops,
                    ff_scratch(1), {0: 0},
                )(hidden, act, bias[3], jnp.stack([vecs[8], after[0], after[1]]), rem_sib)

        y = []
        for sample in range(mine):
            row_spec = pl.BlockSpec((1, tile, channels), lambda i, sample=sample: (sample, i, 0))
            x_spec = pl.BlockSpec((1, tok, channels), lambda i, sample=sample: (sample, 0, 0))
            parts = call(
                functools.partial(ff_end_kernel, layers - 1), (2,),
                [row_spec, row_spec, b_spec[layers - 1], vec_spec(1, channels), vec_spec(4, channels)]
                + [x_spec] * 4 + [any_spec] * 2,
                pl.BlockSpec((tp_size // 2, 1, tok, channels), lambda i: (i, 0, 0, 0)),
                jax.ShapeDtypeStruct((tp_size, 1, tok, channels), BF16), ff_flops // mine,
                ff_scratch(1, pltpu.VMEM((channels, channels), BF16), pltpu.SemaphoreType.DMA((1,))),
                None,
            )(hidden, act, bias[3], vecs[8:9], io_vecs, *x_parts, w_proj, rem_sib)
            y.append([parts[0]] + [swap(parts[m], m) for m in (1, 2, 3)])
            if sample < mine - 1:
                hidden, parts = tie(hidden, parts)
        out = jnp.zeros((tp_size, mine, tok, channels), BF16)
        for m in range(tp_size):
            for sample in range(mine):
                out = lax.dynamic_update_slice(out, y[sample][m][None], (me ^ m, sample, 0, 0))
        return out.reshape(batch, rows_loc, side, channels)

    act_spec = P("dp", "tp", None, None)
    in_specs = (act_spec, P("dp", None, None), P(), P(), P(),
                P(None, None, None, "tp", None), P(None, "tp", None, None),
                P(None, None, "tp", None), P(None, None, None, "tp", None),
                P(None, "tp", None, None), P(None, None, None, "tp"),
                P(None, None, "tp"), P(None, "tp", None))
    return jax.shard_map(body, mesh=mesh, in_specs=in_specs, out_specs=act_spec, check_vma=False)
```

profile of v0, /device:TPU:0, one launch (start us, length us, event | category | flops | bytes accessed | tf_op | source)
XLA Modules:
  0.0 640.1 jit_solution(3311313734812330118)
XLA Ops:
  7.3 2.0 dynamic-slice_bitcast_fusion.7
  9.3 2.6 collective-permute-start.3
  11.8 5.3 convert_bitcast_fusion
  17.7 2.5 copy.37
  20.2 2.5 pad_dynamic-slice_fusion
  22.7 3.9 collective-permute-done.3
  26.7 3.2 dynamic-slice_bitcast_fusion.2
  30.0 1.7 collective-permute-start.1
  35.6 1.7 collective-permute-start.4
  37.4 1.2 constant_dynamic-slice_fusion.1
  38.6 12.6 %copy.51 = bf16[2,1280,2,1280]{3,1,2,0:T(8,128)(2,1)} copy(bf16[2,1280,2,1280]{3,2,1,0:T(2,128)(2,1)} %param.23) | data formatting | bytes 26214400 | tf_op args[10]
  51.2 1.5 dynamic-slice_bitcast_fusion.1
  52.7 1.7 pad_maximum_fusion
  54.4 10.3 %collective-permute-done.2.x3 = bf16[2,144,1280]{2,1,0:T(8,128)(2,1)S(1)} collective-permute-done((bf16[2,144,1280]{2,1,0:T(8,128)(2,1)}, bf16[2,144,1280]{2,1,0:T(8,128)(2,1)S(1)}, u32[]{:S(2)}, u32[]{:S(2)}) %collective-permute-start.2) | collective-permute-done | bytes 737312 | tf_op jit(solution)/shard_map/ppermute | solution.py:288
  64.7 14.3 %shard_map.127 = (f32[2,576,1280]{2,1,0:T(8,128)}, bf16[2,576,1280]{2,1,0:T(8,128)(2,1)}) custom-call(bf16[2,144,1280]{2,1,0:T(8,128)(2,1)S(1)} %get-tuple-element.57.x0, bf16[2,144,1280]{2,1,0:T(8,128)(2,1)S(1)} %collective-permute-done.x1, bf16[2,144,1280]{2,1,0:T(8,128)(2,1)S(1)} %collective-permute-done.1.x2, ...), custom_call_target="tpu_custom_call" | custom-call | flops 3774873600 | bytes 16777216 | tf_op jit(solution)/shard_map/pallas_call | solution.py:355
  79.7 1.8 copy-done.21
  81.5 11.7 %shard_map.128.o0 = bf16[2,576,320]{2,1,0:T(8,128)(2,1)S(1)} custom-call(bf16[2,576,1280]{2,1,0:T(8,128)(2,1)S(1)} %copy-done.21, bf16[2,960,1280]{2,1,0:T(8,128)(2,1)} %bitcast.142), custom_call_target="tpu_custom_call" | custom-call | flops 6228541440 | bytes 16777216 | tf_op jit(solution)/shard_map/pallas_call | solution.py:362
  94.2 11.7 %shard_map.129.o1 = bf16[2,576,320]{2,1,0:T(8,128)(2,1)S(1)} custom-call(bf16[2,576,1280]{2,1,0:T(8,128)(2,1)S(1)} %copy-done.21, bf16[2,960,1280]{2,1,0:T(8,128)(2,1)} %collective-permute-done.5.w_ref), custom_call_target="tpu_custom_call" | custom-call | flops 6228541440 | bytes 16777216 | tf_op jit(solution)/shard_map/pallas_call | solution.py:362
  107.3 1.7 collective-permute-start.7
  109.0 1.7 copy-done.14
  110.7 11.5 %shard_map.130.o2 = bf16[2,576,320]{2,1,0:T(8,128)(2,1)S(1)} custom-call(bf16[2,576,1280]{2,1,0:T(8,128)(2,1)} %get-tuple-element.74.a_ref, bf16[4,240,1280]{2,1,0:T(8,128)(2,1)S(1)} %bitcast.117), custom_call_target="tpu_custom_call" | custom-call | flops 6228541440 | bytes 16777216 | tf_op jit(solution)/shard_map/pallas_call | solution.py:362
  123.2 11.4 %shard_map.131.o3 = bf16[2,576,320]{2,1,0:T(8,128)(2,1)S(1)} custom-call(bf16[2,576,1280]{2,1,0:T(8,128)(2,1)} %get-tuple-element.74.a_ref, bf16[4,240,1280]{2,1,0:T(8,128)(2,1)S(1)} %collective-permute-done.6.w_ref), custom_call_target="tpu_custom_call" | custom-call | flops 6228541440 | bytes 16777216 | tf_op jit(solution)/shard_map/pallas_call | solution.py:362
  135.6 27.4 %collective-permute-done.7 = bf16[3,320,1280]{2,1,0:T(8,128)(2,1)} collective-permute-done((bf16[3,320,1280]{2,1,0:T(8,128)(2,1)}, bf16[3,320,1280]{2,1,0:T(8,128)(2,1)}, u32[]{:S(2)}, u32[]{:S(2)}) %collective-permute-start.7) | collective-permute-done | bytes 2457632 | tf_op jit(solution)/shard_map/ppermute | solution.py:288
  163.5 1.4 collective-permute-start.10
  165.4 9.9 %collective-permute-done.10.kv3 = bf16[2,2,80,640]{3,2,1,0:T(8,128)(2,1)S(1)} collective-permute-done((bf16[2,2,80,640]{3,2,1,0:T(8,128)(2,1)}, bf16[2,2,80,640]{3,2,1,0:T(8,128)(2,1)S(1)}, u32[]{:S(2)}, u32[]{:S(2)}) %collective-permute-start.10) | collective-permute-done | bytes 409632 | tf_op jit(solution)/shard_map/ppermute | solution.py:288
  176.7 1.7 collective-permute-start.9
  178.4 10.0 %collective-permute-done.9.kv2 = bf16[2,2,80,640]{3,2,1,0:T(8,128)(2,1)S(1)} collective-permute-done((bf16[2,2,80,640]{3,2,1,0:T(8,128)(2,1)}, bf16[2,2,80,640]{3,2,1,0:T(8,128)(2,1)S(1)}, u32[]{:S(2)}, u32[]{:S(2)}) %collective-permute-start.9) | collective-permute-done | bytes 409632 | tf_op jit(solution)/shard_map/ppermute | solution.py:288
  188.4 1.2 copy-done.44
  190.2 1.1 dynamic-slice_bitcast_fusion.6
  192.4 2.2 collective-permute-done.13.o2_sib
  194.6 1.7 collective-permute-start.15
  196.3 1.2 copy-done.28
  197.5 32.7 %shard_map.132 = (f32[2,576,1280]{2,1,0:T(8,128)}, bf16[2,576,1280]{2,1,0:T(8,128)(2,1)}) custom-call(f32[2,576,1280]{2,1,0:T(8,128)} %get-tuple-element.61.h_ref, bf16[2,576,320]{2,1,0:T(8,128)(2,1)S(1)} %copy-done.26, bf16[2,576,320]{2,1,0:T(8,128)(2,1)S(1)} %copy-done.28, bf16[2,576,320]{2,1,0:T(8,128)(2,1)} %copy-done.33, ...), custom_call_target="tpu_custom_call", output_to_operand_aliasing={{0}: (0, {})} | custom-call | flops 15099494400 | bytes 16777216 | tf_op jit(solution)/shard_map/pallas_call | solution.py:376
  230.2 2.0 copy-done.23
  232.3 33.0 %shard_map.133.h_ref = f32[2,576,1280]{2,1,0:T(8,128)} custom-call(f32[2,576,1280]{2,1,0:T(8,128)} %get-tuple-element.77.h_ref, bf16[2,576,1280]{2,1,0:T(8,128)(2,1)S(1)} %copy-done.23, f32[2,2,1280]{2,1,0:T(2,128)S(1)} %copy-done.20, f32[2,2,1280]{2,1,0:T(2,128)S(1)} %collective-permute-done.16.b1_ref, ...), custom_call_target="tpu_custom_call", output_to_operand_aliasing={{}: (0, {})} | custom-call | flops 22649241600 | bytes 16777216 | tf_op jit(solution)/shard_map/pallas_call | solution.py:397
  265.5 1.3 slice.166
  267.7 1.2 constant_dynamic-slice_fusion
  268.9 1.6 dynamic-slice_bitcast_fusion
  270.7 1.7 collective-permute-start.20
  272.8 103.4 %collective-permute-done.19.b1_ref = f32[2,2,1280]{2,1,0:T(2,128)S(1)} collective-permute-done((f32[2,2,1280]{2,1,0:T(2,128)S(1)}, f32[2,2,1280]{2,1,0:T(2,128)S(1)}, u32[]{:S(2)}, u32[]{:S(2)}) %collective-permute-start.19) | collective-permute-done | bytes 20512 | tf_op jit(solution)/shard_map/ppermute | solution.py:288
  376.2 18.9 %shard_map.134.h_ref = f32[2,576,1280]{2,1,0:T(8,128)} custom-call(f32[2,576,1280]{2,1,0:T(8,128)} %shard_map.133.h_ref, bf16[2,576,1280]{2,1,0:T(8,128)(2,1)S(1)} %copy-done.24, f32[2,2,1280]{2,1,0:T(2,128)S(1)} %collective-permute-done.19.b1_ref, bf16[4,3,320,1280]{3,2,1,0:T(8,128)(2,1)} %bitcast.146), custom_call_target="tpu_custom_call", output_to_operand_aliasing={{}: (0, {})} | custom-call | flops 11324620800 | bytes 16777216 | tf_op jit(solution)/shard_map/pallas_call | solution.py:403
  395.2 1.5 copy-done.39
  396.7 3.2 collective-permute-done.22.b1_ref
  399.9 21.8 %shard_map.135 = (f32[2,576,1280]{2,1,0:T(8,128)}, bf16[2,576,1280]{2,1,0:T(8,128)(2,1)S(1)}) custom-call(f32[2,576,1280]{2,1,0:T(8,128)} %shard_map.134.h_ref, bf16[2,576,1280]{2,1,0:T(8,128)(2,1)} %get-tuple-element.83.a_ref, f32[2,2,1280]{2,1,0:T(2,128)S(1)} %collective-permute-done.22.b1_ref, ...), custom_call_target="tpu_custom_call", output_to_operand_aliasing={{0}: (0, {})} | custom-call | flops 11324620800 | bytes 16777216 | tf_op jit(solution)/shard_map/pallas_call | solution.py:453
  421.8 12.8 %shard_map.136.o0 = bf16[2,576,320]{2,1,0:T(8,128)(2,1)S(1)} custom-call(bf16[2,576,1280]{2,1,0:T(8,128)(2,1)S(1)} %get-tuple-element.97.a_ref, bf16[2,960,1280]{2,1,0:T(8,128)(2,1)} %bitcast.144), custom_call_target="tpu_custom_call" | custom-call | flops 6228541440 | bytes 16777216 | tf_op jit(solution)/shard_map/pallas_call | solution.py:362
  435.5 11.7 %shard_map.137.o1 = bf16[2,576,320]{2,1,0:T(8,128)(2,1)S(1)} custom-call(bf16[2,576,1280]{2,1,0:T(8,128)(2,1)S(1)} %get-tuple-element.97.a_ref, bf16[2,960,1280]{2,1,0:T(8,128)(2,1)} %collective-permute-done.5.w_ref), custom_call_target="tpu_custom_call" | custom-call | flops 6228541440 | bytes 16777216 | tf_op jit(solution)/shard_map/pallas_call | solution.py:362
  448.7 1.7 copy-done.15
  450.3 11.6 %shard_map.138.o2 = bf16[2,576,320]{2,1,0:T(8,128)(2,1)S(1)} custom-call(bf16[2,576,1280]{2,1,0:T(8,128)(2,1)} %copy-done.22, bf16[4,240,1280]{2,1,0:T(8,128)(2,1)S(1)} %bitcast.119), custom_call_target="tpu_custom_call" | custom-call | flops 6228541440 | bytes 16777216 | tf_op jit(solution)/shard_map/pallas_call | solution.py:362
  462.9 11.5 %shard_map.139.o3 = bf16[2,576,320]{2,1,0:T(8,128)(2,1)S(1)} custom-call(bf16[2,576,1280]{2,1,0:T(8,128)(2,1)} %copy-done.22, bf16[4,240,1280]{2,1,0:T(8,128)(2,1)S(1)} %collective-permute-done.24.w_ref), custom_call_target="tpu_custom_call" | custom-call | flops 6228541440 | bytes 16777216 | tf_op jit(solution)/shard_map/pallas_call | solution.py:362
  475.5 32.9 %shard_map.140 = (f32[2,576,1280]{2,1,0:T(8,128)}, bf16[2,576,1280]{2,1,0:T(8,128)(2,1)}) custom-call(f32[2,576,1280]{2,1,0:T(8,128)} %get-tuple-element.91.h_ref, bf16[2,576,320]{2,1,0:T(8,128)(2,1)S(1)} %copy-done.30, bf16[2,576,320]{2,1,0:T(8,128)(2,1)S(1)} %copy-done.32, bf16[2,576,320]{2,1,0:T(8,128)(2,1)} %copy-done.35, ...), custom_call_target="tpu_custom_call", output_to_operand_aliasing={{0}: (0, {})} | custom-call | flops 15099494400 | bytes 16777216 | tf_op jit(solution)/shard_map/pallas_call | solution.py:376
  508.4 1.8 copy-done.2
  510.2 33.1 %shard_map.141.h_ref = f32[2,576,1280]{2,1,0:T(8,128)} custom-call(f32[2,576,1280]{2,1,0:T(8,128)} %get-tuple-element.100.h_ref, bf16[2,576,1280]{2,1,0:T(8,128)(2,1)S(1)} %copy-done.2, f32[2,2,1280]{2,1,0:T(2,128)S(1)} %copy-done.20, f32[2,2,1280]{2,1,0:T(2,128)S(1)} %collective-permute-done.16.b1_ref, ...), custom_call_target="tpu_custom_call", output_to_operand_aliasing={{}: (0, {})} | custom-call | flops 22649241600 | bytes 16777216 | tf_op jit(solution)/shard_map/pallas_call | solution.py:397
  543.5 19.1 %shard_map.142.h_ref = f32[2,576,1280]{2,1,0:T(8,128)} custom-call(f32[2,576,1280]{2,1,0:T(8,128)} %shard_map.141.h_ref, bf16[2,576,1280]{2,1,0:T(8,128)(2,1)S(1)} %copy-done.3, f32[2,2,1280]{2,1,0:T(2,128)S(1)} %collective-permute-done.19.b1_ref, bf16[4,3,320,1280]{3,2,1,0:T(8,128)(2,1)} %bitcast.148), custom_call_target="tpu_custom_call", output_to_operand_aliasing={{}: (0, {})} | custom-call | flops 11324620800 | bytes 16777216 | tf_op jit(solution)/shard_map/pallas_call | solution.py:403
  562.7 15.5 %shard_map.143 = bf16[4,1,144,1280]{3,2,1,0:T(8,128)(2,1)} custom-call(f32[2,576,1280]{2,1,0:T(8,128)} %shard_map.142.h_ref, bf16[2,576,1280]{2,1,0:T(8,128)(2,1)} %get-tuple-element.104.a_ref, f32[2,2,1280]{2,1,0:T(2,128)S(1)} %collective-permute-done.22.b1_ref, f32[1,1280]{1,0:T(1,128)S(1)} %get-tuple-element.125.vec_ref, f32[4,1280]{1,0:T(4,128)S(1)} %copy-done.13, ...), custom_call_target="tpu_custom_call" | custom-call | flops 5662310400 | bytes 16777216 | tf_op jit(solution)/shard_map/pallas_call | solution.py:464
  578.5 1.2 copy-done.37
  580.2 15.5 %shard_map.144 = bf16[4,1,144,1280]{3,2,1,0:T(8,128)(2,1)} custom-call(f32[2,576,1280]{2,1,0:T(8,128)} %shard_map.142.h_ref, bf16[2,576,1280]{2,1,0:T(8,128)(2,1)} %get-tuple-element.104.a_ref, f32[2,2,1280]{2,1,0:T(2,128)S(1)} %collective-permute-done.22.b1_ref, f32[1,1280]{1,0:T(1,128)S(1)} %get-tuple-element.125.vec_ref, f32[4,1280]{1,0:T(4,128)S(1)} %copy-done.13, ...), custom_call_target="tpu_custom_call" | custom-call | flops 5662310400 | bytes 16777216 | tf_op jit(solution)/shard_map/pallas_call | solution.py:464
  595.7 1.6 slice_bitcast_fusion
  597.5 2.0 collective-permute-start.30
  599.5 1.7 collective-permute-start.32
  601.3 7.6 %collective-permute-done.29 = bf16[1,144,1280]{2,1,0:T(8,128)(2,1)S(1)} collective-permute-done((bf16[1,144,1280]{2,1,0:T(8,128)(2,1)S(1)}, bf16[1,144,1280]{2,1,0:T(8,128)(2,1)S(1)}, u32[]{:S(2)}, u32[]{:S(2)}) %collective-permute-start.29) | collective-permute-done | bytes 368672 | tf_op jit(solution)/shard_map/ppermute | solution.py:288
  608.9 7.9 %collective-permute-done.30 = bf16[1,144,1280]{2,1,0:T(8,128)(2,1)S(1)} collective-permute-done((bf16[1,144,1280]{2,1,0:T(8,128)(2,1)S(1)}, bf16[1,144,1280]{2,1,0:T(8,128)(2,1)S(1)}, u32[]{:S(2)}, u32[]{:S(2)}) %collective-permute-start.30) | collective-permute-done | bytes 368672 | tf_op jit(solution)/shard_map/ppermute | solution.py:288
  616.8 6.7 %collective-permute-done.31 = bf16[1,144,1280]{2,1,0:T(8,128)(2,1)S(1)} collective-permute-done((bf16[1,144,1280]{2,1,0:T(8,128)(2,1)S(1)}, bf16[1,144,1280]{2,1,0:T(8,128)(2,1)S(1)}, u32[]{:S(2)}, u32[]{:S(2)}) %collective-permute-start.31) | collective-permute-done | bytes 368672 | tf_op jit(solution)/shard_map/ppermute | solution.py:288
  623.6 7.9 %collective-permute-done.32 = bf16[1,144,1280]{2,1,0:T(8,128)(2,1)S(1)} collective-permute-done((bf16[1,144,1280]{2,1,0:T(8,128)(2,1)S(1)}, bf16[1,144,1280]{2,1,0:T(8,128)(2,1)S(1)}, u32[]{:S(2)}, u32[]{:S(2)}) %collective-permute-start.32) | collective-permute-done | bytes 368672 | tf_op jit(solution)/shard_map/ppermute | solution.py:288
  631.5 1.6 copy-done.38
  (162 shorter events, 21.5 us)
Async XLA Ops:
  6.5 5.3 copy-start
  6.5 100.3 %all-gather.6.cloned.1.call-start = ((), (), s32[]{:S(2)}) async-start(), calls=%async_computation | async-start | bytes 3072000 | tf_op jit(solution)/shard_map/all_gather | solution.py:312
  6.5 87.6 %collective-permute-start.5 = (bf16[2,960,1280]{2,1,0:T(8,128)(2,1)}, bf16[2,960,1280]{2,1,0:T(8,128)(2,1)}, u32[]{:S(2)}, u32[]{:S(2)}) collective-permute-start(bf16[2,960,1280]{2,1,0:T(8,128)(2,1)} %bitcast.140), channel_id=1, source_target_pairs={{0,1},{1,0},{2,3},{3,2},{4,5},{5,4},{6,7},{7,6},{8,9},{9,8},{10,11... | collective-permute-start | bytes 14745608 | tf_op jit(solution)/shard_map/ppermute | solution.py:288
  9.3 17.4 %collective-permute-start.3 = (bf16[240,1280]{1,0:T(8,128)(2,1)}, bf16[240,1280]{1,0:T(8,128)(2,1)}, u32[]{:S(2)}, u32[]{:S(2)}) collective-permute-start(bf16[240,1280]{1,0:T(8,128)(2,1)} %dynamic-slice_bitcast_fusion.7), channel_id=1, source_target_pairs={{0,2},{1,3},{2,0},{3,1},{4,6},{5,7},{6,4},{7,5},{8,10},{9,11},{10,... | collective-permute-start | bytes 1843208 | tf_op jit(solution)/shard_map/ppermute | solution.py:288
  26.7 96.6 %all-gather.8.cloned.1.call-start = ((), (), s32[]{:S(2)}) async-start(), calls=%async_computation.1 | async-start | bytes 3072000 | tf_op jit(solution)/shard_map/all_gather | solution.py:312
  29.9 34.7 %copy-start.4 = (bf16[2,144,1280]{2,1,0:T(8,128)(2,1)}, bf16[2,144,1280]{2,1,0:T(8,128)(2,1)S(1)}, u32[]{:S(2)}) copy-start(bf16[2,144,1280]{2,1,0:T(8,128)(2,1)S(1)} %get-tuple-element.57.x0) | copy-start | bytes 2211844
  30.0 24.5 %collective-permute-start = (bf16[2,144,1280]{2,1,0:T(8,128)(2,1)}, bf16[2,144,1280]{2,1,0:T(8,128)(2,1)S(1)}, u32[]{:S(2)}, u32[]{:S(2)}) collective-permute-start(bf16[2,144,1280]{2,1,0:T(8,128)(2,1)} %get-tuple-element.111), channel_id=1, source_target_pairs={{0,1},{1,0},{2,3},{3,2},{4,5},{5,4},{6,7},{7,6},{8,9},{9,8},{10,11... | collective-permute-start | bytes 2211848 | tf_op jit(solution)/shard_map/ppermute | solution.py:288
  30.0 24.5 %collective-permute-start.1 = (bf16[2,144,1280]{2,1,0:T(8,128)(2,1)}, bf16[2,144,1280]{2,1,0:T(8,128)(2,1)S(1)}, u32[]{:S(2)}, u32[]{:S(2)}) collective-permute-start(bf16[2,144,1280]{2,1,0:T(8,128)(2,1)} %get-tuple-element.110), channel_id=1, source_target_pairs={{0,2},{1,3},{2,0},{3,1},{4,6},{5,7},{6,4},{7,5},{8,10},{9,11},{10,... | collective-permute-start | bytes 2211848 | tf_op jit(solution)/shard_map/ppermute | solution.py:288
  31.7 33.0 %collective-permute-start.2 = (bf16[2,144,1280]{2,1,0:T(8,128)(2,1)}, bf16[2,144,1280]{2,1,0:T(8,128)(2,1)S(1)}, u32[]{:S(2)}, u32[]{:S(2)}) collective-permute-start(bf16[2,144,1280]{2,1,0:T(8,128)(2,1)} %get-tuple-element.109), channel_id=1, source_target_pairs={{0,3},{1,2},{2,1},{3,0},{4,7},{5,6},{6,5},{7,4},{8,11},{9,10},{10,... | collective-permute-start | bytes 2211848 | tf_op jit(solution)/shard_map/ppermute | solution.py:288
  35.6 43.4 %collective-permute-start.4 = (bf16[240,1280]{1,0:T(8,128)(2,1)}, bf16[240,1280]{1,0:T(8,128)(2,1)}, u32[]{:S(2)}, u32[]{:S(2)}) collective-permute-start(bf16[240,1280]{1,0:T(8,128)(2,1)} %pad_maximum_fusion.3), channel_id=1, source_target_pairs={{0,2},{1,3},{2,0},{3,1},{4,6},{5,7},{6,4},{7,5},{8,10},{9,11},{10,... | collective-permute-start | bytes 1843208 | tf_op jit(solution)/shard_map/ppermute | solution.py:288
  38.6 12.6 %copy-start.43 = (f32[2,9,1280]{2,0,1:T(2,128)S(1)}, f32[2,9,1280]{2,0,1:T(2,128)}, u32[]{:S(2)}) copy-start(f32[2,9,1280]{2,0,1:T(2,128)} %param.17) | copy-start | bytes 276484
  52.7 12.0 %copy-start.12 = (f32[4,1280]{1,0:T(4,128)S(1)}, f32[4,1280]{1,0:T(4,128)}, u32[]{:S(2)}) copy-start(f32[4,1280]{1,0:T(4,128)} %io_ref.5) | copy-start | bytes 61444
  54.4 24.6 %copy-start.6 = (bf16[2,144,1280]{2,1,0:T(8,128)(2,1)}, bf16[2,144,1280]{2,1,0:T(8,128)(2,1)S(1)}, u32[]{:S(2)}) copy-start(bf16[2,144,1280]{2,1,0:T(8,128)(2,1)S(1)} %collective-permute-done.x1) | copy-start | bytes 2211844
  54.4 24.6 %copy-start.8 = (bf16[2,144,1280]{2,1,0:T(8,128)(2,1)}, bf16[2,144,1280]{2,1,0:T(8,128)(2,1)S(1)}, u32[]{:S(2)}) copy-start(bf16[2,144,1280]{2,1,0:T(8,128)(2,1)S(1)} %collective-permute-done.1.x2) | copy-start | bytes 2211844
  64.7 14.3 %copy-start.10 = (bf16[2,144,1280]{2,1,0:T(8,128)(2,1)}, bf16[2,144,1280]{2,1,0:T(8,128)(2,1)S(1)}, u32[]{:S(2)}) copy-start(bf16[2,144,1280]{2,1,0:T(8,128)(2,1)S(1)} %collective-permute-done.2.x3) | copy-start | bytes 2211844
  79.1 186.2 %all-gather.10.cloned.1.call-start = ((), (), s32[]{:S(2)}) async-start(), calls=%async_computation.2 | async-start | bytes 12288000 | tf_op jit(solution)/shard_map/all_gather | solution.py:312
  106.8 16.4 %collective-permute-start.6 = (bf16[4,240,1280]{2,1,0:T(8,128)(2,1)}, bf16[4,240,1280]{2,1,0:T(8,128)(2,1)S(1)}, u32[]{:S(2)}, u32[]{:S(2)}) collective-permute-start(bf16[4,240,1280]{2,1,0:T(8,128)(2,1)} %bitcast.116), channel_id=1, source_target_pairs={{0,1},{1,0},{2,3},{3,2},{4,5},{5,4},{6,7},{7,6},{8,9},{9,8},{10,11... | collective-permute-start | bytes 7372808 | tf_op jit(solution)/shard_map/ppermute | solution.py:288
  107.3 55.6 %collective-permute-start.7 = (bf16[3,320,1280]{2,1,0:T(8,128)(2,1)}, bf16[3,320,1280]{2,1,0:T(8,128)(2,1)}, u32[]{:S(2)}, u32[]{:S(2)}) collective-permute-start(bf16[3,320,1280]{2,1,0:T(8,128)(2,1)} %pad_maximum_fusion), channel_id=1, source_target_pairs={{0,2},{1,3},{2,0},{3,1},{4,6},{5,7},{6,4},{7,5},{8,10},{9,11},{10,... | collective-permute-start | bytes 7372808 | tf_op jit(solution)/shard_map/ppermute | solution.py:288
  109.0 121.2 %collective-permute-start.17 = (bf16[2,2,1280,1280]{3,2,1,0:T(8,128)(2,1)}, bf16[2,2,1280,1280]{3,2,1,0:T(8,128)(2,1)}, u32[]{:S(2)}, u32[]{:S(2)}) collective-permute-start(bf16[2,2,1280,1280]{3,2,1,0:T(8,128)(2,1)} %bitcast.114.own1), channel_id=1, source_target_pairs={{0,1},{1,0},{2,3},{3,2},{4,5},{5,4},{6,7},{7,6},{8,9},{9,8},{10,11... | collective-permute-start | bytes 39321608 | tf_op jit(solution)/shard_map/ppermute | solution.py:288
  135.5 56.7 %copy-start.20 = (f32[2,2,1280]{2,1,0:T(2,128)S(1)}, f32[2,2,1280]{2,1,0:T(2,128)}, u32[]{:S(2)}) copy-start(f32[2,2,1280]{2,1,0:T(2,128)} %b0_ref.3) | copy-start | bytes 61444
  135.5 60.8 %copy-start.26 = (bf16[2,576,320]{2,1,0:T(8,128)(2,1)S(1)}, bf16[2,576,320]{2,1,0:T(8,128)(2,1)}, u32[]{:S(2)}) copy-start(bf16[2,576,320]{2,1,0:T(8,128)(2,1)} %copy-done.25) | copy-start | bytes 2211844
  162.9 285.1 %all-gather.12.cloned.1.call-start = ((), (), s32[]{:S(2)}) async-start(), calls=%async_computation.3 | async-start | bytes 3072000 | tf_op jit(solution)/shard_map/all_gather | solution.py:312
  163.0 67.2 %collective-permute-start.18 = (bf16[2,1280,1280]{2,1,0:T(8,128)(2,1)}, bf16[2,1280,1280]{2,1,0:T(8,128)(2,1)}, u32[]{:S(2)}, u32[]{:S(2)}) collective-permute-start(bf16[2,1280,1280]{2,1,0:T(8,128)(2,1)} %own2.3), channel_id=1, source_target_pairs={{0,1},{1,0},{2,3},{3,2},{4,5},{5,4},{6,7},{7,6},{8,9},{9,8},{10,11... | collective-permute-start | bytes 19660808 | tf_op jit(solution)/shard_map/ppermute | solution.py:288
  163.1 25.4 %collective-permute-start.11 = (bf16[2,320,1280]{2,1,0:T(8,128)(2,1)}, bf16[2,320,1280]{2,1,0:T(8,128)(2,1)S(1)}, u32[]{:S(2)}, u32[]{:S(2)}) collective-permute-start(bf16[2,320,1280]{2,1,0:T(8,128)(2,1)} %bitcast.126), channel_id=1, source_target_pairs={{0,1},{1,0},{2,3},{3,2},{4,5},{5,4},{6,7},{7,6},{8,9},{9,8},{10,11... | collective-permute-start | bytes 4915208 | tf_op jit(solution)/shard_map/ppermute | solution.py:288
  163.5 11.7 %collective-permute-start.10 = (bf16[2,2,80,640]{3,2,1,0:T(8,128)(2,1)}, bf16[2,2,80,640]{3,2,1,0:T(8,128)(2,1)S(1)}, u32[]{:S(2)}, u32[]{:S(2)}) collective-permute-start(bf16[2,2,80,640]{3,2,1,0:T(8,128)(2,1)} %get-tuple-element.113), channel_id=1, source_target_pairs={{0,3},{1,2},{2,1},{3,0},{4,7},{5,6},{6,5},{7,4},{8,11},{9,10},{10,... | collective-permute-start | bytes 1228808 | tf_op jit(solution)/shard_map/ppermute | solution.py:288
  164.9 11.8 %collective-permute-start.8 = (bf16[2,2,80,640]{3,2,1,0:T(8,128)(2,1)}, bf16[2,2,80,640]{3,2,1,0:T(8,128)(2,1)S(1)}, u32[]{:S(2)}, u32[]{:S(2)}) collective-permute-start(bf16[2,2,80,640]{3,2,1,0:T(8,128)(2,1)} %get-tuple-element.114), channel_id=1, source_target_pairs={{0,1},{1,0},{2,3},{3,2},{4,5},{5,4},{6,7},{7,6},{8,9},{9,8},{10,11... | collective-permute-start | bytes 1228808 | tf_op jit(solution)/shard_map/ppermute | solution.py:288
  175.3 21.0 %collective-permute-start.14 = (bf16[4,240,1280]{2,1,0:T(8,128)(2,1)}, bf16[4,240,1280]{2,1,0:T(8,128)(2,1)}, u32[]{:S(2)}, u32[]{:S(2)}) collective-permute-start(bf16[4,240,1280]{2,1,0:T(8,128)(2,1)} %bitcast.149), channel_id=1, source_target_pairs={{0,1},{1,0},{2,3},{3,2},{4,5},{5,4},{6,7},{7,6},{8,9},{9,8},{10,11... | collective-permute-start | bytes 7372808 | tf_op jit(solution)/shard_map/ppermute | solution.py:288
  176.7 53.5 %copy-start.16 = (bf16[2,2,80,640]{3,2,1,0:T(8,128)(2,1)}, bf16[2,2,80,640]{3,2,1,0:T(8,128)(2,1)S(1)}, u32[]{:S(2)}) copy-start(bf16[2,2,80,640]{3,2,1,0:T(8,128)(2,1)S(1)} %collective-permute-done.8.kv1) | copy-start | bytes 1228804
  176.7 11.7 %collective-permute-start.9 = (bf16[2,2,80,640]{3,2,1,0:T(8,128)(2,1)}, bf16[2,2,80,640]{3,2,1,0:T(8,128)(2,1)S(1)}, u32[]{:S(2)}, u32[]{:S(2)}) collective-permute-start(bf16[2,2,80,640]{3,2,1,0:T(8,128)(2,1)} %get-tuple-element.115), channel_id=1, source_target_pairs={{0,2},{1,3},{2,0},{3,1},{4,6},{5,7},{6,4},{7,5},{8,10},{9,11},{10,... | collective-permute-start | bytes 1228808 | tf_op jit(solution)/shard_map/ppermute | solution.py:288
  188.4 41.7 %copy-start.18 = (bf16[2,2,80,640]{3,2,1,0:T(8,128)(2,1)}, bf16[2,2,80,640]{3,2,1,0:T(8,128)(2,1)S(1)}, u32[]{:S(2)}) copy-start(bf16[2,2,80,640]{3,2,1,0:T(8,128)(2,1)S(1)} %collective-permute-done.9.kv2) | copy-start | bytes 1228804
  188.4 3.8 collective-permute-start.12
  189.6 5.0 collective-permute-start.13
  192.3 37.9 %collective-permute-start.16 = (f32[2,2,1280]{2,1,0:T(2,128)S(1)}, f32[2,2,1280]{2,1,0:T(2,128)S(1)}, u32[]{:S(2)}, u32[]{:S(2)}) collective-permute-start(f32[2,2,1280]{2,1,0:T(2,128)S(1)} %copy-done.20), channel_id=1, source_target_pairs={{0,1},{1,0},{2,3},{3,2},{4,5},{5,4},{6,7},{7,6},{8,9},{9,8},{10,11... | collective-permute-start | bytes 61448 | tf_op jit(solution)/shard_map/ppermute | solution.py:288
  194.6 35.6 %collective-permute-start.15 = (bf16[240,1280]{1,0:T(8,128)(2,1)S(1)}, bf16[240,1280]{1,0:T(8,128)(2,1)S(1)}, u32[]{:S(2)}, u32[]{:S(2)}) collective-permute-start(bf16[240,1280]{1,0:T(8,128)(2,1)S(1)} %dynamic-slice_bitcast_fusion.6), channel_id=1, source_target_pairs={{0,2},{1,3},{2,0},{3,1},{4,6},{5,7},{6,4},{7,5},{8,10},{9,11},{10,... | collective-permute-start | bytes 1843208 | tf_op jit(solution)/shard_map/ppermute | solution.py:288
  230.2 35.1 %copy-start.42 = (bf16[240,1280]{1,0:T(8,128)(2,1)}, bf16[240,1280]{1,0:T(8,128)(2,1)S(1)}, u32[]{:S(2)}) copy-start(bf16[240,1280]{1,0:T(8,128)(2,1)S(1)} %collective-permute-done.15) | copy-start | bytes 1843204
  232.3 33.1 %copy-start.40 = (bf16[2,5,64,1280]{3,2,1,0:T(8,128)(2,1)S(1)}, bf16[2,5,64,1280]{3,2,1,0:T(8,128)(2,1)}, u32[]{:S(2)}) copy-start(bf16[2,5,64,1280]{3,2,1,0:T(8,128)(2,1)} %param.19) | copy-start | bytes 4915204
  265.3 134.7 %collective-permute-start.23 = (bf16[4,3,320,1280]{3,2,1,0:T(8,128)(2,1)}, bf16[4,3,320,1280]{3,2,1,0:T(8,128)(2,1)}, u32[]{:S(2)}, u32[]{:S(2)}) collective-permute-start(bf16[4,3,320,1280]{3,2,1,0:T(8,128)(2,1)} %bitcast.145), channel_id=1, source_target_pairs={{0,1},{1,0},{2,3},{3,2},{4,5},{5,4},{6,7},{7,6},{8,9},{9,8},{10,11... | collective-permute-start | bytes 29491208 | tf_op jit(solution)/shard_map/ppermute | solution.py:288
  265.4 278.0 %all-gather.14.cloned.1.call-start = ((), (), s32[]{:S(2)}) async-start(), calls=%async_computation.4 | async-start | bytes 12288000 | tf_op jit(solution)/shard_map/all_gather | solution.py:312
  267.3 127.8 %collective-permute-start.21 = (bf16[4,240,1280]{2,1,0:T(8,128)(2,1)S(1)}, bf16[4,240,1280]{2,1,0:T(8,128)(2,1)}, u32[]{:S(2)}, u32[]{:S(2)}) collective-permute-start(bf16[4,240,1280]{2,1,0:T(8,128)(2,1)S(1)} %pad_maximum_fusion.2), channel_id=1, source_target_pairs={{0,2},{1,3},{2,0},{3,1},{4,6},{5,7},{6,4},{7,5},{8,10},{9,11},{10,... | collective-permute-start | bytes 7372808 | tf_op jit(solution)/shard_map/ppermute | solution.py:288
  270.5 105.7 %copy-start.24 = (bf16[2,576,1280]{2,1,0:T(8,128)(2,1)S(1)}, bf16[2,576,1280]{2,1,0:T(8,128)(2,1)}, u32[]{:S(2)}) copy-start(bf16[2,576,1280]{2,1,0:T(8,128)(2,1)} %get-tuple-element.83.a_ref) | copy-start | bytes 8847364
  270.7 124.4 %collective-permute-start.20 = (bf16[3,320,1280]{2,1,0:T(8,128)(2,1)S(1)}, bf16[3,320,1280]{2,1,0:T(8,128)(2,1)S(1)}, u32[]{:S(2)}, u32[]{:S(2)}) collective-permute-start(bf16[3,320,1280]{2,1,0:T(8,128)(2,1)S(1)} %pad_maximum_fusion.1), channel_id=1, source_target_pairs={{0,2},{1,3},{2,0},{3,1},{4,6},{5,7},{6,4},{7,5},{8,10},{9,11},{10,... | collective-permute-start | bytes 7372808 | tf_op jit(solution)/shard_map/ppermute | solution.py:288
  272.4 103.8 %collective-permute-start.19 = (f32[2,2,1280]{2,1,0:T(2,128)S(1)}, f32[2,2,1280]{2,1,0:T(2,128)S(1)}, u32[]{:S(2)}, u32[]{:S(2)}) collective-permute-start(f32[2,2,1280]{2,1,0:T(2,128)S(1)} %copy-done.20), channel_id=1, source_target_pairs={{0,2},{1,3},{2,0},{3,1},{4,6},{5,7},{6,4},{7,5},{8,10},{9,11},{10,... | collective-permute-start | bytes 61448 | tf_op jit(solution)/shard_map/ppermute | solution.py:288
  396.7 3.3 collective-permute-start.22
  421.8 12.8 %copy-start.22 = (bf16[2,576,1280]{2,1,0:T(8,128)(2,1)}, bf16[2,576,1280]{2,1,0:T(8,128)(2,1)S(1)}, u32[]{:S(2)}) copy-start(bf16[2,576,1280]{2,1,0:T(8,128)(2,1)S(1)} %get-tuple-element.97.a_ref) | copy-start | bytes 8847364
  448.1 14.9 %collective-permute-start.24 = (bf16[4,240,1280]{2,1,0:T(8,128)(2,1)}, bf16[4,240,1280]{2,1,0:T(8,128)(2,1)S(1)}, u32[]{:S(2)}, u32[]{:S(2)}) collective-permute-start(bf16[4,240,1280]{2,1,0:T(8,128)(2,1)} %bitcast.118), channel_id=1, source_target_pairs={{0,1},{1,0},{2,3},{3,2},{4,5},{5,4},{6,7},{7,6},{8,9},{9,8},{10,11... | collective-permute-start | bytes 7372808 | tf_op jit(solution)/shard_map/ppermute | solution.py:288
  448.1 27.3 %collective-permute-start.25 = (bf16[4,240,1280]{2,1,0:T(8,128)(2,1)}, bf16[4,240,1280]{2,1,0:T(8,128)(2,1)}, u32[]{:S(2)}, u32[]{:S(2)}) collective-permute-start(bf16[4,240,1280]{2,1,0:T(8,128)(2,1)} %collective-permute-done.21.rest), channel_id=1, source_target_pairs={{0,1},{1,0},{2,3},{3,2},{4,5},{5,4},{6,7},{7,6},{8,9},{9,8},{10,11... | collective-permute-start | bytes 7372808 | tf_op jit(solution)/shard_map/ppermute | solution.py:288
  462.9 12.5 %copy-start.17 = (bf16[2,2,80,640]{3,2,1,0:T(8,128)(2,1)S(1)}, bf16[2,2,80,640]{3,2,1,0:T(8,128)(2,1)}, u32[]{:S(2)}) copy-start(bf16[2,2,80,640]{3,2,1,0:T(8,128)(2,1)} %copy-done.16) | copy-start | bytes 1228804
  462.9 12.5 %copy-start.19 = (bf16[2,2,80,640]{3,2,1,0:T(8,128)(2,1)S(1)}, bf16[2,2,80,640]{3,2,1,0:T(8,128)(2,1)}, u32[]{:S(2)}) copy-start(bf16[2,2,80,640]{3,2,1,0:T(8,128)(2,1)} %copy-done.18) | copy-start | bytes 1228804
  462.9 12.5 %copy-start.30 = (bf16[2,576,320]{2,1,0:T(8,128)(2,1)S(1)}, bf16[2,576,320]{2,1,0:T(8,128)(2,1)}, u32[]{:S(2)}) copy-start(bf16[2,576,320]{2,1,0:T(8,128)(2,1)} %copy-done.29) | copy-start | bytes 2211844
  462.9 12.5 %copy-start.32 = (bf16[2,576,320]{2,1,0:T(8,128)(2,1)S(1)}, bf16[2,576,320]{2,1,0:T(8,128)(2,1)}, u32[]{:S(2)}) copy-start(bf16[2,576,320]{2,1,0:T(8,128)(2,1)} %copy-done.31) | copy-start | bytes 2211844
  510.2 33.3 %copy-start.3 = (bf16[2,576,1280]{2,1,0:T(8,128)(2,1)S(1)}, bf16[2,576,1280]{2,1,0:T(8,128)(2,1)}, u32[]{:S(2)}) copy-start(bf16[2,576,1280]{2,1,0:T(8,128)(2,1)} %get-tuple-element.104.a_ref) | copy-start | bytes 8847364
  543.4 19.3 %copy-start.5 = (bf16[2,144,1280]{2,1,0:T(8,128)(2,1)S(1)}, bf16[2,144,1280]{2,1,0:T(8,128)(2,1)}, u32[]{:S(2)}) copy-start(bf16[2,144,1280]{2,1,0:T(8,128)(2,1)} %copy-done.4) | copy-start | bytes 2211844
  543.4 19.3 %copy-start.7 = (bf16[2,144,1280]{2,1,0:T(8,128)(2,1)S(1)}, bf16[2,144,1280]{2,1,0:T(8,128)(2,1)}, u32[]{:S(2)}) copy-start(bf16[2,144,1280]{2,1,0:T(8,128)(2,1)} %copy-done.6) | copy-start | bytes 2211844
  543.4 19.3 %copy-start.9 = (bf16[2,144,1280]{2,1,0:T(8,128)(2,1)S(1)}, bf16[2,144,1280]{2,1,0:T(8,128)(2,1)}, u32[]{:S(2)}) copy-start(bf16[2,144,1280]{2,1,0:T(8,128)(2,1)} %copy-done.8) | copy-start | bytes 2211844
  543.4 19.3 %copy-start.11 = (bf16[2,144,1280]{2,1,0:T(8,128)(2,1)S(1)}, bf16[2,144,1280]{2,1,0:T(8,128)(2,1)}, u32[]{:S(2)}) copy-start(bf16[2,144,1280]{2,1,0:T(8,128)(2,1)} %copy-done.10) | copy-start | bytes 2211844
  543.4 19.3 %copy-start.13 = (f32[4,1280]{1,0:T(4,128)S(1)}, f32[4,1280]{1,0:T(4,128)}, u32[]{:S(2)}) copy-start(f32[4,1280]{1,0:T(4,128)} %io_ref.5) | copy-start | bytes 61444
  543.4 19.2 %collective-permute-start.26 = (bf16[4,3,320,1280]{3,2,1,0:T(8,128)(2,1)}, bf16[4,3,320,1280]{3,2,1,0:T(8,128)(2,1)}, u32[]{:S(2)}, u32[]{:S(2)}) collective-permute-start(bf16[4,3,320,1280]{3,2,1,0:T(8,128)(2,1)} %bitcast.147), channel_id=1, source_target_pairs={{0,1},{1,0},{2,3},{3,2},{4,5},{5,4},{6,7},{7,6},{8,9},{9,8},{10,11... | collective-permute-start | bytes 29491208 | tf_op jit(solution)/shard_map/ppermute | solution.py:288
  579.7 19.8 %collective-permute-start.27 = (bf16[1,144,1280]{2,1,0:T(8,128)(2,1)S(1)}, bf16[1,144,1280]{2,1,0:T(8,128)(2,1)S(1)}, u32[]{:S(2)}, u32[]{:S(2)}) collective-permute-start(bf16[1,144,1280]{2,1,0:T(8,128)(2,1)S(1)} %get-tuple-element.123), channel_id=1, source_target_pairs={{0,1},{1,0},{2,3},{3,2},{4,5},{5,4},{6,7},{7,6},{8,9},{9,8},{10,11... | collective-permute-start | bytes 1105928 | tf_op jit(solution)/shard_map/ppermute | solution.py:288
  595.7 37.4 %copy-start.1 = (bf16[2,1024,2,5,64]{1,4,3,2,0:T(8,128)(2,1)S(1)}, bf16[2,1024,2,5,64]{1,4,3,2,0:T(8,128)(2,1)}, u32[]{:S(2)}) copy-start(bf16[2,1024,2,5,64]{1,4,3,2,0:T(8,128)(2,1)} %param.21) | copy-start | bytes 7864324
  597.3 4.0 collective-permute-start.28
  597.5 11.5 %collective-permute-start.29 = (bf16[1,144,1280]{2,1,0:T(8,128)(2,1)S(1)}, bf16[1,144,1280]{2,1,0:T(8,128)(2,1)S(1)}, u32[]{:S(2)}, u32[]{:S(2)}) collective-permute-start(bf16[1,144,1280]{2,1,0:T(8,128)(2,1)S(1)} %get-tuple-element.122), channel_id=1, source_target_pairs={{0,2},{1,3},{2,0},{3,1},{4,6},{5,7},{6,4},{7,5},{8,10},{9,11},{10,... | collective-permute-start | bytes 1105928 | tf_op jit(solution)/shard_map/ppermute | solution.py:288
  597.5 19.4 %collective-permute-start.30 = (bf16[1,144,1280]{2,1,0:T(8,128)(2,1)S(1)}, bf16[1,144,1280]{2,1,0:T(8,128)(2,1)S(1)}, u32[]{:S(2)}, u32[]{:S(2)}) collective-permute-start(bf16[1,144,1280]{2,1,0:T(8,128)(2,1)S(1)} %get-tuple-element.118), channel_id=1, source_target_pairs={{0,2},{1,3},{2,0},{3,1},{4,6},{5,7},{6,4},{7,5},{8,10},{9,11},{10,... | collective-permute-start | bytes 1105928 | tf_op jit(solution)/shard_map/ppermute | solution.py:288
  599.5 24.1 %collective-permute-start.31 = (bf16[1,144,1280]{2,1,0:T(8,128)(2,1)S(1)}, bf16[1,144,1280]{2,1,0:T(8,128)(2,1)S(1)}, u32[]{:S(2)}, u32[]{:S(2)}) collective-permute-start(bf16[1,144,1280]{2,1,0:T(8,128)(2,1)S(1)} %get-tuple-element.121), channel_id=1, source_target_pairs={{0,3},{1,2},{2,1},{3,0},{4,7},{5,6},{6,5},{7,4},{8,11},{9,10},{10,... | collective-permute-start | bytes 1105928 | tf_op jit(solution)/shard_map/ppermute | solution.py:288
  599.5 32.0 %collective-permute-start.32 = (bf16[1,144,1280]{2,1,0:T(8,128)(2,1)S(1)}, bf16[1,144,1280]{2,1,0:T(8,128)(2,1)S(1)}, u32[]{:S(2)}, u32[]{:S(2)}) collective-permute-start(bf16[1,144,1280]{2,1,0:T(8,128)(2,1)S(1)} %get-tuple-element.117), channel_id=1, source_target_pairs={{0,3},{1,2},{2,1},{3,0},{4,7},{5,6},{6,5},{7,4},{8,11},{9,10},{10,... | collective-permute-start | bytes 1105928 | tf_op jit(solution)/shard_map/ppermute | solution.py:288
  (19 other events, 25.1 us)
Sparse Core Ops, SparseCore 0:
  26.8 35.7 all-gather.5
  79.2 35.8 all-gather.7
  163.1 97.0 all-gather.9
  265.5 34.7 all-gather.11
  396.8 95.8 all-gather.13
where the time goes:
time: 649 us; the launch traced here: 640 us
  Pallas kernels  331 us (51%)
  waiting for transfers between devices  203 us (31%)
  local copies, waits for them, and re-layouts  60 us (9%)
  starting transfers between devices  24 us (4%)
  between operations  14.5 us (2%)
    ppermute x33, waiting for transfers between devices, swap(): return lax.ppermute(value, 'tp', [(i, i ^ mask) for i in range(tp_size)])  202 us
    pallas_call x8, Pallas kernels, self_attn(): call(self_kernel, grid, [a_spec, spec], o_spec, o_shape, 2 * total * chan...  94 us
    pallas_call x2, Pallas kernels, feed_forward_pair(): call(functools.partial(ff_pair_kernel, layer), tiles, [t_spec, t_spec] +...  66.1 us
    pallas_call x2, Pallas kernels, middle(): call(functools.partial(mid_kernel, ctx_len, layer, slot), tiles, [t_spec]...  65.6 us
    pallas_call x2, Pallas kernels, feed_forward(): call(functools.partial(ff_kernel, layer), tiles, [t_spec, t_spec, b_spec[...  38.1 us
    unnamed x92, local copies, waits for them, and re-layouts  36.1 us
    pallas_call x2, Pallas kernels, body(): call(functools.partial(ff_end_kernel, layers - 1), (2,), [row_spec, row_s...  31.1 us
    ppermute x33, starting transfers between devices, swap(): return lax.ppermute(value, 'tp', [(i, i ^ mask) for i in range(tp_size)])  23.3 us
  transfers between devices with their start and end apart: 38, of which 14 were waited for; matrix products, arithmetic and copies ran while one was open for 7% of the time, Pallas kernels for 49%

commit v1 on v0

--- a/solution.py
+++ b/solution.py
@@ -17,7 +17,7 @@
 F32 = jnp.float32
 BF16 = jnp.bfloat16
 NT = (((1,), (1,)), ((), ()))
-VMEM_LIMIT = 50 * 1024 * 1024
+VMEM_LIMIT = 67043328
 
 
 def layer_norm(hidden, ln_gain, ln_shift):
@@ -36,7 +36,7 @@
     return (mixed[:, :HEAD] / mixed[:, HEAD:]).astype(BF16)
 
 
-def in_kernel(x0, x1, x2, x3, w_ref, io_ref, ln_ref, h_out, a_out):
+def in_kernel(x0, x1, x2, x3, w_ref, io_ref, ln_ref, h_out, a_out, g_scr):
     tok, channels = x0.shape[1:]
     parts = [ref[0].astype(F32) for ref in (x0, x1, x2, x3)]
     size = channels // GROUPS
@@ -56,25 +56,41 @@
     var = group_average(sum(jnp.sum((p - mean) * (p - mean), axis=0, keepdims=True) for p in parts))
     inverse = lax.rsqrt(var + GN_EPS)
     for i, p in enumerate(parts):
-        normed = ((p - mean) * inverse * io_ref[0:1] + io_ref[1:2]).astype(BF16)
-        h = jnp.dot(normed, w_ref[0], preferred_element_type=F32) + io_ref[2:3]
-        h_out[0, i * tok:(i + 1) * tok, :] = h
-        a_out[0, i * tok:(i + 1) * tok, :] = layer_norm(h, ln_ref[0:1], ln_ref[1:2])
-
-
-def flat(ref):
-    value = ref[...]
-    return value.reshape(-1, value.shape[-1])
-
-
-def self_kernel(a_ref, w_ref, o_ref):
-    width = o_ref.shape[-1]
-    qkv = lax.dot_general(a_ref[0], flat(w_ref), NT, preferred_element_type=F32).astype(BF16)
-    for head in range(width // HEAD):
-        lo = head * HEAD
-        o_ref[0, :, lo:lo + HEAD] = attend(
-            qkv[:, lo:lo + HEAD], qkv[:, width + lo:width + lo + HEAD],
-            qkv[:, 2 * width + lo:2 * width + lo + HEAD])
+        g_scr[i * tok:(i + 1) * tok, :] = ((p - mean) * inverse * io_ref[0:1] + io_ref[1:2]).astype(BF16)
+    h = jnp.dot(g_scr[...], w_ref[0], preferred_element_type=F32) + io_ref[2:3]
+    h_out[0] = h
+    a_out[0] = layer_norm(h, ln_ref[0:1], ln_ref[1:2])
+
+
+def self_kernel(layer, a_ref, own_ref, sib_ref, o0, o1, w, sems):
+    width = o0.shape[-1]
+    copies = []
+    for n, ref in enumerate((own_ref, sib_ref)):
+        if ref.shape[1] == w.shape[1]:
+            pairs = [(ref.at[layer], w.at[n])]
+        else:
+            rows = ref.shape[1]
+            pairs = [(ref.at[d], w.at[n, pl.ds(d * rows, rows)]) for d in range(ref.shape[0])]
+        copies.append([pltpu.make_async_copy(src, to, sems.at[n]) for src, to in pairs])
+
+    @pl.when(pl.program_id(0) == 0)
+    def _():
+        for some in copies:
+            for copy in some:
+                copy.start()
+
+    for n, o_ref in enumerate((o0, o1)):
+        @pl.when(pl.program_id(0) == 0)
+        def _():
+            for copy in copies[n]:
+                copy.wait()
+
+        qkv = lax.dot_general(a_ref[0], w[n], NT, preferred_element_type=F32).astype(BF16)
+        for head in range(width // HEAD):
+            lo = head * HEAD
+            o_ref[0, :, lo:lo + HEAD] = attend(
+                qkv[:, lo:lo + HEAD], qkv[:, width + lo:width + lo + HEAD],
+                qkv[:, 2 * width + lo:2 * width + lo + HEAD])
 
 
 def row_copies(own, sib, rest, rest_sib, layer, slot, dst, sem):
@@ -181,7 +197,7 @@
     groups = ff_copies(layer, shards, w1, w2, sems)
     ff = w1.shape[3]
     chunks = ff // FF_COLS
-    ahead = 2
+    ahead = 2 * chunks
 
     def start(i):
         for copy in groups[i] if i < len(groups) else ():
@@ -213,18 +229,15 @@
     pl.when(step > 0)(functools.partial(run, False))
 
 
-def ff_pair_kernel(layer, h_ref, a_ref, b0_ref, b1_ref, own1, own2, sib1, sib2, h_out, w1, w2, m_scr, sems):
+def ff_kernel(layer, kinds, h_ref, a_ref, *rest):
+    biases, refs = rest[:len(kinds)], list(rest[len(kinds):-5])
+    h_out, w1, w2, m_scr, sems = rest[-5:]
+    shards = [[refs.pop(0) for _ in range(kind)] for kind in kinds]
+
     def finish(update, first):
         h_out[0] = h_ref[0] + update
 
-    ff_steps(layer, a_ref, (b0_ref, b1_ref), ((own1, own2), (sib1, sib2)), w1, w2, m_scr, sems, finish)
-
-
-def ff_kernel(layer, h_ref, a_ref, b1_ref, w_ref, h_out, w1, w2, m_scr, sems):
-    def finish(update, first):
-        h_out[0] = h_ref[0] + update
-
-    ff_steps(layer, a_ref, (b1_ref,), ((w_ref,),), w1, w2, m_scr, sems, finish)
+    ff_steps(layer, a_ref, biases, shards, w1, w2, m_scr, sems, finish)
 
 
 def ff_last_kernel(layer, h_ref, a_ref, b1_ref, vec_ref, w_ref, h_out, a_out, w1, w2, m_scr, sems):
@@ -236,7 +249,7 @@
     ff_steps(layer, a_ref, (b1_ref,), ((w_ref,),), w1, w2, m_scr, sems, finish)
 
 
-def ff_end_kernel(layer, h_ref, a_ref, b1_ref, vec_ref, io_ref, x0, x1, x2, x3, wp_ref, w_ref, y_ref,
+def ff_end_kernel(layer, h_ref, a_ref, b0_ref, b1_ref, vec_ref, io_ref, x0, x1, x2, x3, wp_ref, w0_ref, w1_ref, y_ref,
                   w1, w2, m_scr, wp, wp_sem, sems):
     tok = x0.shape[1]
     last = pltpu.make_async_copy(wp_ref.at[1], wp, wp_sem.at[0])
@@ -253,7 +266,7 @@
         for i, ref in enumerate((x0, x1) if first else (x2, x3)):
             y_ref[i, 0] = (y[i * tok:(i + 1) * tok] + ref[0].astype(F32)).astype(BF16)
 
-    ff_steps(layer, a_ref, (b1_ref,), ((w_ref,),), w1, w2, m_scr, sems, finish)
+    ff_steps(layer, a_ref, (b0_ref, b1_ref), ((w0_ref,), (w1_ref,)), w1, w2, m_scr, sems, finish)
 
 
 def rows_spec(shape):
@@ -356,11 +369,14 @@
             in_kernel, grid,
             [x_spec] * 4 + [fixed_spec((channels, channels), 0), vec_spec(4, channels), vec_spec(2, channels)],
             [a_spec, a_spec], [h_shape, a_shape], 2 * total * channels * channels,
+            [pltpu.VMEM((n_tok, channels), BF16)],
         )(*x_parts, w_proj, io_vecs, block_vecs[0, 0:2])
 
-        def self_attn(act, weight, spec):
-            return call(self_kernel, grid, [a_spec, spec], o_spec, o_shape,
-                        2 * total * channels * 3 * width + 16 * total * n_tok * width)(act, weight)
+        def self_attn(act, first, second, layer):
+            return call(functools.partial(self_kernel, layer), grid,
+                        [a_spec] + [pl.BlockSpec(memory_space=pl.ANY)] * 2, [o_spec, o_spec], [o_shape, o_shape],
+                        4 * total * channels * 3 * width + 32 * total * n_tok * width,
+                        [pltpu.VMEM((2, 3 * width, channels), BF16), pltpu.SemaphoreType.DMA((2,))])(act, first, second)
 
         tile = n_tok // 2
         tiles = (2 * mine,)
@@ -393,44 +409,33 @@
 
         b_spec = [fixed_spec((2, ff), layer) for layer in range(layers)]
 
-        def feed_forward_pair(hidden, act, layer):
-            return call(functools.partial(ff_pair_kernel, layer), tiles,
-                        [t_spec, t_spec] + [b_spec[layer]] * 2 + [any_spec] * 4, t_spec, h_shape,
-                        2 * ff_flops, ff_scratch(2), {0: 0})(
-                        hidden, act, bias[0], bias[1], ff1_t, w_ff2, sib_ff1, sib_ff2)
-
-        def feed_forward(hidden, act, layer, shard, weight):
-            return call(functools.partial(ff_kernel, layer), tiles,
-                        [t_spec, t_spec, b_spec[layer], any_spec], t_spec, h_shape,
-                        ff_flops, ff_scratch(1), {0: 0})(hidden, act, bias[shard], weight)
-
-        def far_spec(rows, slot):
-            return pl.BlockSpec((dp_size, rows // dp_size, channels), lambda i: (0, slot, 0))
+        def feed_forward(hidden, act, layer, *shards):
+            n = len(shards)
+            kinds = tuple(len(weights) for _, weights in shards)
+            return call(functools.partial(ff_kernel, layer, kinds), tiles,
+                        [t_spec, t_spec] + [b_spec[layer]] * n + [any_spec] * sum(kinds), t_spec, h_shape,
+                        n * ff_flops, ff_scratch(n), {0: 0})(
+                        hidden, act, *[bias[i] for i, _ in shards], *[w for _, weights in shards for w in weights])
 
         act, piece = tie(act, far_rest)
         full_rest = gather(piece)
         for layer in range(layers):
             vecs = block_vecs[layer]
-            specs = [fixed_spec((3 * width, channels), layer)] * 2 + [far_spec(3 * width, 0)] * 2
-            m0 = self_attn(act, qkv_t, specs[0])
-            act, m0 = tie(act, m0)
-            m1 = self_attn(act, sib_qkv, specs[1])
-            act, m1, full = tie(act, m1, full_qkv)
+            act, full = tie(act, full_qkv)
             rem = full.reshape(dp_size, -1, channels)
             rem_sib = swap(rem, 1)
+            m0, m1 = self_attn(act, qkv_t, sib_qkv, layer)
             if layer == 0:
-                act, src_a, src_b, src_c = tie(act, qkv_t, ff1_t, w_ff2)
+                act, m0, rest, src_a, src_b, src_c = tie(act, m0, full_rest, qkv_t, ff1_t, w_ff2)
                 far_qkv = swap(piece_of(src_a, 1, 1)[0], 2)
                 far_ff1 = swap(ff_piece(src_b, src_c, 1), 2)
-            m2 = self_attn(act, rem, specs[2])
-            if layer == 0:
-                act, m2, rest = tie(act, m2, full_rest)
                 rest = rest.reshape(dp_size, -1, channels)
-            rest_sib = swap(rest, 1)
-            if layer == 0:
                 act, *src = tie(act, o1_t, q2_t, o2_t)
                 next_rest = swap(jnp.concatenate([w[1].reshape(dp_size, -1, channels) for w in src], axis=1), 2)
-            m3 = self_attn(act, rem_sib, specs[3])
+            else:
+                act, m0 = tie(act, m0)
+            rest_sib = swap(rest, 1)
+            m2, m3 = self_attn(act, rem, rem_sib, layer)
             if layer == 0:
                 act, m3, piece = tie(act, m3, far_ff)
                 full_ff = gather(piece)
@@ -439,14 +444,20 @@
             if layer == 0:
                 act, piece = tie(act, far_qkv)
                 full_qkv = gather(piece)
-            hidden = feed_forward_pair(hidden, act, layer)
+            own, sib = (0, (ff1_t, w_ff2)), (1, (sib_ff1, sib_ff2))
+            if layer == 0:
+                hidden = feed_forward(hidden, act, layer, own, sib)
+            else:
+                hidden = feed_forward(hidden, act, layer, own)
             hidden, act, full = tie(hidden, act, full_ff)
             rem = full.reshape(dp_size, 3, ff // dp_size, channels)
             rem_sib = swap(rem, 1)
-            hidden = feed_forward(hidden, act, layer, 2, rem)
             if layer == 0:
+                hidden = feed_forward(hidden, act, layer, (2, (rem,)))
                 hidden, piece, rest = tie(hidden, far_ff1, next_rest)
                 next_ff = gather(piece)
+            else:
+                hidden = feed_forward(hidden, act, layer, sib)
             if layer < layers - 1:
                 full_ff = next_ff
                 after = block_vecs[layer + 1]
@@ -463,13 +474,13 @@
             x_spec = pl.BlockSpec((1, tok, channels), lambda i, sample=sample: (sample, 0, 0))
             parts = call(
                 functools.partial(ff_end_kernel, layers - 1), (2,),
-                [row_spec, row_spec, b_spec[layers - 1], vec_spec(1, channels), vec_spec(4, channels)]
-                + [x_spec] * 4 + [any_spec] * 2,
+                [row_spec, row_spec] + [b_spec[layers - 1]] * 2 + [vec_spec(1, channels), vec_spec(4, channels)]
+                + [x_spec] * 4 + [any_spec] * 3,
                 pl.BlockSpec((tp_size // 2, 1, tok, channels), lambda i: (i, 0, 0, 0)),
-                jax.ShapeDtypeStruct((tp_size, 1, tok, channels), BF16), ff_flops // mine,
-                ff_scratch(1, pltpu.VMEM((channels, channels), BF16), pltpu.SemaphoreType.DMA((1,))),
+                jax.ShapeDtypeStruct((tp_size, 1, tok, channels), BF16), 2 * ff_flops // mine,
+                ff_scratch(2, pltpu.VMEM((channels, channels), BF16), pltpu.SemaphoreType.DMA((1,))),
                 None,
-            )(hidden, act, bias[3], vecs[8:9], io_vecs, *x_parts, w_proj, rem_sib)
+            )(hidden, act, bias[2], bias[3], vecs[8:9], io_vecs, *x_parts, w_proj, rem, rem_sib)
             y.append([parts[0]] + [swap(parts[m], m) for m in (1, 2, 3)])
             if sample < mine - 1:
                 hidden, parts = tie(hidden, parts)

time: 649 us -> 583 us (0.90)
  waiting for transfers between devices: 203 us -> 147 us
  local copies, waits for them, and re-layouts: 60 us -> 49.5 us
    ppermute x33, waiting for transfers between devices: 202 us -> 137 us  [swap(): return lax.ppermute(value, 'tp', [(i, i ^ mask) for i in range(tp_size)])]
    unnamed x92 -> x26, local copies, waits for them, and re-layouts: 36.1 us -> 15.8 us
    pallas_call x12 -> x8, Pallas kernels: 198 us -> 182 us  [the longest x4 95.2 us: self_attn(): call(functools.partial(self_kernel, layer), grid, [a_spec] + [pl.BlockSpe...]
    pallas_call x2, Pallas kernels: 31.1 us -> 44.8 us  [body(): call(functools.partial(ff_end_kernel, layers - 1), (2,), [row_spec, row_s...]
    all_gather x5, waiting for transfers between devices: 0.05 us -> 9.98 us  [gather(): return lax.all_gather(piece, 'dp', axis=0, tiled=True)]
  transfers between devices with their start and end apart: 38 -> 38, of which waited for: 14 -> 13; matrix products, arithmetic and copies ran while one was open for 7% -> 9% of each run, Pallas kernels for 49% -> 53%
where the time goes in v1:
time: 583 us; the launch traced here: 575 us
  Pallas kernels  329 us (56%)
  waiting for transfers between devices  147 us (25%)
  local copies, waits for them, and re-layouts  49.5 us (8%)
  starting transfers between devices  23.7 us (4%)
  between operations  13.8 us (2%)
  other arithmetic  7.11 us (1%)
    ppermute x33, waiting for transfers between devices, swap(): return lax.ppermute(value, 'tp', [(i, i ^ mask) for i in range(tp_size)])  137 us
    pallas_call x4, Pallas kernels, self_attn(): call(functools.partial(self_kernel, layer), grid, [a_spec] + [pl.BlockSpe...  95.2 us
    pallas_call x4, Pallas kernels, feed_forward(): call(functools.partial(ff_kernel, layer, kinds), tiles, [t_spec, t_spec]...  86.8 us
    pallas_call x2, Pallas kernels, middle(): call(functools.partial(mid_kernel, ctx_len, layer, slot), tiles, [t_spec]...  66.1 us
    pallas_call x2, Pallas kernels, body(): call(functools.partial(ff_end_kernel, layers - 1), (2,), [row_spec, row_s...  44.8 us
    ppermute x33, starting transfers between devices, swap(): return lax.ppermute(value, 'tp', [(i, i ^ mask) for i in range(tp_size)])  23.3 us
    pallas_call x1, Pallas kernels, body(): call(functools.partial(ff_last_kernel, layer), tiles, [t_spec, t_spec, b_...  21.8 us
    unnamed x26, local copies, waits for them, and re-layouts  15.8 us
  transfers between devices with their start and end apart: 38, of which 13 were waited for; matrix products, arithmetic and copies ran while one was open for 9% of the time, Pallas kernels for 53%

profile of v1, /device:TPU:0, one launch (start us, length us, event | category | flops | bytes accessed | tf_op | source)
XLA Modules:
  0.0 575.4 jit_solution(3114193340779490683)
XLA Ops:
  6.5 2.0 dynamic-slice_bitcast_fusion.7
  8.5 3.2 collective-permute-start.3
  11.7 5.7 convert_bitcast_fusion
  18.0 2.5 copy.37
  20.5 2.8 pad_dynamic-slice_fusion
  23.3 2.6 collective-permute-done.3
  26.1 1.7 dynamic-slice_bitcast_fusion.2
  28.2 1.7 collective-permute-start.1
  30.9 1.0 dynamic-slice_bitcast_fusion.8
  31.8 1.0 dynamic-slice_bitcast_fusion.9
  33.7 1.4 collective-permute-start.4
  35.1 1.2 constant_dynamic-slice_fusion.1
  36.3 8.4 %copy.51 = bf16[2,1280,2,1280]{3,1,2,0:T(8,128)(2,1)S(1)} copy(bf16[2,1280,2,1280]{3,2,1,0:T(2,128)(2,1)} %param.23) | data formatting | bytes 26214400 | tf_op args[10]
  45.5 1.1 copy.50
  46.6 2.9 copy-done
  49.6 1.7 pad_maximum_fusion
  51.3 11.6 %collective-permute-done.2.x3 = bf16[2,144,1280]{2,1,0:T(8,128)(2,1)} collective-permute-done((bf16[2,144,1280]{2,1,0:T(8,128)(2,1)}, bf16[2,144,1280]{2,1,0:T(8,128)(2,1)}, u32[]{:S(2)}, u32[]{:S(2)}) %collective-permute-start.2) | collective-permute-done | bytes 737312 | tf_op jit(solution)/shard_map/ppermute | solution.py:301
  62.9 14.4 %shard_map.127 = (f32[2,576,1280]{2,1,0:T(8,128)}, bf16[2,576,1280]{2,1,0:T(8,128)(2,1)}) custom-call(bf16[2,144,1280]{2,1,0:T(8,128)(2,1)} %get-tuple-element.60.x0, bf16[2,144,1280]{2,1,0:T(8,128)(2,1)} %collective-permute-done.x1, bf16[2,144,1280]{2,1,0:T(8,128)(2,1)} %collective-permute-done.1.x2, bf16[2,144,1280]{2,1,0:T(8,128)(2,1)} %collective-permute-done.2.x3, ...), custom_call_target="tpu_custom_call" | custom-call | flops 3774873600 | bytes 16777216 | tf_op jit(solution)/shard_map/pallas_call | solution.py:368
  78.1 1.7 collective-permute-start.7
  79.9 23.6 %shard_map.128 = (bf16[2,576,320]{2,1,0:T(8,128)(2,1)}, bf16[2,576,320]{2,1,0:T(8,128)(2,1)}) custom-call(bf16[2,576,1280]{2,1,0:T(8,128)(2,1)} %get-tuple-element.74.a_ref, bf16[2,960,1280]{2,1,0:T(8,128)(2,1)} %bitcast.141, bf16[2,960,1280]{2,1,0:T(8,128)(2,1)} %collective-permute-done.5.sib_ref), custom_call_target="tpu_custom_call" | custom-call | flops 12457082880 | bytes 16777216 | tf_op jit(solution)/shard_map/pallas_call | solution.py:376
  103.5 9.9 %all-gather.8.cloned.1.call-done = bf16[960,1280]{1,0:T(8,128)(2,1)} async-done(((bf16[240,1280]{1,0:T(8,128)(2,1)}), bf16[960,1280]{1,0:T(8,128)(2,1)}) %all-gather.8.cloned.1.call-update) | async-done | bytes 2457616 | tf_op jit(solution)/shard_map/all_gather | solution.py:325
  113.4 23.8 %shard_map.129 = (bf16[2,576,320]{2,1,0:T(8,128)(2,1)}, bf16[2,576,320]{2,1,0:T(8,128)(2,1)}) custom-call(bf16[2,576,1280]{2,1,0:T(8,128)(2,1)} %get-tuple-element.74.a_ref, bf16[4,240,1280]{2,1,0:T(8,128)(2,1)} %bitcast.153, bf16[4,240,1280]{2,1,0:T(8,128)(2,1)} %collective-permute-done.6.sib_ref), custom_call_target="tpu_custom_call" | custom-call | flops 12457082880 | bytes 16777216 | tf_op jit(solution)/shard_map/pallas_call | solution.py:376
  137.9 1.5 collective-permute-start.10
  139.5 9.8 %collective-permute-done.10.kv3 = bf16[2,2,80,640]{3,2,1,0:T(8,128)(2,1)S(1)} collective-permute-done((bf16[2,2,80,640]{3,2,1,0:T(8,128)(2,1)}, bf16[2,2,80,640]{3,2,1,0:T(8,128)(2,1)S(1)}, u32[]{:S(2)}, u32[]{:S(2)}) %collective-permute-start.10) | collective-permute-done | bytes 409632 | tf_op jit(solution)/shard_map/ppermute | solution.py:301
  150.1 19.7 %collective-permute-done.8.kv1 = bf16[2,2,80,640]{3,2,1,0:T(8,128)(2,1)S(1)} collective-permute-done((bf16[2,2,80,640]{3,2,1,0:T(8,128)(2,1)}, bf16[2,2,80,640]{3,2,1,0:T(8,128)(2,1)S(1)}, u32[]{:S(2)}, u32[]{:S(2)}) %collective-permute-start.8) | collective-permute-done | bytes 409632 | tf_op jit(solution)/shard_map/ppermute | solution.py:301
  169.8 1.5 collective-permute-start.9
  171.2 10.3 %collective-permute-done.9.kv2 = bf16[2,2,80,640]{3,2,1,0:T(8,128)(2,1)S(1)} collective-permute-done((bf16[2,2,80,640]{3,2,1,0:T(8,128)(2,1)}, bf16[2,2,80,640]{3,2,1,0:T(8,128)(2,1)S(1)}, u32[]{:S(2)}, u32[]{:S(2)}) %collective-permute-start.9) | collective-permute-done | bytes 409632 | tf_op jit(solution)/shard_map/ppermute | solution.py:301
  182.2 1.2 copy-done.8
  183.4 1.5 slice_bitcast_fusion.6
  185.8 1.3 copy-done.5
  187.1 2.0 dynamic-slice_bitcast_fusion.6
  189.1 1.2 constant_dynamic-slice_fusion
  190.3 1.5 dynamic-slice_bitcast_fusion
  191.9 1.7 pad_maximum_fusion.1
  193.5 1.6 pad_maximum_fusion.2
  195.6 1.5 collective-permute-start.21
  197.6 33.1 %shard_map.130 = (f32[2,576,1280]{2,1,0:T(8,128)}, bf16[2,576,1280]{2,1,0:T(8,128)(2,1)}) custom-call(f32[2,576,1280]{2,1,0:T(8,128)} %get-tuple-element.64.h_ref, bf16[2,576,320]{2,1,0:T(8,128)(2,1)} %get-tuple-element.71.o0, bf16[2,576,320]{2,1,0:T(8,128)(2,1)} %get-tuple-element.72.o1, ...), custom_call_target="tpu_custom_call", output_to_operand_aliasing={{0}: (0, {})} | custom-call | flops 15099494400 | bytes 16777216 | tf_op jit(solution)/shard_map/pallas_call | solution.py:392
  230.7 33.7 %collective-permute-done.15 = bf16[240,1280]{1,0:T(8,128)(2,1)} collective-permute-done((bf16[240,1280]{1,0:T(8,128)(2,1)}, bf16[240,1280]{1,0:T(8,128)(2,1)}, u32[]{:S(2)}, u32[]{:S(2)}) %collective-permute-start.15) | collective-permute-done | bytes 614432 | tf_op jit(solution)/shard_map/ppermute | solution.py:301
  264.4 1.5 collective-permute-start.20
  266.0 31.7 %shard_map.131.h_ref = f32[2,576,1280]{2,1,0:T(8,128)} custom-call(f32[2,576,1280]{2,1,0:T(8,128)} %get-tuple-element.80.h_ref, bf16[2,576,1280]{2,1,0:T(8,128)(2,1)} %get-tuple-element.86.a_ref, f32[2,2,1280]{2,1,0:T(2,128)} %rest_0_.3, f32[2,2,1280]{2,1,0:T(2,128)} %collective-permute-done.16.rest_1_.rest_0_, ...), custom_call_target="tpu_custom_call", output_to_operand_aliasing={{}: (0, {})} | custom-call | flops 22649241600 | bytes 16777216 | tf_op jit(solution)/shard_map/pallas_call | solution.py:415
  298.4 21.2 %collective-permute-done.19.rest_0_.b0_ref = f32[2,2,1280]{2,1,0:T(2,128)} collective-permute-done((f32[2,2,1280]{2,1,0:T(2,128)}, f32[2,2,1280]{2,1,0:T(2,128)}, u32[]{:S(2)}, u32[]{:S(2)}) %collective-permute-start.19) | collective-permute-done | bytes 20512 | tf_op jit(solution)/shard_map/ppermute | solution.py:301
  319.6 18.4 %shard_map.132.h_ref = f32[2,576,1280]{2,1,0:T(8,128)} custom-call(f32[2,576,1280]{2,1,0:T(8,128)} %shard_map.131.h_ref, bf16[2,576,1280]{2,1,0:T(8,128)(2,1)} %get-tuple-element.86.a_ref, f32[2,2,1280]{2,1,0:T(2,128)} %collective-permute-done.19.rest_0_.b0_ref, bf16[4,3,320,1280]{3,2,1,0:T(8,128)(2,1)} %bitcast.146), custom_call_target="tpu_custom_call", output_to_operand_aliasing={{}: (0, {})} | custom-call | flops 11324620800 | bytes 16777216 | tf_op jit(solution)/shard_map/pallas_call | solution.py:415
  338.1 1.4 pad_maximum_fusion.4.vec_ref
  339.5 2.3 collective-permute-done.22.b1_ref
  341.8 21.8 %shard_map.133 = (f32[2,576,1280]{2,1,0:T(8,128)}, bf16[2,576,1280]{2,1,0:T(8,128)(2,1)}) custom-call(f32[2,576,1280]{2,1,0:T(8,128)} %shard_map.132.h_ref, bf16[2,576,1280]{2,1,0:T(8,128)(2,1)} %get-tuple-element.86.a_ref, f32[2,2,1280]{2,1,0:T(2,128)} %collective-permute-done.22.b1_ref, ...), custom_call_target="tpu_custom_call", output_to_operand_aliasing={{0}: (0, {})} | custom-call | flops 11324620800 | bytes 16777216 | tf_op jit(solution)/shard_map/pallas_call | solution.py:464
  364.2 1.4 stack.11.vec_ref
  365.6 23.8 %shard_map.134 = (bf16[2,576,320]{2,1,0:T(8,128)(2,1)}, bf16[2,576,320]{2,1,0:T(8,128)(2,1)}) custom-call(bf16[2,576,1280]{2,1,0:T(8,128)(2,1)} %get-tuple-element.101.a_ref, bf16[2,960,1280]{2,1,0:T(8,128)(2,1)} %bitcast.143, bf16[2,960,1280]{2,1,0:T(8,128)(2,1)} %collective-permute-done.5.sib_ref), custom_call_target="tpu_custom_call" | custom-call | flops 12457082880 | bytes 16777216 | tf_op jit(solution)/shard_map/pallas_call | solution.py:376
  389.4 24.0 %shard_map.135 = (bf16[2,576,320]{2,1,0:T(8,128)(2,1)}, bf16[2,576,320]{2,1,0:T(8,128)(2,1)}) custom-call(bf16[2,576,1280]{2,1,0:T(8,128)(2,1)} %get-tuple-element.101.a_ref, bf16[4,240,1280]{2,1,0:T(8,128)(2,1)} %bitcast.155, bf16[4,240,1280]{2,1,0:T(8,128)(2,1)} %collective-permute-done.24.sib_ref), custom_call_target="tpu_custom_call" | custom-call | flops 12457082880 | bytes 16777216 | tf_op jit(solution)/shard_map/pallas_call | solution.py:376
  413.4 33.0 %shard_map.136 = (f32[2,576,1280]{2,1,0:T(8,128)}, bf16[2,576,1280]{2,1,0:T(8,128)(2,1)}) custom-call(f32[2,576,1280]{2,1,0:T(8,128)} %get-tuple-element.94.h_ref, bf16[2,576,320]{2,1,0:T(8,128)(2,1)} %get-tuple-element.99.o0, bf16[2,576,320]{2,1,0:T(8,128)(2,1)} %get-tuple-element.100.o1, ...), custom_call_target="tpu_custom_call", output_to_operand_aliasing={{0}: (0, {})} | custom-call | flops 15099494400 | bytes 16777216 | tf_op jit(solution)/shard_map/pallas_call | solution.py:392
  446.5 18.3 %shard_map.137.h_ref = f32[2,576,1280]{2,1,0:T(8,128)} custom-call(f32[2,576,1280]{2,1,0:T(8,128)} %get-tuple-element.106.h_ref, bf16[2,576,1280]{2,1,0:T(8,128)(2,1)} %get-tuple-element.110.a_ref, f32[2,2,1280]{2,1,0:T(2,128)} %rest_0_.3, bf16[2,2,1280,1280]{3,2,1,0:T(8,128)(2,1)} %bitcast.118, ...), custom_call_target="tpu_custom_call", output_to_operand_aliasing={{}: (0, {})} | custom-call | flops 11324620800 | bytes 16777216 | tf_op jit(solution)/shard_map/pallas_call | solution.py:415
  464.9 18.3 %shard_map.138.h_ref = f32[2,576,1280]{2,1,0:T(8,128)} custom-call(f32[2,576,1280]{2,1,0:T(8,128)} %shard_map.137.h_ref, bf16[2,576,1280]{2,1,0:T(8,128)(2,1)} %get-tuple-element.110.a_ref, f32[2,2,1280]{2,1,0:T(2,128)} %collective-permute-done.16.rest_1_.rest_0_, ...), custom_call_target="tpu_custom_call", output_to_operand_aliasing={{}: (0, {})} | custom-call | flops 11324620800 | bytes 16777216 | tf_op jit(solution)/shard_map/pallas_call | solution.py:415
  483.2 22.5 %shard_map.139 = bf16[4,1,144,1280]{3,2,1,0:T(8,128)(2,1)} custom-call(f32[2,576,1280]{2,1,0:T(8,128)} %shard_map.138.h_ref, bf16[2,576,1280]{2,1,0:T(8,128)(2,1)} %get-tuple-element.110.a_ref, f32[2,2,1280]{2,1,0:T(2,128)} %collective-permute-done.19.rest_0_.b0_ref, f32[2,2,1280]{2,1,0:T(2,128)} %collective-permute-done.22.b1_ref, ...), custom_call_target="tpu_custom_call" | custom-call | flops 11324620800 | bytes 16777216 | tf_op jit(solution)/shard_map/pallas_call | solution.py:475
  505.8 1.8 broadcast_in_dim.21
  507.7 1.1 slice_bitcast_fusion.1
  509.3 22.3 %shard_map.140 = bf16[4,1,144,1280]{3,2,1,0:T(8,128)(2,1)} custom-call(f32[2,576,1280]{2,1,0:T(8,128)} %shard_map.138.h_ref, bf16[2,576,1280]{2,1,0:T(8,128)(2,1)} %get-tuple-element.110.a_ref, f32[2,2,1280]{2,1,0:T(2,128)} %collective-permute-done.19.rest_0_.b0_ref, f32[2,2,1280]{2,1,0:T(2,128)} %collective-permute-done.22.b1_ref, ...), custom_call_target="tpu_custom_call" | custom-call | flops 11324620800 | bytes 16777216 | tf_op jit(solution)/shard_map/pallas_call | solution.py:475
  531.6 2.2 slice_bitcast_fusion
  533.9 1.0 collective-permute-start.29
  534.9 1.1 collective-permute-start.30
  536.4 1.3 collective-permute-start.32
  537.7 1.7 bitcast_dynamic-update-slice_fusion.5
  540.2 5.2 collective-permute-done.29
  546.1 7.1 %collective-permute-done.30 = bf16[1,144,1280]{2,1,0:T(8,128)(2,1)S(1)} collective-permute-done((bf16[1,144,1280]{2,1,0:T(8,128)(2,1)S(1)}, bf16[1,144,1280]{2,1,0:T(8,128)(2,1)S(1)}, u32[]{:S(2)}, u32[]{:S(2)}) %collective-permute-start.30) | collective-permute-done | bytes 368672 | tf_op jit(solution)/shard_map/ppermute | solution.py:301
  554.0 6.0 %collective-permute-done.31 = bf16[1,144,1280]{2,1,0:T(8,128)(2,1)S(1)} collective-permute-done((bf16[1,144,1280]{2,1,0:T(8,128)(2,1)S(1)}, bf16[1,144,1280]{2,1,0:T(8,128)(2,1)S(1)}, u32[]{:S(2)}, u32[]{:S(2)}) %collective-permute-start.31) | collective-permute-done | bytes 368672 | tf_op jit(solution)/shard_map/ppermute | solution.py:301
  560.8 7.1 %collective-permute-done.32 = bf16[1,144,1280]{2,1,0:T(8,128)(2,1)S(1)} collective-permute-done((bf16[1,144,1280]{2,1,0:T(8,128)(2,1)S(1)}, bf16[1,144,1280]{2,1,0:T(8,128)(2,1)S(1)}, u32[]{:S(2)}, u32[]{:S(2)}) %collective-permute-start.32) | collective-permute-done | bytes 368672 | tf_op jit(solution)/shard_map/ppermute | solution.py:301
  (92 shorter events, 15.3 us)
Async XLA Ops:
  6.5 71.0 %all-gather.6.cloned.1.call-start = ((), (), s32[]{:S(2)}) async-start(), calls=%async_computation | async-start | bytes 3072000 | tf_op jit(solution)/shard_map/all_gather | solution.py:325
  8.5 17.4 %collective-permute-start.3 = (bf16[240,1280]{1,0:T(8,128)(2,1)}, bf16[240,1280]{1,0:T(8,128)(2,1)}, u32[]{:S(2)}, u32[]{:S(2)}) collective-permute-start(bf16[240,1280]{1,0:T(8,128)(2,1)} %dynamic-slice_bitcast_fusion.7), channel_id=1, source_target_pairs={{0,2},{1,3},{2,0},{3,1},{4,6},{5,7},{6,4},{7,5},{8,10},{9,11},{10,... | collective-permute-start | bytes 1843208 | tf_op jit(solution)/shard_map/ppermute | solution.py:301
  20.5 5.5 copy-start.1
  25.9 87.5 %all-gather.8.cloned.1.call-start = ((), (), s32[]{:S(2)}) async-start(), calls=%async_computation.1 | async-start | bytes 3072000 | tf_op jit(solution)/shard_map/all_gather | solution.py:325
  26.0 53.9 %collective-permute-start.5 = (bf16[2,960,1280]{2,1,0:T(8,128)(2,1)}, bf16[2,960,1280]{2,1,0:T(8,128)(2,1)}, u32[]{:S(2)}, u32[]{:S(2)}) collective-permute-start(bf16[2,960,1280]{2,1,0:T(8,128)(2,1)} %bitcast.140), channel_id=1, source_target_pairs={{0,1},{1,0},{2,3},{3,2},{4,5},{5,4},{6,7},{7,6},{8,9},{9,8},{10,11... | collective-permute-start | bytes 14745608 | tf_op jit(solution)/shard_map/ppermute | solution.py:301
  27.7 23.5 %collective-permute-start = (bf16[2,144,1280]{2,1,0:T(8,128)(2,1)}, bf16[2,144,1280]{2,1,0:T(8,128)(2,1)}, u32[]{:S(2)}, u32[]{:S(2)}) collective-permute-start(bf16[2,144,1280]{2,1,0:T(8,128)(2,1)} %get-tuple-element.117), channel_id=1, source_target_pairs={{0,1},{1,0},{2,3},{3,2},{4,5},{5,4},{6,7},{7,6},{8,9},{9,8},{10,11... | collective-permute-start | bytes 2211848 | tf_op jit(solution)/shard_map/ppermute | solution.py:301
  28.2 23.1 %collective-permute-start.1 = (bf16[2,144,1280]{2,1,0:T(8,128)(2,1)}, bf16[2,144,1280]{2,1,0:T(8,128)(2,1)}, u32[]{:S(2)}, u32[]{:S(2)}) collective-permute-start(bf16[2,144,1280]{2,1,0:T(8,128)(2,1)} %get-tuple-element.116), channel_id=1, source_target_pairs={{0,2},{1,3},{2,0},{3,1},{4,6},{5,7},{6,4},{7,5},{8,10},{9,11},{10,... | collective-permute-start | bytes 2211848 | tf_op jit(solution)/shard_map/ppermute | solution.py:301
  29.9 33.0 %collective-permute-start.2 = (bf16[2,144,1280]{2,1,0:T(8,128)(2,1)}, bf16[2,144,1280]{2,1,0:T(8,128)(2,1)}, u32[]{:S(2)}, u32[]{:S(2)}) collective-permute-start(bf16[2,144,1280]{2,1,0:T(8,128)(2,1)} %get-tuple-element.115), channel_id=1, source_target_pairs={{0,3},{1,2},{2,1},{3,0},{4,7},{5,6},{6,5},{7,4},{8,11},{9,10},{10,... | collective-permute-start | bytes 2211848 | tf_op jit(solution)/shard_map/ppermute | solution.py:301
  33.7 43.6 %collective-permute-start.4 = (bf16[240,1280]{1,0:T(8,128)(2,1)}, bf16[240,1280]{1,0:T(8,128)(2,1)}, u32[]{:S(2)}, u32[]{:S(2)}) collective-permute-start(bf16[240,1280]{1,0:T(8,128)(2,1)} %pad_maximum_fusion.3), channel_id=1, source_target_pairs={{0,2},{1,3},{2,0},{3,1},{4,6},{5,7},{6,4},{7,5},{8,10},{9,11},{10,... | collective-permute-start | bytes 1843208 | tf_op jit(solution)/shard_map/ppermute | solution.py:301
  44.7 4.8 copy-start
  77.3 220.4 %all-gather.10.cloned.1.call-start = ((), (), s32[]{:S(2)}) async-start(), calls=%async_computation.2 | async-start | bytes 12288000 | tf_op jit(solution)/shard_map/all_gather | solution.py:325
  77.5 35.9 %collective-permute-start.6 = (bf16[4,240,1280]{2,1,0:T(8,128)(2,1)}, bf16[4,240,1280]{2,1,0:T(8,128)(2,1)}, u32[]{:S(2)}, u32[]{:S(2)}) collective-permute-start(bf16[4,240,1280]{2,1,0:T(8,128)(2,1)} %bitcast.152), channel_id=1, source_target_pairs={{0,1},{1,0},{2,3},{3,2},{4,5},{5,4},{6,7},{7,6},{8,9},{9,8},{10,11... | collective-permute-start | bytes 7372808 | tf_op jit(solution)/shard_map/ppermute | solution.py:301
  78.1 59.1 %collective-permute-start.7 = (bf16[3,320,1280]{2,1,0:T(8,128)(2,1)}, bf16[3,320,1280]{2,1,0:T(8,128)(2,1)}, u32[]{:S(2)}, u32[]{:S(2)}) collective-permute-start(bf16[3,320,1280]{2,1,0:T(8,128)(2,1)} %pad_maximum_fusion), channel_id=1, source_target_pairs={{0,2},{1,3},{2,0},{3,1},{4,6},{5,7},{6,4},{7,5},{8,10},{9,11},{10,... | collective-permute-start | bytes 7372808 | tf_op jit(solution)/shard_map/ppermute | solution.py:301
  137.2 48.4 %copy-start.3 = (bf16[2,5,64,1280]{3,2,1,0:T(8,128)(2,1)S(1)}, bf16[2,5,64,1280]{3,2,1,0:T(8,128)(2,1)}, u32[]{:S(2)}) copy-start(bf16[2,5,64,1280]{3,2,1,0:T(8,128)(2,1)} %param.19) | copy-start | bytes 4915204
  137.2 48.5 %copy-start.4 = (bf16[2,1280,5,64]{1,3,2,0:T(8,128)(2,1)S(1)}, bf16[2,1280,5,64]{1,3,2,0:T(8,128)(2,1)}, u32[]{:S(2)}) copy-start(bf16[2,1280,5,64]{1,3,2,0:T(8,128)(2,1)} %param.20) | copy-start | bytes 4915204
  137.3 226.4 %all-gather.12.cloned.1.call-start = ((), (), s32[]{:S(2)}) async-start(), calls=%async_computation.3 | async-start | bytes 3072000 | tf_op jit(solution)/shard_map/all_gather | solution.py:325
  137.3 128.7 %collective-permute-start.17 = (bf16[2,2,1280,1280]{3,2,1,0:T(8,128)(2,1)}, bf16[2,2,1280,1280]{3,2,1,0:T(8,128)(2,1)}, u32[]{:S(2)}, u32[]{:S(2)}) collective-permute-start(bf16[2,2,1280,1280]{3,2,1,0:T(8,128)(2,1)} %bitcast.115), channel_id=1, source_target_pairs={{0,1},{1,0},{2,3},{3,2},{4,5},{5,4},{6,7},{7,6},{8,9},{9,8},{10,11... | collective-permute-start | bytes 39321608 | tf_op jit(solution)/shard_map/ppermute | solution.py:301
  137.4 128.6 %collective-permute-start.18 = (bf16[2,1280,1280]{2,1,0:T(8,128)(2,1)}, bf16[2,1280,1280]{2,1,0:T(8,128)(2,1)}, u32[]{:S(2)}, u32[]{:S(2)}) collective-permute-start(bf16[2,1280,1280]{2,1,0:T(8,128)(2,1)} %rest_2_.1), channel_id=1, source_target_pairs={{0,1},{1,0},{2,3},{3,2},{4,5},{5,4},{6,7},{7,6},{8,9},{9,8},{10,11... | collective-permute-start | bytes 19660808 | tf_op jit(solution)/shard_map/ppermute | solution.py:301
  137.9 43.6 %collective-permute-start.11 = (bf16[2,320,1280]{2,1,0:T(8,128)(2,1)}, bf16[2,320,1280]{2,1,0:T(8,128)(2,1)S(1)}, u32[]{:S(2)}, u32[]{:S(2)}) collective-permute-start(bf16[2,320,1280]{2,1,0:T(8,128)(2,1)} %bitcast.125), channel_id=1, source_target_pairs={{0,1},{1,0},{2,3},{3,2},{4,5},{5,4},{6,7},{7,6},{8,9},{9,8},{10,11... | collective-permute-start | bytes 4915208 | tf_op jit(solution)/shard_map/ppermute | solution.py:301
  137.9 11.3 %collective-permute-start.10 = (bf16[2,2,80,640]{3,2,1,0:T(8,128)(2,1)}, bf16[2,2,80,640]{3,2,1,0:T(8,128)(2,1)S(1)}, u32[]{:S(2)}, u32[]{:S(2)}) collective-permute-start(bf16[2,2,80,640]{3,2,1,0:T(8,128)(2,1)} %get-tuple-element.119), channel_id=1, source_target_pairs={{0,3},{1,2},{2,1},{3,0},{4,7},{5,6},{6,5},{7,4},{8,11},{9,10},{10,... | collective-permute-start | bytes 1228808 | tf_op jit(solution)/shard_map/ppermute | solution.py:301
  139.4 30.3 %collective-permute-start.8 = (bf16[2,2,80,640]{3,2,1,0:T(8,128)(2,1)}, bf16[2,2,80,640]{3,2,1,0:T(8,128)(2,1)S(1)}, u32[]{:S(2)}, u32[]{:S(2)}) collective-permute-start(bf16[2,2,80,640]{3,2,1,0:T(8,128)(2,1)} %get-tuple-element.120), channel_id=1, source_target_pairs={{0,1},{1,0},{2,3},{3,2},{4,5},{5,4},{6,7},{7,6},{8,9},{9,8},{10,11... | collective-permute-start | bytes 1228808 | tf_op jit(solution)/shard_map/ppermute | solution.py:301
  149.2 32.3 %copy-start.9 = (bf16[2,2,80,640]{3,2,1,0:T(8,128)(2,1)}, bf16[2,2,80,640]{3,2,1,0:T(8,128)(2,1)S(1)}, u32[]{:S(2)}) copy-start(bf16[2,2,80,640]{3,2,1,0:T(8,128)(2,1)S(1)} %collective-permute-done.10.kv3) | copy-start | bytes 1228804
  149.2 47.8 %collective-permute-start.14 = (bf16[4,240,1280]{2,1,0:T(8,128)(2,1)}, bf16[4,240,1280]{2,1,0:T(8,128)(2,1)}, u32[]{:S(2)}, u32[]{:S(2)}) collective-permute-start(bf16[4,240,1280]{2,1,0:T(8,128)(2,1)} %bitcast.150), channel_id=1, source_target_pairs={{0,1},{1,0},{2,3},{3,2},{4,5},{5,4},{6,7},{7,6},{8,9},{9,8},{10,11... | collective-permute-start | bytes 7372808 | tf_op jit(solution)/shard_map/ppermute | solution.py:301
  169.8 11.7 %copy-start.10 = (bf16[2,2,80,640]{3,2,1,0:T(8,128)(2,1)}, bf16[2,2,80,640]{3,2,1,0:T(8,128)(2,1)S(1)}, u32[]{:S(2)}) copy-start(bf16[2,2,80,640]{3,2,1,0:T(8,128)(2,1)S(1)} %collective-permute-done.8.kv1) | copy-start | bytes 1228804
  169.8 11.7 %collective-permute-start.9 = (bf16[2,2,80,640]{3,2,1,0:T(8,128)(2,1)}, bf16[2,2,80,640]{3,2,1,0:T(8,128)(2,1)S(1)}, u32[]{:S(2)}, u32[]{:S(2)}) collective-permute-start(bf16[2,2,80,640]{3,2,1,0:T(8,128)(2,1)} %get-tuple-element.121), channel_id=1, source_target_pairs={{0,2},{1,3},{2,0},{3,1},{4,6},{5,7},{6,4},{7,5},{8,10},{9,11},{10,... | collective-permute-start | bytes 1228808 | tf_op jit(solution)/shard_map/ppermute | solution.py:301
  181.5 0.8 copy-start.11
  181.5 13.6 %collective-permute-start.12 = (bf16[2,320,1280]{2,1,0:T(8,128)(2,1)}, bf16[2,320,1280]{2,1,0:T(8,128)(2,1)}, u32[]{:S(2)}, u32[]{:S(2)}) collective-permute-start(bf16[2,320,1280]{2,1,0:T(8,128)(2,1)} %bitcast.130), channel_id=1, source_target_pairs={{0,1},{1,0},{2,3},{3,2},{4,5},{5,4},{6,7},{7,6},{8,9},{9,8},{10,11... | collective-permute-start | bytes 4915208 | tf_op jit(solution)/shard_map/ppermute | solution.py:301
  182.2 1.2 copy-start.8
  183.4 12.2 %collective-permute-start.13 = (bf16[2,320,1280]{2,1,0:T(8,128)(2,1)}, bf16[2,320,1280]{2,1,0:T(8,128)(2,1)}, u32[]{:S(2)}, u32[]{:S(2)}) collective-permute-start(bf16[2,320,1280]{2,1,0:T(8,128)(2,1)} %bitcast.135), channel_id=1, source_target_pairs={{0,1},{1,0},{2,3},{3,2},{4,5},{5,4},{6,7},{7,6},{8,9},{9,8},{10,11... | collective-permute-start | bytes 4915208 | tf_op jit(solution)/shard_map/ppermute | solution.py:301
  185.6 1.4 copy-start.5
  195.1 70.8 %collective-permute-start.16 = (f32[2,2,1280]{2,1,0:T(2,128)}, f32[2,2,1280]{2,1,0:T(2,128)}, u32[]{:S(2)}, u32[]{:S(2)}) collective-permute-start(f32[2,2,1280]{2,1,0:T(2,128)} %rest_0_.3), channel_id=1, source_target_pairs={{0,1},{1,0},{2,3},{3,2},{4,5},{5,4},{6,7},{7,6},{8,9},{9,8},{10,11... | collective-permute-start | bytes 61448 | tf_op jit(solution)/shard_map/ppermute | solution.py:301
  195.6 142.4 %collective-permute-start.21 = (bf16[4,240,1280]{2,1,0:T(8,128)(2,1)}, bf16[4,240,1280]{2,1,0:T(8,128)(2,1)}, u32[]{:S(2)}, u32[]{:S(2)}) collective-permute-start(bf16[4,240,1280]{2,1,0:T(8,128)(2,1)} %pad_maximum_fusion.2), channel_id=1, source_target_pairs={{0,2},{1,3},{2,0},{3,1},{4,6},{5,7},{6,4},{7,5},{8,10},{9,11},{10,... | collective-permute-start | bytes 7372808 | tf_op jit(solution)/shard_map/ppermute | solution.py:301
  197.1 67.3 %collective-permute-start.15 = (bf16[240,1280]{1,0:T(8,128)(2,1)}, bf16[240,1280]{1,0:T(8,128)(2,1)}, u32[]{:S(2)}, u32[]{:S(2)}) collective-permute-start(bf16[240,1280]{1,0:T(8,128)(2,1)} %dynamic-slice_bitcast_fusion.6), channel_id=1, source_target_pairs={{0,2},{1,3},{2,0},{3,1},{4,6},{5,7},{6,4},{7,5},{8,10},{9,11},{10,... | collective-permute-start | bytes 1843208 | tf_op jit(solution)/shard_map/ppermute | solution.py:301
  264.4 73.6 %collective-permute-start.20 = (bf16[3,320,1280]{2,1,0:T(8,128)(2,1)}, bf16[3,320,1280]{2,1,0:T(8,128)(2,1)}, u32[]{:S(2)}, u32[]{:S(2)}) collective-permute-start(bf16[3,320,1280]{2,1,0:T(8,128)(2,1)} %pad_maximum_fusion.1), channel_id=1, source_target_pairs={{0,2},{1,3},{2,0},{3,1},{4,6},{5,7},{6,4},{7,5},{8,10},{9,11},{10,... | collective-permute-start | bytes 7372808 | tf_op jit(solution)/shard_map/ppermute | solution.py:301
  265.9 198.9 %all-gather.14.cloned.1.call-start = ((), (), s32[]{:S(2)}) async-start(), calls=%async_computation.4 | async-start | bytes 12288000 | tf_op jit(solution)/shard_map/all_gather | solution.py:325
  297.7 44.1 %collective-permute-start.23 = (bf16[4,3,320,1280]{3,2,1,0:T(8,128)(2,1)}, bf16[4,3,320,1280]{3,2,1,0:T(8,128)(2,1)}, u32[]{:S(2)}, u32[]{:S(2)}) collective-permute-start(bf16[4,3,320,1280]{3,2,1,0:T(8,128)(2,1)} %bitcast.145), channel_id=1, source_target_pairs={{0,1},{1,0},{2,3},{3,2},{4,5},{5,4},{6,7},{7,6},{8,9},{9,8},{10,11... | collective-permute-start | bytes 29491208 | tf_op jit(solution)/shard_map/ppermute | solution.py:301
  297.8 21.8 %collective-permute-start.19 = (f32[2,2,1280]{2,1,0:T(2,128)}, f32[2,2,1280]{2,1,0:T(2,128)}, u32[]{:S(2)}, u32[]{:S(2)}) collective-permute-start(f32[2,2,1280]{2,1,0:T(2,128)} %rest_0_.3), channel_id=1, source_target_pairs={{0,2},{1,3},{2,0},{3,1},{4,6},{5,7},{6,4},{7,5},{8,10},{9,11},{10,... | collective-permute-start | bytes 61448 | tf_op jit(solution)/shard_map/ppermute | solution.py:301
  338.1 3.8 collective-permute-start.22
  363.6 25.8 %collective-permute-start.24 = (bf16[4,240,1280]{2,1,0:T(8,128)(2,1)}, bf16[4,240,1280]{2,1,0:T(8,128)(2,1)}, u32[]{:S(2)}, u32[]{:S(2)}) collective-permute-start(bf16[4,240,1280]{2,1,0:T(8,128)(2,1)} %bitcast.154), channel_id=1, source_target_pairs={{0,1},{1,0},{2,3},{3,2},{4,5},{5,4},{6,7},{7,6},{8,9},{9,8},{10,11... | collective-permute-start | bytes 7372808 | tf_op jit(solution)/shard_map/ppermute | solution.py:301
  363.8 49.7 %collective-permute-start.25 = (bf16[4,240,1280]{2,1,0:T(8,128)(2,1)}, bf16[4,240,1280]{2,1,0:T(8,128)(2,1)}, u32[]{:S(2)}, u32[]{:S(2)}) collective-permute-start(bf16[4,240,1280]{2,1,0:T(8,128)(2,1)} %collective-permute-done.21.rest), channel_id=1, source_target_pairs={{0,1},{1,0},{2,3},{3,2},{4,5},{5,4},{6,7},{7,6},{8,9},{9,8},{10,11... | collective-permute-start | bytes 7372808 | tf_op jit(solution)/shard_map/ppermute | solution.py:301
  464.8 18.4 %collective-permute-start.26 = (bf16[4,3,320,1280]{3,2,1,0:T(8,128)(2,1)}, bf16[4,3,320,1280]{3,2,1,0:T(8,128)(2,1)}, u32[]{:S(2)}, u32[]{:S(2)}) collective-permute-start(bf16[4,3,320,1280]{3,2,1,0:T(8,128)(2,1)} %bitcast.147), channel_id=1, source_target_pairs={{0,1},{1,0},{2,3},{3,2},{4,5},{5,4},{6,7},{7,6},{8,9},{9,8},{10,11... | collective-permute-start | bytes 29491208 | tf_op jit(solution)/shard_map/ppermute | solution.py:301
  505.8 1.9 copy-start.2
  508.8 27.6 %collective-permute-start.27 = (bf16[1,144,1280]{2,1,0:T(8,128)(2,1)}, bf16[1,144,1280]{2,1,0:T(8,128)(2,1)}, u32[]{:S(2)}, u32[]{:S(2)}) collective-permute-start(bf16[1,144,1280]{2,1,0:T(8,128)(2,1)} %get-tuple-element.129), channel_id=1, source_target_pairs={{0,1},{1,0},{2,3},{3,2},{4,5},{5,4},{6,7},{7,6},{8,9},{9,8},{10,11... | collective-permute-start | bytes 1105928 | tf_op jit(solution)/shard_map/ppermute | solution.py:301
  531.5 2.3 copy-start.7
  531.6 4.4 copy-start.6
  533.8 5.6 collective-permute-start.28
  533.9 11.5 %collective-permute-start.29 = (bf16[1,144,1280]{2,1,0:T(8,128)(2,1)S(1)}, bf16[1,144,1280]{2,1,0:T(8,128)(2,1)S(1)}, u32[]{:S(2)}, u32[]{:S(2)}) collective-permute-start(bf16[1,144,1280]{2,1,0:T(8,128)(2,1)S(1)} %copy-done.7), channel_id=1, source_target_pairs={{0,2},{1,3},{2,0},{3,1},{4,6},{5,7},{6,4},{7,5},{8,10},{9,11},{10,... | collective-permute-start | bytes 1105928 | tf_op jit(solution)/shard_map/ppermute | solution.py:301
  534.9 18.4 %collective-permute-start.30 = (bf16[1,144,1280]{2,1,0:T(8,128)(2,1)S(1)}, bf16[1,144,1280]{2,1,0:T(8,128)(2,1)S(1)}, u32[]{:S(2)}, u32[]{:S(2)}) collective-permute-start(bf16[1,144,1280]{2,1,0:T(8,128)(2,1)S(1)} %get-tuple-element.124), channel_id=1, source_target_pairs={{0,2},{1,3},{2,0},{3,1},{4,6},{5,7},{6,4},{7,5},{8,10},{9,11},{10,... | collective-permute-start | bytes 1105928 | tf_op jit(solution)/shard_map/ppermute | solution.py:301
  535.9 24.1 %collective-permute-start.31 = (bf16[1,144,1280]{2,1,0:T(8,128)(2,1)S(1)}, bf16[1,144,1280]{2,1,0:T(8,128)(2,1)S(1)}, u32[]{:S(2)}, u32[]{:S(2)}) collective-permute-start(bf16[1,144,1280]{2,1,0:T(8,128)(2,1)S(1)} %copy-done.6), channel_id=1, source_target_pairs={{0,3},{1,2},{2,1},{3,0},{4,7},{5,6},{6,5},{7,4},{8,11},{9,10},{10,... | collective-permute-start | bytes 1105928 | tf_op jit(solution)/shard_map/ppermute | solution.py:301
  536.4 31.5 %collective-permute-start.32 = (bf16[1,144,1280]{2,1,0:T(8,128)(2,1)S(1)}, bf16[1,144,1280]{2,1,0:T(8,128)(2,1)S(1)}, u32[]{:S(2)}, u32[]{:S(2)}) collective-permute-start(bf16[1,144,1280]{2,1,0:T(8,128)(2,1)S(1)} %get-tuple-element.123), channel_id=1, source_target_pairs={{0,3},{1,2},{2,1},{3,0},{4,7},{5,6},{6,5},{7,4},{8,11},{9,10},{10,... | collective-permute-start | bytes 1105928 | tf_op jit(solution)/shard_map/ppermute | solution.py:301
Sparse Core Ops, SparseCore 0:
  26.0 35.7 all-gather.5
  77.4 35.9 all-gather.7
  137.4 95.7 all-gather.9
  266.0 33.5 all-gather.11
  338.2 95.7 all-gather.13

commit v2 on v1

--- a/solution.py
+++ b/solution.py
@@ -116,12 +116,6 @@
     copies = [row_copies(own, sib, rest, rest_sib, layer, slot + i, dst, sems.at[i]) for i, (own, sib, dst) in enumerate(
         ((o1_own, o1_sib, w_out1), (q2_own, q2_sib, w_q), (o2_own, o2_sib, w_out2)))]
 
-    def wait(i):
-        @pl.when(step == 0)
-        def _():
-            for copy in copies[i]:
-                copy.wait()
-
     @pl.when(step == 0)
     def _():
         for some in copies:
@@ -130,65 +124,80 @@
         k_scr[...] = jnp.zeros_like(k_scr)
         v_scr[...] = jnp.zeros_like(v_scr)
 
-    @pl.when(step % 2 == 0)
-    def _():
-        live = lax.broadcasted_iota(jnp.int32, (keys, HEAD), 0) < valid
-        for shard, ref in enumerate((kv0, kv1, kv2, kv3)):
-            kv = ref[0, 0]
-            for head in range(heads):
-                place = shard * heads + head
-                g, r = place // group, place % group
-                rows = slice(r * lanes, r * lanes + keys)
-                at = slice(r * HEAD, (r + 1) * HEAD)
-                k_scr[g, rows, at] = kv[:, head * HEAD:(head + 1) * HEAD]
-                v_scr[g, rows, at] = kv[:, width + head * HEAD:width + (head + 1) * HEAD]
-                v_scr[g, rows, cols + r * HEAD:cols + (r + 1) * HEAD] = live.astype(BF16)
-
+    one = (lax.broadcasted_iota(jnp.int32, (keys, HEAD), 0) < valid).astype(BF16)
+    for shard, ref in enumerate((kv0, kv1, kv2, kv3)):
+        kv = ref[0, 0]
+        for head in range(heads):
+            place = shard * heads + head
+            g, r = place // group, place % group
+            rows = slice(r * lanes, r * lanes + keys)
+            at = slice(r * HEAD, (r + 1) * HEAD)
+            k_scr[g, rows, at] = kv[:, head * HEAD:(head + 1) * HEAD]
+            v_scr[g, rows, at] = kv[:, width + head * HEAD:width + (head + 1) * HEAD]
+            v_scr[g, rows, cols + r * HEAD:cols + (r + 1) * HEAD] = one
     for i, o_ref in enumerate((o0, o1, o2, o3)):
         o_all[:, i * width:(i + 1) * width] = o_ref[0]
-    wait(0)
-    h = h_ref[0] + jnp.dot(o_all[...], w_out1[...], preferred_element_type=F32) + vec_ref[0:1]
-    act = layer_norm(h, vec_ref[1:2], vec_ref[2:3])
-    wait(1)
-    q = lax.dot_general(act, w_q[...], NT, preferred_element_type=F32).astype(BF16)
-    live = lax.broadcasted_iota(jnp.int32, (q.shape[0], lanes), 1) < valid
-    for g in range(k_scr.shape[0]):
-        at = slice(g * cols, (g + 1) * cols)
-        scores = lax.dot_general(q[:, at], k_scr[g], NT, preferred_element_type=F32)
-        for r in range(group):
-            sl = slice(r * lanes, (r + 1) * lanes)
-            s = jnp.where(live, scores[:, sl], -jnp.inf)
-            top = jnp.max(s, axis=-1, keepdims=True)
-            p_scr[g, :, sl] = jnp.exp2((s - top) * (HEAD ** -0.5 * LOG2E)).astype(BF16)
-        mixed = jnp.dot(p_scr[g], v_scr[g], preferred_element_type=F32)
-        o_all[:, at] = (mixed[:, :cols] / mixed[:, cols:]).astype(BF16)
-    wait(2)
-    h = h + jnp.dot(o_all[...], w_out2[...], preferred_element_type=F32) + vec_ref[3:4]
-    h_out[0] = h
-    a_out[0] = layer_norm(h, vec_ref[4:5], vec_ref[5:6])
+
+    half = h_ref.shape[1] // 2
+    halves = [slice(0, half), slice(half, 2 * half)]
+
+    def run(first):
+        def wait(i):
+            if first:
+                for copy in copies[i]:
+                    copy.wait()
+
+        wait(0)
+        h = [h_ref[0, at, :] + jnp.dot(o_all[at, :], w_out1[...], preferred_element_type=F32) + vec_ref[0:1] for at in halves]
+        for at, value in zip(halves, h):
+            h_out[0, at, :] = value
+        act = [layer_norm(value, vec_ref[1:2], vec_ref[2:3]) for value in h]
+        wait(1)
+        q = [lax.dot_general(value, w_q[...], NT, preferred_element_type=F32).astype(BF16) for value in act]
+        live = lax.broadcasted_iota(jnp.int32, (half, lanes), 1) < valid
+        for g in range(k_scr.shape[0]):
+            at = slice(g * cols, (g + 1) * cols)
+            scores = [lax.dot_general(value[:, at], k_scr[g], NT, preferred_element_type=F32) for value in q]
+            for rows, part in zip(halves, scores):
+                for r in range(group):
+                    sl = slice(r * lanes, (r + 1) * lanes)
+                    s = jnp.where(live, part[:, sl], -jnp.inf)
+                    top = jnp.max(s, axis=-1, keepdims=True)
+                    p_scr[g, rows, sl] = jnp.exp2((s - top) * (HEAD ** -0.5 * LOG2E)).astype(BF16)
+            for rows in halves:
+                mixed = jnp.dot(p_scr[g, rows, :], v_scr[g], preferred_element_type=F32)
+                o_all[rows, at] = (mixed[:, :cols] / mixed[:, cols:]).astype(BF16)
+        wait(2)
+        h = [h_out[0, at, :] + jnp.dot(o_all[at, :], w_out2[...], preferred_element_type=F32) + vec_ref[3:4] for at in halves]
+        for at, value in zip(halves, h):
+            h_out[0, at, :] = value
+            a_out[0, at, :] = layer_norm(value, vec_ref[4:5], vec_ref[5:6])
+
+    pl.when(step == 0)(functools.partial(run, True))
+    pl.when(step > 0)(functools.partial(run, False))
 
 
 FF_COLS = 256
 
 
 def ff_copies(layer, shards, w1, w2, sems):
-    ff = w1.shape[3]
+    channels, ff = w1.shape[2:]
     chunks = ff // FF_COLS
     first, second = [], []
     for n, refs in enumerate(shards):
+        packed = refs[0].shape[2] != channels
+        rows = refs[0].shape[2]
+        pieces = range(refs[0].shape[0])
         for j in range(chunks):
             at = pl.ds(j * FF_COLS, FF_COLS)
-            if len(refs) == 2:
+            if packed:
+                first.append([(refs[0].at[d, pl.ds(0, 2), :, at], w1.at[n, :, pl.ds(d * rows, rows), at]) for d in pieces])
+            else:
                 first.append([(refs[0].at[layer, :, :, at], w1.at[n, :, :, at])])
-            else:
-                rows = refs[0].shape[2]
-                first.append([(refs[0].at[d, pl.ds(0, 2), :, at], w1.at[n, :, pl.ds(d * rows, rows), at])
-                              for d in range(refs[0].shape[0])])
         if len(refs) == 2:
-            second.append([(refs[1].at[layer], w2.at[pl.ds(n * ff, ff)])])
+            second.append([(refs[1].at[layer if refs[1].shape[0] > 1 else 0], w2.at[pl.ds(n * ff, ff)])])
         else:
-            rows = refs[0].shape[2]
-            second.append([(refs[0].at[d, 2], w2.at[pl.ds(n * ff + d * rows, rows)]) for d in range(refs[0].shape[0])])
+            second.append([(refs[0].at[d, 2], w2.at[pl.ds(n * ff + d * rows, rows)]) for d in pieces])
     return [[pltpu.make_async_copy(src, to, sems.at[i]) for src, to in pairs] for i, pairs in enumerate(first + second)]
 
 
@@ -197,7 +206,7 @@
     groups = ff_copies(layer, shards, w1, w2, sems)
     ff = w1.shape[3]
     chunks = ff // FF_COLS
-    ahead = 2 * chunks
+    ahead = len(groups)
 
     def start(i):
         for copy in groups[i] if i < len(groups) else ():
@@ -249,16 +258,15 @@
     ff_steps(layer, a_ref, (b1_ref,), ((w_ref,),), w1, w2, m_scr, sems, finish)
 
 
-def ff_end_kernel(layer, h_ref, a_ref, b0_ref, b1_ref, vec_ref, io_ref, x0, x1, x2, x3, wp_ref, w0_ref, w1_ref, y_ref,
-                  w1, w2, m_scr, wp, wp_sem, sems):
+def ff_end_kernel(layer, h_ref, a_ref, b1, b2, b3, vec_ref, io_ref, x0, x1, x2, x3, wp_ref, *rest):
+    refs, (y_ref, w1, w2, m_scr, wp, wp_sem, sems) = rest[:-7], rest[-7:]
+    shards = [refs[i:i + 2] for i in range(0, len(refs), 2)]
     tok = x0.shape[1]
     last = pltpu.make_async_copy(wp_ref.at[1], wp, wp_sem.at[0])
 
-    @pl.when(pl.program_id(0) == 0)
-    def _():
-        last.start()
-
     def finish(update, first):
+        if first:
+            last.start()
         h = h_ref[0] + update + vec_ref[0:1]
         if first:
             last.wait()
@@ -266,7 +274,7 @@
         for i, ref in enumerate((x0, x1) if first else (x2, x3)):
             y_ref[i, 0] = (y[i * tok:(i + 1) * tok] + ref[0].astype(F32)).astype(BF16)
 
-    ff_steps(layer, a_ref, (b0_ref, b1_ref), ((w0_ref,), (w1_ref,)), w1, w2, m_scr, sems, finish)
+    ff_steps(layer, a_ref, (b1, b2, b3), shards, w1, w2, m_scr, sems, finish)
 
 
 def rows_spec(shape):
@@ -386,17 +394,16 @@
         cross_groups = SHARDS * width // (group * HEAD)
 
         def middle(hidden, mixed, vecs, layer, slot, rest, rest_sib):
-            ot_spec = pl.BlockSpec((1, tile, width), lambda i: (i // 2, i % 2, 0))
-            kv_spec = pl.BlockSpec((1, 1, ctx_pad, 2 * width), lambda i: (layer, i // 2, 0, 0))
+            kv_spec = pl.BlockSpec((1, 1, ctx_pad, 2 * width), lambda i: (layer, i, 0, 0))
             square = pltpu.VMEM((channels, channels), BF16)
             return call(
-                functools.partial(mid_kernel, ctx_len, layer, slot), tiles,
-                [t_spec] + [ot_spec] * 4 + [kv_spec] * 4 + [vec_spec(6, channels)] + [any_spec] * 8,
-                [t_spec, t_spec], [h_shape, a_shape], 8 * total * channels * channels,
-                [pltpu.VMEM((tile, channels), BF16), square, square, square,
+                functools.partial(mid_kernel, ctx_len, layer, slot), grid,
+                [a_spec] + [o_spec] * 4 + [kv_spec] * 4 + [vec_spec(6, channels)] + [any_spec] * 8,
+                [a_spec, a_spec], [h_shape, a_shape], 8 * total * channels * channels,
+                [pltpu.VMEM((n_tok, channels), BF16), square, square, square,
                  pltpu.VMEM((cross_groups, group * 128, group * HEAD), BF16),
                  pltpu.VMEM((cross_groups, group * 128, 2 * group * HEAD), BF16),
-                 pltpu.VMEM((cross_groups, tile, group * 128), BF16),
+                 pltpu.VMEM((cross_groups, n_tok, group * 128), BF16),
                  pltpu.SemaphoreType.DMA((3,))], {0: 0},
             )(hidden, *mixed, *kv_parts, vecs, o1_t, sib_o1, q2_t, sib_q2, o2_t, sib_o2, rest, rest_sib)
 
@@ -425,41 +432,35 @@
             rem = full.reshape(dp_size, -1, channels)
             rem_sib = swap(rem, 1)
             m0, m1 = self_attn(act, qkv_t, sib_qkv, layer)
-            if layer == 0:
-                act, m0, rest, src_a, src_b, src_c = tie(act, m0, full_rest, qkv_t, ff1_t, w_ff2)
-                far_qkv = swap(piece_of(src_a, 1, 1)[0], 2)
-                far_ff1 = swap(ff_piece(src_b, src_c, 1), 2)
-                rest = rest.reshape(dp_size, -1, channels)
-                act, *src = tie(act, o1_t, q2_t, o2_t)
-                next_rest = swap(jnp.concatenate([w[1].reshape(dp_size, -1, channels) for w in src], axis=1), 2)
-            else:
-                act, m0 = tie(act, m0)
-            rest_sib = swap(rest, 1)
+            act, m0 = tie(act, m0)
+            if layer == 1:
+                rest_sib = swap(rest, 1)
             m2, m3 = self_attn(act, rem, rem_sib, layer)
             if layer == 0:
-                act, m3, piece = tie(act, m3, far_ff)
+                act, m3, piece, rest = tie(act, m3, far_ff, full_rest)
                 full_ff = gather(piece)
+                rest = rest.reshape(dp_size, -1, channels)
+                rest_sib = swap(rest, 1)
+                act, src_a, src_b, src_c, *src = tie(act, qkv_t, ff1_t, w_ff2, o1_t, q2_t, o2_t)
+                far_qkv = swap(piece_of(src_a, 1, 1)[0], 2)
+                far_ff1 = swap(piece_of(src_b, 1, 2)[0], 2)
+                next_rest = swap(jnp.concatenate([w[1].reshape(dp_size, -1, channels) for w in src], axis=1), 2)
+                next_ff2 = swap(src_c[1:], 2)
+            else:
+                m3, next_ff2 = tie(m3, next_ff2)
+                next_ff2_sib = swap(next_ff2, 1)
             hidden, act = middle(hidden, [m0, m1, m2, m3], jnp.stack([vecs[i] for i in (6, 2, 3, 7, 4, 5)]),
                                  layer, 0, rest, rest_sib)
             if layer == 0:
                 act, piece = tie(act, far_qkv)
                 full_qkv = gather(piece)
-            own, sib = (0, (ff1_t, w_ff2)), (1, (sib_ff1, sib_ff2))
-            if layer == 0:
-                hidden = feed_forward(hidden, act, layer, own, sib)
-            else:
-                hidden = feed_forward(hidden, act, layer, own)
-            hidden, act, full = tie(hidden, act, full_ff)
-            rem = full.reshape(dp_size, 3, ff // dp_size, channels)
-            rem_sib = swap(rem, 1)
-            if layer == 0:
+                hidden = feed_forward(hidden, act, layer, (0, (ff1_t, w_ff2)), (1, (sib_ff1, sib_ff2)))
+                hidden, act, full, piece = tie(hidden, act, full_ff, far_ff1)
+                next_ff = gather(piece)
+                rem = full.reshape(dp_size, 3, ff // dp_size, channels)
+                rem_sib = swap(rem, 1)
                 hidden = feed_forward(hidden, act, layer, (2, (rem,)))
-                hidden, piece, rest = tie(hidden, far_ff1, next_rest)
-                next_ff = gather(piece)
-            else:
-                hidden = feed_forward(hidden, act, layer, sib)
-            if layer < layers - 1:
-                full_ff = next_ff
+                hidden, rest = tie(hidden, next_rest)
                 after = block_vecs[layer + 1]
                 hidden, act = call(
                     functools.partial(ff_last_kernel, layer), tiles,
@@ -468,19 +469,23 @@
                     ff_scratch(1), {0: 0},
                 )(hidden, act, bias[3], jnp.stack([vecs[8], after[0], after[1]]), rem_sib)
 
+        hidden, act, full = tie(hidden, act, next_ff)
+        rem = full.reshape(dp_size, 2, ff // dp_size, channels)
+        ff_weights = [sib_ff1, sib_ff2, rem, next_ff2, swap(rem, 1), next_ff2_sib]
+        hidden = feed_forward(hidden, act, layers - 1, (0, (ff1_t, w_ff2)))
         y = []
         for sample in range(mine):
             row_spec = pl.BlockSpec((1, tile, channels), lambda i, sample=sample: (sample, i, 0))
             x_spec = pl.BlockSpec((1, tok, channels), lambda i, sample=sample: (sample, 0, 0))
             parts = call(
                 functools.partial(ff_end_kernel, layers - 1), (2,),
-                [row_spec, row_spec] + [b_spec[layers - 1]] * 2 + [vec_spec(1, channels), vec_spec(4, channels)]
-                + [x_spec] * 4 + [any_spec] * 3,
+                [row_spec, row_spec] + [b_spec[layers - 1]] * 3 + [vec_spec(1, channels), vec_spec(4, channels)]
+                + [x_spec] * 4 + [any_spec] * 7,
                 pl.BlockSpec((tp_size // 2, 1, tok, channels), lambda i: (i, 0, 0, 0)),
-                jax.ShapeDtypeStruct((tp_size, 1, tok, channels), BF16), 2 * ff_flops // mine,
-                ff_scratch(2, pltpu.VMEM((channels, channels), BF16), pltpu.SemaphoreType.DMA((1,))),
+                jax.ShapeDtypeStruct((tp_size, 1, tok, channels), BF16), 3 * ff_flops // mine,
+                ff_scratch(3, pltpu.VMEM((channels, channels), BF16), pltpu.SemaphoreType.DMA((1,))),
                 None,
-            )(hidden, act, bias[2], bias[3], vecs[8:9], io_vecs, *x_parts, w_proj, rem, rem_sib)
+            )(hidden, act, *bias[1:], vecs[8:9], io_vecs, *x_parts, w_proj, *ff_weights)
             y.append([parts[0]] + [swap(parts[m], m) for m in (1, 2, 3)])
             if sample < mine - 1:
                 hidden, parts = tie(hidden, parts)

time: 583 us -> 569 us (0.976)
  Pallas kernels: 329 us -> 314 us
    pallas_call x4 -> x3, Pallas kernels: 86.8 us -> 67.8 us  [feed_forward(): call(functools.partial(ff_kernel, layer, kinds), tiles, [t_spec, t_spec]...]
    pallas_call x2, Pallas kernels: 44.8 us -> 58.4 us  [body(): call(functools.partial(ff_end_kernel, layers - 1), (2,), [row_spec, row_s...]
    all_gather x5, waiting for transfers between devices: 9.98 us -> 0.16 us  [gather(): return lax.all_gather(piece, 'dp', axis=0, tiled=True)]
    pallas_call x2, Pallas kernels: 66.1 us -> 58.6 us  [middle(): call(functools.partial(mid_kernel, ctx_len, layer, slot), grid, [a_spec]...]
    ppermute x33 -> x35, waiting for transfers between devices: 137 us -> 143 us  [swap(): return lax.ppermute(value, 'tp', [(i, i ^ mask) for i in range(tp_size)])]
    ppermute x33 -> x35, starting transfers between devices: 23.3 us -> 25.8 us  [swap(): return lax.ppermute(value, 'tp', [(i, i ^ mask) for i in range(tp_size)])]
    unnamed x26 -> x42, local copies, waits for them, and re-layouts: 15.8 us -> 14.6 us
  transfers between devices with their start and end apart: 38 -> 40, of which waited for: 13 -> 13; matrix products, arithmetic and copies ran while one was open for 9% -> 9% of each run, Pallas kernels for 53% -> 51%
where the time goes in v2:
time: 569 us; the launch traced here: 562 us
  Pallas kernels  314 us (55%)
  waiting for transfers between devices  144 us (25%)
  local copies, waits for them, and re-layouts  52.8 us (9%)
  starting transfers between devices  26.2 us (5%)
  between operations  14.1 us (2%)
  matrix products  5.74 us (1%)
    ppermute x35, waiting for transfers between devices, swap(): return lax.ppermute(value, 'tp', [(i, i ^ mask) for i in range(tp_size)])  143 us
    pallas_call x4, Pallas kernels, self_attn(): call(functools.partial(self_kernel, layer), grid, [a_spec] + [pl.BlockSpe...  94.7 us
    pallas_call x3, Pallas kernels, feed_forward(): call(functools.partial(ff_kernel, layer, kinds), tiles, [t_spec, t_spec]...  67.8 us
    pallas_call x2, Pallas kernels, middle(): call(functools.partial(mid_kernel, ctx_len, layer, slot), grid, [a_spec]...  58.6 us
    pallas_call x2, Pallas kernels, body(): call(functools.partial(ff_end_kernel, layers - 1), (2,), [row_spec, row_s...  58.4 us
    ppermute x35, starting transfers between devices, swap(): return lax.ppermute(value, 'tp', [(i, i ^ mask) for i in range(tp_size)])  25.8 us
    pallas_call x1, Pallas kernels, body(): call(functools.partial(ff_last_kernel, layer), tiles, [t_spec, t_spec, b_...  20.5 us
    unnamed x42, local copies, waits for them, and re-layouts  14.6 us
  transfers between devices with their start and end apart: 40, of which 13 were waited for; matrix products, arithmetic and copies ran while one was open for 9% of the time, Pallas kernels for 51%

profile of v2, /device:TPU:0, one launch (start us, length us, event | category | flops | bytes accessed | tf_op | source)
XLA Modules:
  0.0 561.6 jit_solution(12635510845115954777)
XLA Ops:
  6.5 2.0 dynamic-slice_bitcast_fusion.7
  8.5 3.2 collective-permute-start.3
  11.7 5.7 %convert_bitcast_fusion = bf16[2,8,77,2,5,64]{2,5,1,4,3,0:T(8,128)(2,1)S(1)} fusion(bf16[2,1024,2,5,64]{1,4,3,2,0:T(8,128)(2,1)} %param.21, bf16[8,77,1024,1,1,1]{2,0,1,5,4,3:T(8,128)(2,1)} %bitcast.156), kind=kOutput, calls=%fused_computation.2 | convolution fusion | flops 1615595520 | bytes 5459968 | tf_op jit(solution)/shard_map/blc,rcjhd->rbljhd/dot_general | solution.py:356
  18.0 2.5 copy.36
  20.5 2.7 pad_dynamic-slice_fusion
  23.3 2.6 collective-permute-done.3
  26.0 1.7 dynamic-slice_bitcast_fusion.2
  28.2 1.7 collective-permute-start.1
  29.9 0.9 dynamic-slice_bitcast_fusion.10
  30.9 1.0 dynamic-slice_bitcast_fusion.8
  31.8 1.0 dynamic-slice_bitcast_fusion.9
  32.8 0.9 pad_maximum_fusion.2
  33.7 1.4 collective-permute-start.4
  35.1 1.2 constant_dynamic-slice_fusion
  36.3 8.4 %copy.50 = bf16[2,1280,2,1280]{3,1,2,0:T(8,128)(2,1)S(1)} copy(bf16[2,1280,2,1280]{3,2,1,0:T(2,128)(2,1)} %param.23) | data formatting | bytes 26214400 | tf_op args[10]
  45.5 1.1 copy.49
  46.6 2.9 copy-done
  49.6 1.6 pad_maximum_fusion
  51.2 11.7 %collective-permute-done.2.x3 = bf16[2,144,1280]{2,1,0:T(8,128)(2,1)} collective-permute-done((bf16[2,144,1280]{2,1,0:T(8,128)(2,1)}, bf16[2,144,1280]{2,1,0:T(8,128)(2,1)}, u32[]{:S(2)}, u32[]{:S(2)}) %collective-permute-start.2) | collective-permute-done | bytes 737312 | tf_op jit(solution)/shard_map/ppermute | solution.py:309
  62.9 14.4 %shard_map.127 = (f32[2,576,1280]{2,1,0:T(8,128)}, bf16[2,576,1280]{2,1,0:T(8,128)(2,1)}) custom-call(bf16[2,144,1280]{2,1,0:T(8,128)(2,1)} %get-tuple-element.61.x0, bf16[2,144,1280]{2,1,0:T(8,128)(2,1)} %collective-permute-done.x1, bf16[2,144,1280]{2,1,0:T(8,128)(2,1)} %collective-permute-done.1.x2, bf16[2,144,1280]{2,1,0:T(8,128)(2,1)} %collective-permute-done.2.x3, ...), custom_call_target="tpu_custom_call" | custom-call | flops 3774873600 | bytes 16777216 | tf_op jit(solution)/shard_map/pallas_call | solution.py:376
  78.2 1.7 collective-permute-start.7
  79.9 23.6 %shard_map.128 = (bf16[2,576,320]{2,1,0:T(8,128)(2,1)}, bf16[2,576,320]{2,1,0:T(8,128)(2,1)}) custom-call(bf16[2,576,1280]{2,1,0:T(8,128)(2,1)} %get-tuple-element.73.a_ref, bf16[2,960,1280]{2,1,0:T(8,128)(2,1)} %bitcast.141, bf16[2,960,1280]{2,1,0:T(8,128)(2,1)} %collective-permute-done.5.sib_ref), custom_call_target="tpu_custom_call" | custom-call | flops 12457082880 | bytes 16777216 | tf_op jit(solution)/shard_map/pallas_call | solution.py:384
  103.6 24.0 %shard_map.129 = (bf16[2,576,320]{2,1,0:T(8,128)(2,1)}, bf16[2,576,320]{2,1,0:T(8,128)(2,1)}) custom-call(bf16[2,576,1280]{2,1,0:T(8,128)(2,1)} %get-tuple-element.73.a_ref, bf16[4,240,1280]{2,1,0:T(8,128)(2,1)} %bitcast.153, bf16[4,240,1280]{2,1,0:T(8,128)(2,1)} %collective-permute-done.6.sib_ref), custom_call_target="tpu_custom_call" | custom-call | flops 12457082880 | bytes 16777216 | tf_op jit(solution)/shard_map/pallas_call | solution.py:384
  127.5 6.3 %collective-permute-done.7 = bf16[3,320,1280]{2,1,0:T(8,128)(2,1)} collective-permute-done((bf16[3,320,1280]{2,1,0:T(8,128)(2,1)}, bf16[3,320,1280]{2,1,0:T(8,128)(2,1)}, u32[]{:S(2)}, u32[]{:S(2)}) %collective-permute-start.7) | collective-permute-done | bytes 2457632 | tf_op jit(solution)/shard_map/ppermute | solution.py:309
  134.4 1.4 collective-permute-start.10
  136.3 9.8 %collective-permute-done.10.kv3 = bf16[2,2,80,640]{3,2,1,0:T(8,128)(2,1)S(1)} collective-permute-done((bf16[2,2,80,640]{3,2,1,0:T(8,128)(2,1)}, bf16[2,2,80,640]{3,2,1,0:T(8,128)(2,1)S(1)}, u32[]{:S(2)}, u32[]{:S(2)}) %collective-permute-start.10) | collective-permute-done | bytes 409632 | tf_op jit(solution)/shard_map/ppermute | solution.py:309
  146.6 1.0 collective-permute-done.8.kv1
  147.6 1.7 collective-permute-start.9
  149.3 10.0 %collective-permute-done.9.kv2 = bf16[2,2,80,640]{3,2,1,0:T(8,128)(2,1)S(1)} collective-permute-done((bf16[2,2,80,640]{3,2,1,0:T(8,128)(2,1)}, bf16[2,2,80,640]{3,2,1,0:T(8,128)(2,1)S(1)}, u32[]{:S(2)}, u32[]{:S(2)}) %collective-permute-start.9) | collective-permute-done | bytes 409632 | tf_op jit(solution)/shard_map/ppermute | solution.py:309
  160.1 1.2 copy-done.16
  161.3 1.6 slice_bitcast_fusion.6
  163.5 2.0 dynamic-slice_bitcast_fusion.6
  165.5 2.7 dynamic-slice_bitcast_fusion
  168.2 1.7 collective-permute-start.15
  170.5 29.3 %shard_map.130 = (f32[2,576,1280]{2,1,0:T(8,128)}, bf16[2,576,1280]{2,1,0:T(8,128)(2,1)}) custom-call(f32[2,576,1280]{2,1,0:T(8,128)} %get-tuple-element.65.h_ref, bf16[2,576,320]{2,1,0:T(8,128)(2,1)} %get-tuple-element.71.o0, bf16[2,576,320]{2,1,0:T(8,128)(2,1)} %get-tuple-element.72.o1, ...), custom_call_target="tpu_custom_call", output_to_operand_aliasing={{0}: (0, {})} | custom-call | flops 15099494400 | bytes 16777216 | tf_op jit(solution)/shard_map/pallas_call | solution.py:399
  199.8 31.1 %shard_map.131.h_ref = f32[2,576,1280]{2,1,0:T(8,128)} custom-call(f32[2,576,1280]{2,1,0:T(8,128)} %get-tuple-element.80.h_ref, bf16[2,576,1280]{2,1,0:T(8,128)(2,1)} %get-tuple-element.87.a_ref, f32[2,2,1280]{2,1,0:T(2,128)} %rest_0_.3, f32[2,2,1280]{2,1,0:T(2,128)} %collective-permute-done.16.rest_1_.b1, ...), custom_call_target="tpu_custom_call", output_to_operand_aliasing={{}: (0, {})} | custom-call | flops 22649241600 | bytes 16777216 | tf_op jit(solution)/shard_map/pallas_call | solution.py:422
  231.7 1.4 slice.168
  233.3 1.6 pad_maximum_fusion.1
  234.9 1.7 collective-permute-start.21
  236.9 1.0 collective-permute-start.22
  238.5 52.9 %collective-permute-done.20.rest_0_.b2 = f32[2,2,1280]{2,1,0:T(2,128)} collective-permute-done((f32[2,2,1280]{2,1,0:T(2,128)}, f32[2,2,1280]{2,1,0:T(2,128)}, u32[]{:S(2)}, u32[]{:S(2)}) %collective-permute-start.20) | collective-permute-done | bytes 20512 | tf_op jit(solution)/shard_map/ppermute | solution.py:309
  291.4 18.4 %shard_map.132.h_ref = f32[2,576,1280]{2,1,0:T(8,128)} custom-call(f32[2,576,1280]{2,1,0:T(8,128)} %shard_map.131.h_ref, bf16[2,576,1280]{2,1,0:T(8,128)(2,1)} %get-tuple-element.87.a_ref, f32[2,2,1280]{2,1,0:T(2,128)} %collective-permute-done.20.rest_0_.b2, bf16[4,3,320,1280]{3,2,1,0:T(8,128)(2,1)} %bitcast.146), custom_call_target="tpu_custom_call", output_to_operand_aliasing={{}: (0, {})} | custom-call | flops 11324620800 | bytes 16777216 | tf_op jit(solution)/shard_map/pallas_call | solution.py:422
  309.8 20.5 %shard_map.133 = (f32[2,576,1280]{2,1,0:T(8,128)}, bf16[2,576,1280]{2,1,0:T(8,128)(2,1)}) custom-call(f32[2,576,1280]{2,1,0:T(8,128)} %shard_map.132.h_ref, bf16[2,576,1280]{2,1,0:T(8,128)(2,1)} %get-tuple-element.87.a_ref, f32[2,2,1280]{2,1,0:T(2,128)} %collective-permute-done.22.b1_ref.b3, ...), custom_call_target="tpu_custom_call", output_to_operand_aliasing={{0}: (0, {})} | custom-call | flops 11324620800 | bytes 16777216 | tf_op jit(solution)/shard_map/pallas_call | solution.py:465
  330.5 4.0 slice.177
  334.5 1.6 collective-permute-start.25
  337.0 23.6 %shard_map.134 = (bf16[2,576,320]{2,1,0:T(8,128)(2,1)}, bf16[2,576,320]{2,1,0:T(8,128)(2,1)}) custom-call(bf16[2,576,1280]{2,1,0:T(8,128)(2,1)} %get-tuple-element.100.a_ref, bf16[2,960,1280]{2,1,0:T(8,128)(2,1)} %bitcast.143, bf16[2,960,1280]{2,1,0:T(8,128)(2,1)} %collective-permute-done.5.sib_ref), custom_call_target="tpu_custom_call" | custom-call | flops 12457082880 | bytes 16777216 | tf_op jit(solution)/shard_map/pallas_call | solution.py:384
  360.6 23.6 %shard_map.135 = (bf16[2,576,320]{2,1,0:T(8,128)(2,1)}, bf16[2,576,320]{2,1,0:T(8,128)(2,1)}) custom-call(bf16[2,576,1280]{2,1,0:T(8,128)(2,1)} %get-tuple-element.100.a_ref, bf16[4,240,1280]{2,1,0:T(8,128)(2,1)} %bitcast.155, bf16[4,240,1280]{2,1,0:T(8,128)(2,1)} %collective-permute-done.24.sib_ref), custom_call_target="tpu_custom_call" | custom-call | flops 12457082880 | bytes 16777216 | tf_op jit(solution)/shard_map/pallas_call | solution.py:384
  384.2 23.9 %collective-permute-done.25.rest_3_ = bf16[1,1280,1280]{2,1,0:T(8,128)(2,1)} collective-permute-done((bf16[1,1280,1280]{2,1,0:T(8,128)(2,1)}, bf16[1,1280,1280]{2,1,0:T(8,128)(2,1)}, u32[]{:S(2)}, u32[]{:S(2)}) %collective-permute-start.25) | collective-permute-done | bytes 3276832 | tf_op jit(solution)/shard_map/ppermute | solution.py:309
  408.1 29.3 %shard_map.136 = (f32[2,576,1280]{2,1,0:T(8,128)}, bf16[2,576,1280]{2,1,0:T(8,128)(2,1)}) custom-call(f32[2,576,1280]{2,1,0:T(8,128)} %get-tuple-element.93.h_ref, bf16[2,576,320]{2,1,0:T(8,128)(2,1)} %get-tuple-element.98.o0, bf16[2,576,320]{2,1,0:T(8,128)(2,1)} %get-tuple-element.99.o1, ...), custom_call_target="tpu_custom_call", output_to_operand_aliasing={{0}: (0, {})} | custom-call | flops 15099494400 | bytes 16777216 | tf_op jit(solution)/shard_map/pallas_call | solution.py:399
  438.0 18.3 %shard_map.137.h_ref = f32[2,576,1280]{2,1,0:T(8,128)} custom-call(f32[2,576,1280]{2,1,0:T(8,128)} %get-tuple-element.110.h_ref, bf16[2,576,1280]{2,1,0:T(8,128)(2,1)} %get-tuple-element.111.a_ref, f32[2,2,1280]{2,1,0:T(2,128)} %rest_0_.3, bf16[2,2,1280,1280]{3,2,1,0:T(8,128)(2,1)} %bitcast.118, ...), custom_call_target="tpu_custom_call", output_to_operand_aliasing={{}: (0, {})} | custom-call | flops 11324620800 | bytes 16777216 | tf_op jit(solution)/shard_map/pallas_call | solution.py:422
  456.3 29.2 %shard_map.138 = bf16[4,1,144,1280]{3,2,1,0:T(8,128)(2,1)} custom-call(f32[2,576,1280]{2,1,0:T(8,128)} %shard_map.137.h_ref, bf16[2,576,1280]{2,1,0:T(8,128)(2,1)} %get-tuple-element.111.a_ref, f32[2,2,1280]{2,1,0:T(2,128)} %collective-permute-done.16.rest_1_.b1, f32[2,2,1280]{2,1,0:T(2,128)} %collective-permute-done.20.rest_0_.b2, ...), custom_call_target="tpu_custom_call" | custom-call | flops 16986931200 | bytes 16777216 | tf_op jit(solution)/shard_map/pallas_call | solution.py:480
  485.5 1.8 broadcast_in_dim.21
  487.4 1.1 slice_bitcast_fusion.1
  488.6 29.2 %shard_map.139 = bf16[4,1,144,1280]{3,2,1,0:T(8,128)(2,1)} custom-call(f32[2,576,1280]{2,1,0:T(8,128)} %shard_map.137.h_ref, bf16[2,576,1280]{2,1,0:T(8,128)(2,1)} %get-tuple-element.111.a_ref, f32[2,2,1280]{2,1,0:T(2,128)} %collective-permute-done.16.rest_1_.b1, f32[2,2,1280]{2,1,0:T(2,128)} %collective-permute-done.20.rest_0_.b2, ...), custom_call_target="tpu_custom_call" | custom-call | flops 16986931200 | bytes 16777216 | tf_op jit(solution)/shard_map/pallas_call | solution.py:480
  517.8 2.2 slice_bitcast_fusion
  520.5 1.6 collective-permute-start.31
  523.3 1.0 collective-permute-start.34
  524.3 1.7 bitcast_dynamic-update-slice_fusion.5
  526.0 0.8 bitcast_dynamic-update-slice_fusion.4
  526.8 5.2 collective-permute-done.31
  532.0 0.8 bitcast_dynamic-update-slice_fusion.3
  532.7 7.1 %collective-permute-done.32 = bf16[1,144,1280]{2,1,0:T(8,128)(2,1)S(1)} collective-permute-done((bf16[1,144,1280]{2,1,0:T(8,128)(2,1)S(1)}, bf16[1,144,1280]{2,1,0:T(8,128)(2,1)S(1)}, u32[]{:S(2)}, u32[]{:S(2)}) %collective-permute-start.32) | collective-permute-done | bytes 368672 | tf_op jit(solution)/shard_map/ppermute | solution.py:309
  540.6 6.3 %collective-permute-done.33 = bf16[1,144,1280]{2,1,0:T(8,128)(2,1)S(1)} collective-permute-done((bf16[1,144,1280]{2,1,0:T(8,128)(2,1)S(1)}, bf16[1,144,1280]{2,1,0:T(8,128)(2,1)S(1)}, u32[]{:S(2)}, u32[]{:S(2)}) %collective-permute-start.33) | collective-permute-done | bytes 368672 | tf_op jit(solution)/shard_map/ppermute | solution.py:309
  547.7 6.2 %collective-permute-done.34 = bf16[1,144,1280]{2,1,0:T(8,128)(2,1)S(1)} collective-permute-done((bf16[1,144,1280]{2,1,0:T(8,128)(2,1)S(1)}, bf16[1,144,1280]{2,1,0:T(8,128)(2,1)S(1)}, u32[]{:S(2)}, u32[]{:S(2)}) %collective-permute-start.34) | collective-permute-done | bytes 368672 | tf_op jit(solution)/shard_map/ppermute | solution.py:309
  (110 shorter events, 13.8 us)
Async XLA Ops:
  6.5 71.0 %all-gather.6.cloned.1.call-start = ((), (), s32[]{:S(2)}) async-start(), calls=%async_computation | async-start | bytes 3072000 | tf_op jit(solution)/shard_map/all_gather | solution.py:333
  8.5 17.4 %collective-permute-start.3 = (bf16[240,1280]{1,0:T(8,128)(2,1)}, bf16[240,1280]{1,0:T(8,128)(2,1)}, u32[]{:S(2)}, u32[]{:S(2)}) collective-permute-start(bf16[240,1280]{1,0:T(8,128)(2,1)} %dynamic-slice_bitcast_fusion.7), channel_id=1, source_target_pairs={{0,2},{1,3},{2,0},{3,1},{4,6},{5,7},{6,4},{7,5},{8,10},{9,11},{10,... | collective-permute-start | bytes 1843208 | tf_op jit(solution)/shard_map/ppermute | solution.py:309
  20.5 5.5 copy-start.1
  25.9 107.9 %all-gather.8.cloned.1.call-start = ((), (), s32[]{:S(2)}) async-start(), calls=%async_computation.1 | async-start | bytes 3072000 | tf_op jit(solution)/shard_map/all_gather | solution.py:333
  25.9 54.0 %collective-permute-start.5 = (bf16[2,960,1280]{2,1,0:T(8,128)(2,1)}, bf16[2,960,1280]{2,1,0:T(8,128)(2,1)}, u32[]{:S(2)}, u32[]{:S(2)}) collective-permute-start(bf16[2,960,1280]{2,1,0:T(8,128)(2,1)} %bitcast.140), channel_id=1, source_target_pairs={{0,1},{1,0},{2,3},{3,2},{4,5},{5,4},{6,7},{7,6},{8,9},{9,8},{10,11... | collective-permute-start | bytes 14745608 | tf_op jit(solution)/shard_map/ppermute | solution.py:309
  27.7 23.5 %collective-permute-start = (bf16[2,144,1280]{2,1,0:T(8,128)(2,1)}, bf16[2,144,1280]{2,1,0:T(8,128)(2,1)}, u32[]{:S(2)}, u32[]{:S(2)}) collective-permute-start(bf16[2,144,1280]{2,1,0:T(8,128)(2,1)} %get-tuple-element.119), channel_id=1, source_target_pairs={{0,1},{1,0},{2,3},{3,2},{4,5},{5,4},{6,7},{7,6},{8,9},{9,8},{10,11... | collective-permute-start | bytes 2211848 | tf_op jit(solution)/shard_map/ppermute | solution.py:309
  28.2 23.1 %collective-permute-start.1 = (bf16[2,144,1280]{2,1,0:T(8,128)(2,1)}, bf16[2,144,1280]{2,1,0:T(8,128)(2,1)}, u32[]{:S(2)}, u32[]{:S(2)}) collective-permute-start(bf16[2,144,1280]{2,1,0:T(8,128)(2,1)} %get-tuple-element.118), channel_id=1, source_target_pairs={{0,2},{1,3},{2,0},{3,1},{4,6},{5,7},{6,4},{7,5},{8,10},{9,11},{10,... | collective-permute-start | bytes 2211848 | tf_op jit(solution)/shard_map/ppermute | solution.py:309
  29.9 33.0 %collective-permute-start.2 = (bf16[2,144,1280]{2,1,0:T(8,128)(2,1)}, bf16[2,144,1280]{2,1,0:T(8,128)(2,1)}, u32[]{:S(2)}, u32[]{:S(2)}) collective-permute-start(bf16[2,144,1280]{2,1,0:T(8,128)(2,1)} %get-tuple-element.117), channel_id=1, source_target_pairs={{0,3},{1,2},{2,1},{3,0},{4,7},{5,6},{6,5},{7,4},{8,11},{9,10},{10,... | collective-permute-start | bytes 2211848 | tf_op jit(solution)/shard_map/ppermute | solution.py:309
  33.7 43.6 %collective-permute-start.4 = (bf16[240,1280]{1,0:T(8,128)(2,1)}, bf16[240,1280]{1,0:T(8,128)(2,1)}, u32[]{:S(2)}, u32[]{:S(2)}) collective-permute-start(bf16[240,1280]{1,0:T(8,128)(2,1)} %pad_maximum_fusion.2), channel_id=1, source_target_pairs={{0,2},{1,3},{2,0},{3,1},{4,6},{5,7},{6,4},{7,5},{8,10},{9,11},{10,... | collective-permute-start | bytes 1843208 | tf_op jit(solution)/shard_map/ppermute | solution.py:309
  44.7 4.8 copy-start
  77.3 153.8 %all-gather.10.cloned.1.call-start = ((), (), s32[]{:S(2)}) async-start(), calls=%async_computation.2 | async-start | bytes 12288000 | tf_op jit(solution)/shard_map/all_gather | solution.py:333
  77.6 26.0 %collective-permute-start.6 = (bf16[4,240,1280]{2,1,0:T(8,128)(2,1)}, bf16[4,240,1280]{2,1,0:T(8,128)(2,1)}, u32[]{:S(2)}, u32[]{:S(2)}) collective-permute-start(bf16[4,240,1280]{2,1,0:T(8,128)(2,1)} %bitcast.152), channel_id=1, source_target_pairs={{0,1},{1,0},{2,3},{3,2},{4,5},{5,4},{6,7},{7,6},{8,9},{9,8},{10,11... | collective-permute-start | bytes 7372808 | tf_op jit(solution)/shard_map/ppermute | solution.py:309
  78.2 55.6 %collective-permute-start.7 = (bf16[3,320,1280]{2,1,0:T(8,128)(2,1)}, bf16[3,320,1280]{2,1,0:T(8,128)(2,1)}, u32[]{:S(2)}, u32[]{:S(2)}) collective-permute-start(bf16[3,320,1280]{2,1,0:T(8,128)(2,1)} %pad_maximum_fusion), channel_id=1, source_target_pairs={{0,2},{1,3},{2,0},{3,1},{4,6},{5,7},{6,4},{7,5},{8,10},{9,11},{10,... | collective-permute-start | bytes 7372808 | tf_op jit(solution)/shard_map/ppermute | solution.py:309
  79.9 119.9 %collective-permute-start.17 = (bf16[2,2,1280,1280]{3,2,1,0:T(8,128)(2,1)}, bf16[2,2,1280,1280]{3,2,1,0:T(8,128)(2,1)}, u32[]{:S(2)}, u32[]{:S(2)}) collective-permute-start(bf16[2,2,1280,1280]{3,2,1,0:T(8,128)(2,1)} %bitcast.115), channel_id=1, source_target_pairs={{0,1},{1,0},{2,3},{3,2},{4,5},{5,4},{6,7},{7,6},{8,9},{9,8},{10,11... | collective-permute-start | bytes 39321608 | tf_op jit(solution)/shard_map/ppermute | solution.py:309
  133.8 196.6 %all-gather.12.cloned.1.call-start = ((), (), s32[]{:S(2)}) async-start(), calls=%async_computation.3 | async-start | bytes 3072000 | tf_op jit(solution)/shard_map/all_gather | solution.py:333
  133.9 65.9 %collective-permute-start.18 = (bf16[2,1280,1280]{2,1,0:T(8,128)(2,1)}, bf16[2,1280,1280]{2,1,0:T(8,128)(2,1)}, u32[]{:S(2)}, u32[]{:S(2)}) collective-permute-start(bf16[2,1280,1280]{2,1,0:T(8,128)(2,1)} %rest_2_.1), channel_id=1, source_target_pairs={{0,1},{1,0},{2,3},{3,2},{4,5},{5,4},{6,7},{7,6},{8,9},{9,8},{10,11... | collective-permute-start | bytes 19660808 | tf_op jit(solution)/shard_map/ppermute | solution.py:309
  133.9 25.4 %collective-permute-start.11 = (bf16[2,320,1280]{2,1,0:T(8,128)(2,1)}, bf16[2,320,1280]{2,1,0:T(8,128)(2,1)S(1)}, u32[]{:S(2)}, u32[]{:S(2)}) collective-permute-start(bf16[2,320,1280]{2,1,0:T(8,128)(2,1)} %bitcast.125), channel_id=1, source_target_pairs={{0,1},{1,0},{2,3},{3,2},{4,5},{5,4},{6,7},{7,6},{8,9},{9,8},{10,11... | collective-permute-start | bytes 4915208 | tf_op jit(solution)/shard_map/ppermute | solution.py:309
  134.4 11.7 %collective-permute-start.10 = (bf16[2,2,80,640]{3,2,1,0:T(8,128)(2,1)}, bf16[2,2,80,640]{3,2,1,0:T(8,128)(2,1)S(1)}, u32[]{:S(2)}, u32[]{:S(2)}) collective-permute-start(bf16[2,2,80,640]{3,2,1,0:T(8,128)(2,1)} %get-tuple-element.121), channel_id=1, source_target_pairs={{0,3},{1,2},{2,1},{3,0},{4,7},{5,6},{6,5},{7,4},{8,11},{9,10},{10,... | collective-permute-start | bytes 1228808 | tf_op jit(solution)/shard_map/ppermute | solution.py:309
  135.8 11.8 %collective-permute-start.8 = (bf16[2,2,80,640]{3,2,1,0:T(8,128)(2,1)}, bf16[2,2,80,640]{3,2,1,0:T(8,128)(2,1)S(1)}, u32[]{:S(2)}, u32[]{:S(2)}) collective-permute-start(bf16[2,2,80,640]{3,2,1,0:T(8,128)(2,1)} %get-tuple-element.122), channel_id=1, source_target_pairs={{0,1},{1,0},{2,3},{3,2},{4,5},{5,4},{6,7},{7,6},{8,9},{9,8},{10,11... | collective-permute-start | bytes 1228808 | tf_op jit(solution)/shard_map/ppermute | solution.py:309
  146.1 13.2 %copy-start.17 = (bf16[2,2,80,640]{3,2,1,0:T(8,128)(2,1)}, bf16[2,2,80,640]{3,2,1,0:T(8,128)(2,1)S(1)}, u32[]{:S(2)}) copy-start(bf16[2,2,80,640]{3,2,1,0:T(8,128)(2,1)S(1)} %collective-permute-done.10.kv3) | copy-start | bytes 1228804
  146.1 24.0 %collective-permute-start.14 = (bf16[4,240,1280]{2,1,0:T(8,128)(2,1)}, bf16[4,240,1280]{2,1,0:T(8,128)(2,1)}, u32[]{:S(2)}, u32[]{:S(2)}) collective-permute-start(bf16[4,240,1280]{2,1,0:T(8,128)(2,1)} %bitcast.150), channel_id=1, source_target_pairs={{0,1},{1,0},{2,3},{3,2},{4,5},{5,4},{6,7},{7,6},{8,9},{9,8},{10,11... | collective-permute-start | bytes 7372808 | tf_op jit(solution)/shard_map/ppermute | solution.py:309
  147.6 11.7 %copy-start.18 = (bf16[2,2,80,640]{3,2,1,0:T(8,128)(2,1)}, bf16[2,2,80,640]{3,2,1,0:T(8,128)(2,1)S(1)}, u32[]{:S(2)}) copy-start(bf16[2,2,80,640]{3,2,1,0:T(8,128)(2,1)S(1)} %collective-permute-done.8.kv1) | copy-start | bytes 1228804
  147.6 11.7 %collective-permute-start.9 = (bf16[2,2,80,640]{3,2,1,0:T(8,128)(2,1)}, bf16[2,2,80,640]{3,2,1,0:T(8,128)(2,1)S(1)}, u32[]{:S(2)}, u32[]{:S(2)}) collective-permute-start(bf16[2,2,80,640]{3,2,1,0:T(8,128)(2,1)} %get-tuple-element.123), channel_id=1, source_target_pairs={{0,2},{1,3},{2,0},{3,1},{4,6},{5,7},{6,4},{7,5},{8,10},{9,11},{10,... | collective-permute-start | bytes 1228808 | tf_op jit(solution)/shard_map/ppermute | solution.py:309
  159.3 0.8 copy-start.19
  159.3 8.9 %collective-permute-start.12 = (bf16[2,320,1280]{2,1,0:T(8,128)(2,1)}, bf16[2,320,1280]{2,1,0:T(8,128)(2,1)}, u32[]{:S(2)}, u32[]{:S(2)}) collective-permute-start(bf16[2,320,1280]{2,1,0:T(8,128)(2,1)} %bitcast.130), channel_id=1, source_target_pairs={{0,1},{1,0},{2,3},{3,2},{4,5},{5,4},{6,7},{7,6},{8,9},{9,8},{10,11... | collective-permute-start | bytes 4915208 | tf_op jit(solution)/shard_map/ppermute | solution.py:309
  160.1 1.2 copy-start.16
  161.3 8.6 %collective-permute-start.13 = (bf16[2,320,1280]{2,1,0:T(8,128)(2,1)}, bf16[2,320,1280]{2,1,0:T(8,128)(2,1)}, u32[]{:S(2)}, u32[]{:S(2)}) collective-permute-start(bf16[2,320,1280]{2,1,0:T(8,128)(2,1)} %bitcast.135), channel_id=1, source_target_pairs={{0,1},{1,0},{2,3},{3,2},{4,5},{5,4},{6,7},{7,6},{8,9},{9,8},{10,11... | collective-permute-start | bytes 4915208 | tf_op jit(solution)/shard_map/ppermute | solution.py:309
  168.2 31.6 %collective-permute-start.15 = (bf16[240,1280]{1,0:T(8,128)(2,1)}, bf16[240,1280]{1,0:T(8,128)(2,1)}, u32[]{:S(2)}, u32[]{:S(2)}) collective-permute-start(bf16[240,1280]{1,0:T(8,128)(2,1)} %dynamic-slice_bitcast_fusion.6), channel_id=1, source_target_pairs={{0,2},{1,3},{2,0},{3,1},{4,6},{5,7},{6,4},{7,5},{8,10},{9,11},{10,... | collective-permute-start | bytes 1843208 | tf_op jit(solution)/shard_map/ppermute | solution.py:309
  169.9 29.9 %collective-permute-start.16 = (f32[2,2,1280]{2,1,0:T(2,128)}, f32[2,2,1280]{2,1,0:T(2,128)}, u32[]{:S(2)}, u32[]{:S(2)}) collective-permute-start(f32[2,2,1280]{2,1,0:T(2,128)} %rest_0_.3), channel_id=1, source_target_pairs={{0,1},{1,0},{2,3},{3,2},{4,5},{5,4},{6,7},{7,6},{8,9},{9,8},{10,11... | collective-permute-start | bytes 61448 | tf_op jit(solution)/shard_map/ppermute | solution.py:309
  170.2 60.8 %collective-permute-start.19 = (bf16[2,320,1280]{2,1,0:T(8,128)(2,1)}, bf16[2,320,1280]{2,1,0:T(8,128)(2,1)}, u32[]{:S(2)}, u32[]{:S(2)}) collective-permute-start(bf16[2,320,1280]{2,1,0:T(8,128)(2,1)} %dynamic-slice_bitcast_fusion), channel_id=1, source_target_pairs={{0,2},{1,3},{2,0},{3,1},{4,6},{5,7},{6,4},{7,5},{8,10},{9,11},{10,... | collective-permute-start | bytes 4915208 | tf_op jit(solution)/shard_map/ppermute | solution.py:309
  230.9 2.2 copy-start.3
  230.9 2.3 copy-start.4
  231.1 78.8 %collective-permute-start.23 = (bf16[4,3,320,1280]{3,2,1,0:T(8,128)(2,1)}, bf16[4,3,320,1280]{3,2,1,0:T(8,128)(2,1)}, u32[]{:S(2)}, u32[]{:S(2)}) collective-permute-start(bf16[4,3,320,1280]{3,2,1,0:T(8,128)(2,1)} %bitcast.145), channel_id=1, source_target_pairs={{0,1},{1,0},{2,3},{3,2},{4,5},{5,4},{6,7},{7,6},{8,9},{9,8},{10,11... | collective-permute-start | bytes 29491208 | tf_op jit(solution)/shard_map/ppermute | solution.py:309
  231.1 206.4 %all-gather.14.cloned.1.call-start = ((), (), s32[]{:S(2)}) async-start(), calls=%async_computation.4 | async-start | bytes 8192000 | tf_op jit(solution)/shard_map/all_gather | solution.py:333
  233.2 4.7 copy-start.13
  233.2 4.6 copy-start.14
  233.2 4.6 copy-start.15
  234.9 74.9 %collective-permute-start.21 = (bf16[4,240,1280]{2,1,0:T(8,128)(2,1)}, bf16[4,240,1280]{2,1,0:T(8,128)(2,1)}, u32[]{:S(2)}, u32[]{:S(2)}) collective-permute-start(bf16[4,240,1280]{2,1,0:T(8,128)(2,1)} %pad_maximum_fusion.1), channel_id=1, source_target_pairs={{0,2},{1,3},{2,0},{3,1},{4,6},{5,7},{6,4},{7,5},{8,10},{9,11},{10,... | collective-permute-start | bytes 7372808 | tf_op jit(solution)/shard_map/ppermute | solution.py:309
  236.5 54.8 %collective-permute-start.20 = (f32[2,2,1280]{2,1,0:T(2,128)}, f32[2,2,1280]{2,1,0:T(2,128)}, u32[]{:S(2)}, u32[]{:S(2)}) collective-permute-start(f32[2,2,1280]{2,1,0:T(2,128)} %rest_0_.3), channel_id=1, source_target_pairs={{0,2},{1,3},{2,0},{3,1},{4,6},{5,7},{6,4},{7,5},{8,10},{9,11},{10,... | collective-permute-start | bytes 61448 | tf_op jit(solution)/shard_map/ppermute | solution.py:309
  236.9 72.9 %collective-permute-start.22 = (f32[2,2,1280]{2,1,0:T(2,128)}, f32[2,2,1280]{2,1,0:T(2,128)}, u32[]{:S(2)}, u32[]{:S(2)}) collective-permute-start(f32[2,2,1280]{2,1,0:T(2,128)} %rest_0_.3), channel_id=1, source_target_pairs={{0,3},{1,2},{2,1},{3,0},{4,7},{5,6},{6,5},{7,4},{8,11},{9,10},{10,... | collective-permute-start | bytes 61448 | tf_op jit(solution)/shard_map/ppermute | solution.py:309
  330.4 5.9 %copy-start.7 = (f32[1,1280]{1,0:T(1,128)S(1)}, f32[1,1280]{1,0:T(1,128)}, u32[]{:S(2)}) copy-start(f32[1,1280]{1,0:T(1,128)} %get-tuple-element.134) | copy-start | bytes 15364
  330.4 5.9 %copy-start.8 = (f32[1,1280]{1,0:T(1,128)S(1)}, f32[1,1280]{1,0:T(1,128)}, u32[]{:S(2)}) copy-start(f32[1,1280]{1,0:T(1,128)} %get-tuple-element.135) | copy-start | bytes 15364
  330.4 5.9 %copy-start.9 = (f32[1,1280]{1,0:T(1,128)S(1)}, f32[1,1280]{1,0:T(1,128)}, u32[]{:S(2)}) copy-start(f32[1,1280]{1,0:T(1,128)} %get-tuple-element.136) | copy-start | bytes 15364
  330.4 5.9 %copy-start.10 = (f32[1,1280]{1,0:T(1,128)S(1)}, f32[1,1280]{1,0:T(1,128)}, u32[]{:S(2)}) copy-start(f32[1,1280]{1,0:T(1,128)} %get-tuple-element.137) | copy-start | bytes 15364
  330.4 5.9 %copy-start.11 = (f32[1,1280]{1,0:T(1,128)S(1)}, f32[1,1280]{1,0:T(1,128)}, u32[]{:S(2)}) copy-start(f32[1,1280]{1,0:T(1,128)} %get-tuple-element.138) | copy-start | bytes 15364
  330.5 5.9 %copy-start.12 = (f32[1,1280]{1,0:T(1,128)S(1)}, f32[1,1280]{1,0:T(1,128)}, u32[]{:S(2)}) copy-start(f32[1,1280]{1,0:T(1,128)} %get-tuple-element.148) | copy-start | bytes 15364
  330.5 30.2 %collective-permute-start.24 = (bf16[4,240,1280]{2,1,0:T(8,128)(2,1)}, bf16[4,240,1280]{2,1,0:T(8,128)(2,1)}, u32[]{:S(2)}, u32[]{:S(2)}) collective-permute-start(bf16[4,240,1280]{2,1,0:T(8,128)(2,1)} %bitcast.154), channel_id=1, source_target_pairs={{0,1},{1,0},{2,3},{3,2},{4,5},{5,4},{6,7},{7,6},{8,9},{9,8},{10,11... | collective-permute-start | bytes 7372808 | tf_op jit(solution)/shard_map/ppermute | solution.py:309
  334.5 73.6 %collective-permute-start.25 = (bf16[1,1280,1280]{2,1,0:T(8,128)(2,1)}, bf16[1,1280,1280]{2,1,0:T(8,128)(2,1)}, u32[]{:S(2)}, u32[]{:S(2)}) collective-permute-start(bf16[1,1280,1280]{2,1,0:T(8,128)(2,1)} %slice.177), channel_id=1, source_target_pairs={{0,2},{1,3},{2,0},{3,1},{4,6},{5,7},{6,4},{7,5},{8,10},{9,11},{10,... | collective-permute-start | bytes 9830408 | tf_op jit(solution)/shard_map/ppermute | solution.py:309
  336.1 72.0 %collective-permute-start.26 = (bf16[4,240,1280]{2,1,0:T(8,128)(2,1)}, bf16[4,240,1280]{2,1,0:T(8,128)(2,1)}, u32[]{:S(2)}, u32[]{:S(2)}) collective-permute-start(bf16[4,240,1280]{2,1,0:T(8,128)(2,1)} %collective-permute-done.21.rest), channel_id=1, source_target_pairs={{0,1},{1,0},{2,3},{3,2},{4,5},{5,4},{6,7},{7,6},{8,9},{9,8},{10,11... | collective-permute-start | bytes 7372808 | tf_op jit(solution)/shard_map/ppermute | solution.py:309
  437.5 18.8 %collective-permute-start.27 = (bf16[4,2,320,1280]{3,2,1,0:T(8,128)(2,1)}, bf16[4,2,320,1280]{3,2,1,0:T(8,128)(2,1)}, u32[]{:S(2)}, u32[]{:S(2)}) collective-permute-start(bf16[4,2,320,1280]{3,2,1,0:T(8,128)(2,1)} %bitcast.147), channel_id=1, source_target_pairs={{0,1},{1,0},{2,3},{3,2},{4,5},{5,4},{6,7},{7,6},{8,9},{9,8},{10,11... | collective-permute-start | bytes 19660808 | tf_op jit(solution)/shard_map/ppermute | solution.py:309
  437.5 18.8 %collective-permute-start.28 = (bf16[1,1280,1280]{2,1,0:T(8,128)(2,1)}, bf16[1,1280,1280]{2,1,0:T(8,128)(2,1)}, u32[]{:S(2)}, u32[]{:S(2)}) collective-permute-start(bf16[1,1280,1280]{2,1,0:T(8,128)(2,1)} %collective-permute-done.25.rest_3_), channel_id=1, source_target_pairs={{0,1},{1,0},{2,3},{3,2},{4,5},{5,4},{6,7},{7,6},{8,9},{9,8},{10,11... | collective-permute-start | bytes 9830408 | tf_op jit(solution)/shard_map/ppermute | solution.py:309
  485.5 1.9 copy-start.2
  488.5 34.7 %collective-permute-start.29 = (bf16[1,144,1280]{2,1,0:T(8,128)(2,1)}, bf16[1,144,1280]{2,1,0:T(8,128)(2,1)}, u32[]{:S(2)}, u32[]{:S(2)}) collective-permute-start(bf16[1,144,1280]{2,1,0:T(8,128)(2,1)} %get-tuple-element.131), channel_id=1, source_target_pairs={{0,1},{1,0},{2,3},{3,2},{4,5},{5,4},{6,7},{7,6},{8,9},{9,8},{10,11... | collective-permute-start | bytes 1105928 | tf_op jit(solution)/shard_map/ppermute | solution.py:309
  517.8 2.7 copy-start.6
  517.8 4.7 copy-start.5
  520.0 6.0 %collective-permute-start.30 = (bf16[1,144,1280]{2,1,0:T(8,128)(2,1)S(1)}, bf16[1,144,1280]{2,1,0:T(8,128)(2,1)S(1)}, u32[]{:S(2)}, u32[]{:S(2)}) collective-permute-start(bf16[1,144,1280]{2,1,0:T(8,128)(2,1)S(1)} %get-tuple-element.127), channel_id=1, source_target_pairs={{0,1},{1,0},{2,3},{3,2},{4,5},{5,4},{6,7},{7,6},{8,9},{9,8},{10,11... | collective-permute-start | bytes 1105928 | tf_op jit(solution)/shard_map/ppermute | solution.py:309
  520.5 11.5 %collective-permute-start.31 = (bf16[1,144,1280]{2,1,0:T(8,128)(2,1)S(1)}, bf16[1,144,1280]{2,1,0:T(8,128)(2,1)S(1)}, u32[]{:S(2)}, u32[]{:S(2)}) collective-permute-start(bf16[1,144,1280]{2,1,0:T(8,128)(2,1)S(1)} %copy-done.6), channel_id=1, source_target_pairs={{0,2},{1,3},{2,0},{3,1},{4,6},{5,7},{6,4},{7,5},{8,10},{9,11},{10,... | collective-permute-start | bytes 1105928 | tf_op jit(solution)/shard_map/ppermute | solution.py:309
  522.2 17.7 %collective-permute-start.32 = (bf16[1,144,1280]{2,1,0:T(8,128)(2,1)S(1)}, bf16[1,144,1280]{2,1,0:T(8,128)(2,1)S(1)}, u32[]{:S(2)}, u32[]{:S(2)}) collective-permute-start(bf16[1,144,1280]{2,1,0:T(8,128)(2,1)S(1)} %get-tuple-element.126), channel_id=1, source_target_pairs={{0,2},{1,3},{2,0},{3,1},{4,6},{5,7},{6,4},{7,5},{8,10},{9,11},{10,... | collective-permute-start | bytes 1105928 | tf_op jit(solution)/shard_map/ppermute | solution.py:309
  522.5 24.4 %collective-permute-start.33 = (bf16[1,144,1280]{2,1,0:T(8,128)(2,1)S(1)}, bf16[1,144,1280]{2,1,0:T(8,128)(2,1)S(1)}, u32[]{:S(2)}, u32[]{:S(2)}) collective-permute-start(bf16[1,144,1280]{2,1,0:T(8,128)(2,1)S(1)} %copy-done.5), channel_id=1, source_target_pairs={{0,3},{1,2},{2,1},{3,0},{4,7},{5,6},{6,5},{7,4},{8,11},{9,10},{10,... | collective-permute-start | bytes 1105928 | tf_op jit(solution)/shard_map/ppermute | solution.py:309
  523.3 30.6 %collective-permute-start.34 = (bf16[1,144,1280]{2,1,0:T(8,128)(2,1)S(1)}, bf16[1,144,1280]{2,1,0:T(8,128)(2,1)S(1)}, u32[]{:S(2)}, u32[]{:S(2)}) collective-permute-start(bf16[1,144,1280]{2,1,0:T(8,128)(2,1)S(1)} %get-tuple-element.125), channel_id=1, source_target_pairs={{0,3},{1,2},{2,1},{3,0},{4,7},{5,6},{6,5},{7,4},{8,11},{9,10},{10,... | collective-permute-start | bytes 1105928 | tf_op jit(solution)/shard_map/ppermute | solution.py:309
Sparse Core Ops, SparseCore 0:
  26.0 35.7 all-gather.5
  77.4 35.9 all-gather.7
  133.9 97.0 all-gather.9
  232.7 34.4 all-gather.11
  268.8 68.4 all-gather.13

commit v3 on v2

--- a/solution.py
+++ b/solution.py
@@ -249,16 +249,16 @@
     ff_steps(layer, a_ref, biases, shards, w1, w2, m_scr, sems, finish)
 
 
-def ff_last_kernel(layer, h_ref, a_ref, b1_ref, vec_ref, w_ref, h_out, a_out, w1, w2, m_scr, sems):
+def ff_last_kernel(layer, h_ref, a_ref, b1_ref, vec_ref, w1_ref, w2_ref, h_out, a_out, w1, w2, m_scr, sems):
     def finish(update, first):
         h = h_ref[0] + update + vec_ref[0:1]
         h_out[0] = h
         a_out[0] = layer_norm(h, vec_ref[1:2], vec_ref[2:3])
 
-    ff_steps(layer, a_ref, (b1_ref,), ((w_ref,),), w1, w2, m_scr, sems, finish)
-
-
-def ff_end_kernel(layer, h_ref, a_ref, b1, b2, b3, vec_ref, io_ref, x0, x1, x2, x3, wp_ref, *rest):
+    ff_steps(layer, a_ref, (b1_ref,), ((w1_ref, w2_ref),), w1, w2, m_scr, sems, finish)
+
+
+def ff_end_kernel(layer, h_ref, a_ref, b1, b2, b3, vec_ref, io_ref, x0, x1, wp_ref, *rest):
     refs, (y_ref, w1, w2, m_scr, wp, wp_sem, sems) = rest[:-7], rest[-7:]
     shards = [refs[i:i + 2] for i in range(0, len(refs), 2)]
     tok = x0.shape[1]
@@ -271,7 +271,7 @@
         if first:
             last.wait()
         y = jnp.dot(h.astype(BF16), wp[...], preferred_element_type=F32) + io_ref[3:4]
-        for i, ref in enumerate((x0, x1) if first else (x2, x3)):
+        for i, ref in enumerate((x0, x1)):
             y_ref[i, 0] = (y[i * tok:(i + 1) * tok] + ref[0].astype(F32)).astype(BF16)
 
     ff_steps(layer, a_ref, (b1, b2, b3), shards, w1, w2, m_scr, sems, finish)
@@ -338,9 +338,6 @@
         o2_t = w_o2.reshape(layers, width, channels)
         ff1_t = w_ff1.transpose(0, 2, 1, 3)
 
-        def ff_piece(ff1, ff2, layer):
-            return jnp.concatenate([piece_of(ff1, layer, 2)[0], piece_of(ff2, layer, 1)])
-
         x_rows = latents.reshape(tp_size, mine, tok, channels)
 
         def group_of(array, index):
@@ -360,10 +357,10 @@
         kv_out[0], piece = tie(kv_out[0], far_qkv)
         full_qkv = gather(piece)
         kv_parts = [kv_out[0]] + [swap(kv_out[m], m) for m in (1, 2, 3)]
-        ff_src = ff_piece(ff1_t, w_ff2, 0)
-        far_ff = swap(ff_src, 2)
+        ff_src = [piece_of(ff1_t, 0, 2)[0], piece_of(w_ff2, 0, 1)[0]]
+        far_ff, far_second = swap(ff_src[0], 2), swap(ff_src[1], 2)
         sib_ff1, sib_ff2 = swap(ff1_t, 1), swap(w_ff2, 1)
-        x_parts = list(tie(*x_parts, ff_src, *kv_out))[:tp_size]
+        x_parts = list(tie(*x_parts, *ff_src, *kv_out))[:tp_size]
 
         grid = (mine,)
         total = mine * n_tok
@@ -433,12 +430,16 @@
             rem_sib = swap(rem, 1)
             m0, m1 = self_attn(act, qkv_t, sib_qkv, layer)
             act, m0 = tie(act, m0)
-            if layer == 1:
+            if layer == 0:
+                act, piece = tie(act, far_ff)
+                full_ff = gather(piece)
+            else:
+                m0, rest = tie(m0, next_rest)
                 rest_sib = swap(rest, 1)
             m2, m3 = self_attn(act, rem, rem_sib, layer)
             if layer == 0:
-                act, m3, piece, rest = tie(act, m3, far_ff, full_rest)
-                full_ff = gather(piece)
+                act, m3, piece, rest = tie(act, m3, far_second, full_rest)
+                full_second = gather(piece)
                 rest = rest.reshape(dp_size, -1, channels)
                 rest_sib = swap(rest, 1)
                 act, src_a, src_b, src_c, *src = tie(act, qkv_t, ff1_t, w_ff2, o1_t, q2_t, o2_t)
@@ -446,9 +447,6 @@
                 far_ff1 = swap(piece_of(src_b, 1, 2)[0], 2)
                 next_rest = swap(jnp.concatenate([w[1].reshape(dp_size, -1, channels) for w in src], axis=1), 2)
                 next_ff2 = swap(src_c[1:], 2)
-            else:
-                m3, next_ff2 = tie(m3, next_ff2)
-                next_ff2_sib = swap(next_ff2, 1)
             hidden, act = middle(hidden, [m0, m1, m2, m3], jnp.stack([vecs[i] for i in (6, 2, 3, 7, 4, 5)]),
                                  layer, 0, rest, rest_sib)
             if layer == 0:
@@ -457,42 +455,45 @@
                 hidden = feed_forward(hidden, act, layer, (0, (ff1_t, w_ff2)), (1, (sib_ff1, sib_ff2)))
                 hidden, act, full, piece = tie(hidden, act, full_ff, far_ff1)
                 next_ff = gather(piece)
-                rem = full.reshape(dp_size, 3, ff // dp_size, channels)
+                rem = full.reshape(dp_size, 2, ff // dp_size, channels)
                 rem_sib = swap(rem, 1)
-                hidden = feed_forward(hidden, act, layer, (2, (rem,)))
-                hidden, rest = tie(hidden, next_rest)
+                hidden, second = tie(hidden, full_second[None])
+                second_sib = swap(second, 1)
+                hidden = feed_forward(hidden, act, layer, (2, (rem, second)))
                 after = block_vecs[layer + 1]
                 hidden, act = call(
                     functools.partial(ff_last_kernel, layer), tiles,
-                    [t_spec, t_spec, b_spec[layer], vec_spec(3, channels), any_spec],
+                    [t_spec, t_spec, b_spec[layer], vec_spec(3, channels), any_spec, any_spec],
                     [t_spec, t_spec], [h_shape, a_shape], ff_flops,
                     ff_scratch(1), {0: 0},
-                )(hidden, act, bias[3], jnp.stack([vecs[8], after[0], after[1]]), rem_sib)
-
-        hidden, act, full = tie(hidden, act, next_ff)
+                )(hidden, act, bias[3], jnp.stack([vecs[8], after[0], after[1]]), rem_sib, second_sib)
+
+        hidden, act, full, next_ff2 = tie(hidden, act, next_ff, next_ff2)
+        next_ff2_sib = swap(next_ff2, 1)
         rem = full.reshape(dp_size, 2, ff // dp_size, channels)
         ff_weights = [sib_ff1, sib_ff2, rem, next_ff2, swap(rem, 1), next_ff2_sib]
         hidden = feed_forward(hidden, act, layers - 1, (0, (ff1_t, w_ff2)))
-        y = []
-        for sample in range(mine):
-            row_spec = pl.BlockSpec((1, tile, channels), lambda i, sample=sample: (sample, i, 0))
-            x_spec = pl.BlockSpec((1, tok, channels), lambda i, sample=sample: (sample, 0, 0))
-            parts = call(
-                functools.partial(ff_end_kernel, layers - 1), (2,),
+        parts = [None] * tp_size
+        split = tp_size // 2
+        for half in (1, 0):
+            row_spec = pl.BlockSpec((1, tile, channels), lambda i, half=half: (i, half, 0))
+            pair = call(
+                functools.partial(ff_end_kernel, layers - 1), grid,
                 [row_spec, row_spec] + [b_spec[layers - 1]] * 3 + [vec_spec(1, channels), vec_spec(4, channels)]
-                + [x_spec] * 4 + [any_spec] * 7,
-                pl.BlockSpec((tp_size // 2, 1, tok, channels), lambda i: (i, 0, 0, 0)),
-                jax.ShapeDtypeStruct((tp_size, 1, tok, channels), BF16), 3 * ff_flops // mine,
+                + [x_spec] * 2 + [any_spec] * 7,
+                pl.BlockSpec((split, 1, tok, channels), lambda i: (0, i, 0, 0)),
+                jax.ShapeDtypeStruct((split, mine, tok, channels), BF16), 3 * ff_flops // 2,
                 ff_scratch(3, pltpu.VMEM((channels, channels), BF16), pltpu.SemaphoreType.DMA((1,))),
                 None,
-            )(hidden, act, *bias[1:], vecs[8:9], io_vecs, *x_parts, w_proj, *ff_weights)
-            y.append([parts[0]] + [swap(parts[m], m) for m in (1, 2, 3)])
-            if sample < mine - 1:
-                hidden, parts = tie(hidden, parts)
+            )(hidden, act, *bias[1:], vecs[8:9], io_vecs, *x_parts[half * split:(half + 1) * split], w_proj, *ff_weights)
+            for i in range(split):
+                m = half * split + i
+                parts[m] = swap(pair[i], m) if m else pair[i]
+            if half:
+                hidden, pair = tie(hidden, pair)
         out = jnp.zeros((tp_size, mine, tok, channels), BF16)
-        for m in range(tp_size):
-            for sample in range(mine):
-                out = lax.dynamic_update_slice(out, y[sample][m][None], (me ^ m, sample, 0, 0))
+        for m in (0, 2, 3, 1):
+            out = lax.dynamic_update_index_in_dim(out, parts[m], me ^ m, 0)
         return out.reshape(batch, rows_loc, side, channels)
 
     act_spec = P("dp", "tp", None, None)

time: 569 us -> 510 us (0.90)
  waiting for transfers between devices: 144 us -> 90.5 us
  starting transfers between devices: 26.2 us -> 20.1 us
    ppermute x35 -> x34, waiting for transfers between devices: 143 us -> 90.3 us  [swap(): return lax.ppermute(value, 'tp', [(i, i ^ mask) for i in range(tp_size)])]
    ppermute x35 -> x34, starting transfers between devices: 25.8 us -> 19.3 us  [swap(): return lax.ppermute(value, 'tp', [(i, i ^ mask) for i in range(tp_size)])]
    unnamed x42 -> x38, local copies, waits for them, and re-layouts: 14.6 us -> 17.8 us
  transfers between devices with their start and end apart: 40 -> 40, of which waited for: 13 -> 8; matrix products, arithmetic and copies ran while one was open for 9% -> 11% of each run, Pallas kernels for 51% -> 57%
where the time goes in v3:
time: 510 us; the launch traced here: 502 us
  Pallas kernels  315 us (62%)
  waiting for transfers between devices  90.5 us (18%)
  local copies, waits for them, and re-layouts  53.8 us (11%)
  starting transfers between devices  20.1 us (4%)
  between operations  14.4 us (3%)
  matrix products  5.74 us (1%)
    pallas_call x4, Pallas kernels, self_attn(): call(functools.partial(self_kernel, layer), grid, [a_spec] + [pl.BlockSpe...  94.8 us
    ppermute x34, waiting for transfers between devices, swap(): return lax.ppermute(value, 'tp', [(i, i ^ mask) for i in range(tp_size)])  90.3 us
    pallas_call x3, Pallas kernels, feed_forward(): call(functools.partial(ff_kernel, layer, kinds), tiles, [t_spec, t_spec]...  68.6 us
    pallas_call x2, Pallas kernels, middle(): call(functools.partial(mid_kernel, ctx_len, layer, slot), grid, [a_spec]...  58.6 us
    pallas_call x2, Pallas kernels, body(): call(functools.partial(ff_end_kernel, layers - 1), grid, [row_spec, row_s...  58.1 us
    pallas_call x1, Pallas kernels, body(): call(functools.partial(ff_last_kernel, layer), tiles, [t_spec, t_spec, b_...  20.1 us
    ppermute x34, starting transfers between devices, swap(): return lax.ppermute(value, 'tp', [(i, i ^ mask) for i in range(tp_size)])  19.3 us
    unnamed x38, local copies, waits for them, and re-layouts  17.8 us
  transfers between devices with their start and end apart: 40, of which 8 were waited for; matrix products, arithmetic and copies ran while one was open for 11% of the time, Pallas kernels for 57%

profile of v3, /device:TPU:0, one launch (start us, length us, event | category | flops | bytes accessed | tf_op | source)
XLA Modules:
  0.0 502.2 jit_solution(16113141177565279750)
XLA Ops:
  6.5 2.0 dynamic-slice_bitcast_fusion.8
  8.5 3.2 collective-permute-start.3
  11.7 5.7 %convert_bitcast_fusion = bf16[2,8,77,2,5,64]{2,5,1,4,3,0:T(8,128)(2,1)S(1)} fusion(bf16[2,1024,2,5,64]{1,4,3,2,0:T(8,128)(2,1)} %param.21, bf16[8,77,1024,1,1,1]{2,0,1,5,4,3:T(8,128)(2,1)} %bitcast.149), kind=kOutput, calls=%fused_computation.2 | convolution fusion | flops 1615595520 | bytes 5459968 | tf_op jit(solution)/shard_map/blc,rcjhd->rbljhd/dot_general | solution.py:353
  18.0 2.5 copy.34
  20.5 2.7 pad_dynamic-slice_fusion
  23.3 2.6 collective-permute-done.3
  26.0 1.7 dynamic-slice_bitcast_fusion.3
  28.2 1.7 collective-permute-start.1
  29.9 0.9 dynamic-slice_bitcast_fusion.9
  30.9 1.0 dynamic-slice_bitcast_fusion.10
  31.8 1.0 dynamic-slice_bitcast_fusion.11
  32.8 0.9 pad_maximum_fusion.1
  33.7 1.4 collective-permute-start.4
  35.1 12.5 %copy.48 = bf16[2,1280,2,1280]{3,1,2,0:T(8,128)(2,1)} copy(bf16[2,1280,2,1280]{3,2,1,0:T(2,128)(2,1)} %param.23) | data formatting | bytes 26214400 | tf_op args[10]
  47.5 2.8 dynamic-slice_bitcast_fusion.1
  50.3 0.7 slice.143
  51.0 0.6 copy.47
  51.6 2.1 dynamic-slice_bitcast_fusion.2
  53.7 9.2 %collective-permute-done.2.x3.x1 = bf16[2,144,1280]{2,1,0:T(8,128)(2,1)} collective-permute-done((bf16[2,144,1280]{2,1,0:T(8,128)(2,1)}, bf16[2,144,1280]{2,1,0:T(8,128)(2,1)}, u32[]{:S(2)}, u32[]{:S(2)}) %collective-permute-start.2) | collective-permute-done | bytes 737312 | tf_op jit(solution)/shard_map/ppermute | solution.py:309
  62.9 14.4 %shard_map.127 = (f32[2,576,1280]{2,1,0:T(8,128)}, bf16[2,576,1280]{2,1,0:T(8,128)(2,1)}) custom-call(bf16[2,144,1280]{2,1,0:T(8,128)(2,1)} %get-tuple-element.64.x0, bf16[2,144,1280]{2,1,0:T(8,128)(2,1)} %collective-permute-done.x1, bf16[2,144,1280]{2,1,0:T(8,128)(2,1)} %collective-permute-done.1.x2.x0, bf16[2,144,1280]{2,1,0:T(8,128)(2,1)} %collective-permute-done.2.x3.x1, ...), custom_call_target="tpu_custom_call" | custom-call | flops 3774873600 | bytes 16777216 | tf_op jit(solution)/shard_map/pallas_call | solution.py:373
  77.6 0.7 collective-permute-start.6
  78.2 23.6 %shard_map.128 = (bf16[2,576,320]{2,1,0:T(8,128)(2,1)}, bf16[2,576,320]{2,1,0:T(8,128)(2,1)}) custom-call(bf16[2,576,1280]{2,1,0:T(8,128)(2,1)} %get-tuple-element.77.a_ref, bf16[2,960,1280]{2,1,0:T(8,128)(2,1)} %bitcast.132, bf16[2,960,1280]{2,1,0:T(8,128)(2,1)} %collective-permute-done.5.sib_ref), custom_call_target="tpu_custom_call" | custom-call | flops 12457082880 | bytes 16777216 | tf_op jit(solution)/shard_map/pallas_call | solution.py:381
  101.9 14.3 %collective-permute-done.6 = bf16[2,320,1280]{2,1,0:T(8,128)(2,1)} collective-permute-done((bf16[2,320,1280]{2,1,0:T(8,128)(2,1)}, bf16[2,320,1280]{2,1,0:T(8,128)(2,1)}, u32[]{:S(2)}, u32[]{:S(2)}) %collective-permute-start.6) | collective-permute-done | bytes 1638432 | tf_op jit(solution)/shard_map/ppermute | solution.py:309
  117.2 0.8 collective-permute-start.8
  118.1 22.4 %collective-permute-done.7.sib_ref = bf16[4,240,1280]{2,1,0:T(8,128)(2,1)} collective-permute-done((bf16[4,240,1280]{2,1,0:T(8,128)(2,1)}, bf16[4,240,1280]{2,1,0:T(8,128)(2,1)}, u32[]{:S(2)}, u32[]{:S(2)}) %collective-permute-start.7) | collective-permute-done | bytes 2457632 | tf_op jit(solution)/shard_map/ppermute | solution.py:309
  140.5 23.6 %shard_map.129 = (bf16[2,576,320]{2,1,0:T(8,128)(2,1)}, bf16[2,576,320]{2,1,0:T(8,128)(2,1)}) custom-call(bf16[2,576,1280]{2,1,0:T(8,128)(2,1)} %get-tuple-element.77.a_ref, bf16[4,240,1280]{2,1,0:T(8,128)(2,1)} %bitcast.146, bf16[4,240,1280]{2,1,0:T(8,128)(2,1)} %collective-permute-done.7.sib_ref), custom_call_target="tpu_custom_call" | custom-call | flops 12457082880 | bytes 16777216 | tf_op jit(solution)/shard_map/pallas_call | solution.py:381
  165.2 3.3 collective-permute-done.9.kv1
  168.6 7.8 %collective-permute-done.10.kv2 = bf16[2,2,80,640]{3,2,1,0:T(8,128)(2,1)S(1)} collective-permute-done((bf16[2,2,80,640]{3,2,1,0:T(8,128)(2,1)}, bf16[2,2,80,640]{3,2,1,0:T(8,128)(2,1)S(1)}, u32[]{:S(2)}, u32[]{:S(2)}) %collective-permute-start.10) | collective-permute-done | bytes 409632 | tf_op jit(solution)/shard_map/ppermute | solution.py:309
  176.4 11.5 %collective-permute-done.11.kv3 = bf16[2,2,80,640]{3,2,1,0:T(8,128)(2,1)S(1)} collective-permute-done((bf16[2,2,80,640]{3,2,1,0:T(8,128)(2,1)}, bf16[2,2,80,640]{3,2,1,0:T(8,128)(2,1)S(1)}, u32[]{:S(2)}, u32[]{:S(2)}) %collective-permute-start.11) | collective-permute-done | bytes 409632 | tf_op jit(solution)/shard_map/ppermute | solution.py:309
  188.0 0.7 copy-done.17
  188.7 1.2 copy-done.14
  189.9 1.6 slice_bitcast_fusion.3
  191.5 0.7 stack.9.vec_ref
  192.1 2.0 dynamic-slice_bitcast_fusion.7
  194.2 2.8 dynamic-slice_bitcast_fusion
  196.9 1.2 collective-permute-start.16
  198.2 0.9 collective-permute-start.20
  199.2 29.3 %shard_map.130 = (f32[2,576,1280]{2,1,0:T(8,128)}, bf16[2,576,1280]{2,1,0:T(8,128)(2,1)}) custom-call(f32[2,576,1280]{2,1,0:T(8,128)} %get-tuple-element.68.h_ref, bf16[2,576,320]{2,1,0:T(8,128)(2,1)} %get-tuple-element.74.o0, bf16[2,576,320]{2,1,0:T(8,128)(2,1)} %get-tuple-element.75.o1, ...), custom_call_target="tpu_custom_call", output_to_operand_aliasing={{0}: (0, {})} | custom-call | flops 15099494400 | bytes 16777216 | tf_op jit(solution)/shard_map/pallas_call | solution.py:396
  228.6 31.2 %shard_map.131.h_ref = f32[2,576,1280]{2,1,0:T(8,128)} custom-call(f32[2,576,1280]{2,1,0:T(8,128)} %get-tuple-element.84.h_ref, bf16[2,576,1280]{2,1,0:T(8,128)(2,1)} %get-tuple-element.93.a_ref, f32[2,2,1280]{2,1,0:T(2,128)} %rest_0_.3, f32[2,2,1280]{2,1,0:T(2,128)} %collective-permute-done.17.rest_1_.b1, ...), custom_call_target="tpu_custom_call", output_to_operand_aliasing={{}: (0, {})} | custom-call | flops 22649241600 | bytes 16777216 | tf_op jit(solution)/shard_map/pallas_call | solution.py:419
  260.5 1.0 collective-permute-start.21
  261.9 1.2 slice.164
  263.3 1.6 pad_maximum_fusion
  264.9 1.1 collective-permute-start.25
  265.9 0.6 pad_maximum_fusion.2.vec_ref
  266.6 19.1 %shard_map.132.h_ref = f32[2,576,1280]{2,1,0:T(8,128)} custom-call(f32[2,576,1280]{2,1,0:T(8,128)} %shard_map.131.h_ref, bf16[2,576,1280]{2,1,0:T(8,128)(2,1)} %get-tuple-element.93.a_ref, f32[2,2,1280]{2,1,0:T(2,128)} %collective-permute-done.21.rest_0_.b2, bf16[4,2,320,1280]{3,2,1,0:T(8,128)(2,1)} %bitcast.137, ...), custom_call_target="tpu_custom_call", output_to_operand_aliasing={{}: (0, {})} | custom-call | flops 11324620800 | bytes 16777216 | tf_op jit(solution)/shard_map/pallas_call | solution.py:419
  285.7 20.1 %shard_map.133 = (f32[2,576,1280]{2,1,0:T(8,128)}, bf16[2,576,1280]{2,1,0:T(8,128)(2,1)}) custom-call(f32[2,576,1280]{2,1,0:T(8,128)} %shard_map.132.h_ref, bf16[2,576,1280]{2,1,0:T(8,128)(2,1)} %get-tuple-element.93.a_ref, f32[2,2,1280]{2,1,0:T(2,128)} %collective-permute-done.22.b1_ref.b3, ...), custom_call_target="tpu_custom_call", output_to_operand_aliasing={{0}: (0, {})} | custom-call | flops 11324620800 | bytes 16777216 | tf_op jit(solution)/shard_map/pallas_call | solution.py:464
  306.2 24.0 %shard_map.134 = (bf16[2,576,320]{2,1,0:T(8,128)(2,1)}, bf16[2,576,320]{2,1,0:T(8,128)(2,1)}) custom-call(bf16[2,576,1280]{2,1,0:T(8,128)(2,1)} %get-tuple-element.107.a_ref, bf16[2,960,1280]{2,1,0:T(8,128)(2,1)} %bitcast.134, bf16[2,960,1280]{2,1,0:T(8,128)(2,1)} %collective-permute-done.5.sib_ref), custom_call_target="tpu_custom_call" | custom-call | flops 12457082880 | bytes 16777216 | tf_op jit(solution)/shard_map/pallas_call | solution.py:381
  330.5 3.8 slice.177
  334.3 0.6 collective-permute-start.28
  335.0 0.7 stack.11.vec_ref
  335.6 23.5 %shard_map.135 = (bf16[2,576,320]{2,1,0:T(8,128)(2,1)}, bf16[2,576,320]{2,1,0:T(8,128)(2,1)}) custom-call(bf16[2,576,1280]{2,1,0:T(8,128)(2,1)} %get-tuple-element.107.a_ref, bf16[4,240,1280]{2,1,0:T(8,128)(2,1)} %bitcast.148, bf16[4,240,1280]{2,1,0:T(8,128)(2,1)} %collective-permute-done.26.sib_ref), custom_call_target="tpu_custom_call" | custom-call | flops 12457082880 | bytes 16777216 | tf_op jit(solution)/shard_map/pallas_call | solution.py:381
  359.2 29.3 %shard_map.136 = (f32[2,576,1280]{2,1,0:T(8,128)}, bf16[2,576,1280]{2,1,0:T(8,128)(2,1)}) custom-call(f32[2,576,1280]{2,1,0:T(8,128)} %get-tuple-element.96.h_ref, bf16[2,576,320]{2,1,0:T(8,128)(2,1)} %get-tuple-element.105.o0, bf16[2,576,320]{2,1,0:T(8,128)(2,1)} %get-tuple-element.106.o1, ...), custom_call_target="tpu_custom_call", output_to_operand_aliasing={{0}: (0, {})} | custom-call | flops 15099494400 | bytes 16777216 | tf_op jit(solution)/shard_map/pallas_call | solution.py:396
  388.5 19.2 %collective-permute-done.28.rest_3_ = bf16[1,1280,1280]{2,1,0:T(8,128)(2,1)} collective-permute-done((bf16[1,1280,1280]{2,1,0:T(8,128)(2,1)}, bf16[1,1280,1280]{2,1,0:T(8,128)(2,1)}, u32[]{:S(2)}, u32[]{:S(2)}) %collective-permute-start.28) | collective-permute-done | bytes 3276832 | tf_op jit(solution)/shard_map/ppermute | solution.py:309
  408.3 18.3 %shard_map.137.h_ref = f32[2,576,1280]{2,1,0:T(8,128)} custom-call(f32[2,576,1280]{2,1,0:T(8,128)} %get-tuple-element.116.h_ref, bf16[2,576,1280]{2,1,0:T(8,128)(2,1)} %get-tuple-element.117.a_ref, f32[2,2,1280]{2,1,0:T(2,128)} %rest_0_.3, bf16[2,2,1280,1280]{3,2,1,0:T(8,128)(2,1)} %bitcast.109, ...), custom_call_target="tpu_custom_call", output_to_operand_aliasing={{}: (0, {})} | custom-call | flops 11324620800 | bytes 16777216 | tf_op jit(solution)/shard_map/pallas_call | solution.py:419
  426.6 29.2 %shard_map.138 = bf16[2,2,144,1280]{3,2,1,0:T(8,128)(2,1)} custom-call(f32[2,576,1280]{2,1,0:T(8,128)} %shard_map.137.h_ref, bf16[2,576,1280]{2,1,0:T(8,128)(2,1)} %get-tuple-element.117.a_ref, f32[2,2,1280]{2,1,0:T(2,128)} %collective-permute-done.17.rest_1_.b1, f32[2,2,1280]{2,1,0:T(2,128)} %collective-permute-done.21.rest_0_.b2, ...), custom_call_target="tpu_custom_call" | custom-call | flops 16986931200 | bytes 16777216 | tf_op jit(solution)/shard_map/pallas_call | solution.py:480
  455.9 2.6 slice_bitcast_fusion.1
  458.4 0.7 collective-permute-start.31
  459.2 0.6 collective-permute-start.32
  459.8 28.9 %shard_map.139 = bf16[2,2,144,1280]{3,2,1,0:T(8,128)(2,1)} custom-call(f32[2,576,1280]{2,1,0:T(8,128)} %shard_map.137.h_ref, bf16[2,576,1280]{2,1,0:T(8,128)(2,1)} %get-tuple-element.117.a_ref, f32[2,2,1280]{2,1,0:T(2,128)} %collective-permute-done.17.rest_1_.b1, f32[2,2,1280]{2,1,0:T(2,128)} %collective-permute-done.21.rest_0_.b2, ...), custom_call_target="tpu_custom_call" | custom-call | flops 16986931200 | bytes 16777216 | tf_op jit(solution)/shard_map/pallas_call | solution.py:480
  488.8 1.2 copy-done.2
  490.1 0.8 collective-permute-start.33
  491.0 1.2 bitcast_dynamic-update-slice_fusion.2
  492.1 1.2 bitcast_dynamic-update-slice_fusion.1
  493.4 1.6 copy-done
  (103 shorter events, 6.7 us)
Async XLA Ops:
  6.5 71.7 %all-gather.7.cloned.1.call-start = ((), (), s32[]{:S(2)}) async-start(), calls=%async_computation | async-start | bytes 3072000 | tf_op jit(solution)/shard_map/all_gather | solution.py:333
  8.5 17.4 %collective-permute-start.3 = (bf16[240,1280]{1,0:T(8,128)(2,1)}, bf16[240,1280]{1,0:T(8,128)(2,1)}, u32[]{:S(2)}, u32[]{:S(2)}) collective-permute-start(bf16[240,1280]{1,0:T(8,128)(2,1)} %dynamic-slice_bitcast_fusion.8), channel_id=1, source_target_pairs={{0,2},{1,3},{2,0},{3,1},{4,6},{5,7},{6,4},{7,5},{8,10},{9,11},{10,... | collective-permute-start | bytes 1843208 | tf_op jit(solution)/shard_map/ppermute | solution.py:309
  20.5 5.5 %copy-start.1 = (bf16[8,6,24,1280]{3,2,1,0:T(8,128)(2,1)S(1)}, bf16[8,6,24,1280]{3,2,1,0:T(8,128)(2,1)}, u32[]{:S(2)}) copy-start(bf16[8,6,24,1280]{3,2,1,0:T(8,128)(2,1)} %param.13) | copy-start | bytes 8847364
  25.9 138.2 %all-gather.9.cloned.1.call-start = ((), (), s32[]{:S(2)}) async-start(), calls=%async_computation.1 | async-start | bytes 3072000 | tf_op jit(solution)/shard_map/all_gather | solution.py:333
  25.9 52.3 %collective-permute-start.5 = (bf16[2,960,1280]{2,1,0:T(8,128)(2,1)}, bf16[2,960,1280]{2,1,0:T(8,128)(2,1)}, u32[]{:S(2)}, u32[]{:S(2)}) collective-permute-start(bf16[2,960,1280]{2,1,0:T(8,128)(2,1)} %bitcast.131), channel_id=1, source_target_pairs={{0,1},{1,0},{2,3},{3,2},{4,5},{5,4},{6,7},{7,6},{8,9},{9,8},{10,11... | collective-permute-start | bytes 14745608 | tf_op jit(solution)/shard_map/ppermute | solution.py:309
  27.7 26.0 %collective-permute-start = (bf16[2,144,1280]{2,1,0:T(8,128)(2,1)}, bf16[2,144,1280]{2,1,0:T(8,128)(2,1)}, u32[]{:S(2)}, u32[]{:S(2)}) collective-permute-start(bf16[2,144,1280]{2,1,0:T(8,128)(2,1)} %get-tuple-element.125), channel_id=1, source_target_pairs={{0,1},{1,0},{2,3},{3,2},{4,5},{5,4},{6,7},{7,6},{8,9},{9,8},{10,11... | collective-permute-start | bytes 2211848 | tf_op jit(solution)/shard_map/ppermute | solution.py:309
  28.2 25.6 %collective-permute-start.1 = (bf16[2,144,1280]{2,1,0:T(8,128)(2,1)}, bf16[2,144,1280]{2,1,0:T(8,128)(2,1)}, u32[]{:S(2)}, u32[]{:S(2)}) collective-permute-start(bf16[2,144,1280]{2,1,0:T(8,128)(2,1)} %get-tuple-element.124), channel_id=1, source_target_pairs={{0,2},{1,3},{2,0},{3,1},{4,6},{5,7},{6,4},{7,5},{8,10},{9,11},{10,... | collective-permute-start | bytes 2211848 | tf_op jit(solution)/shard_map/ppermute | solution.py:309
  29.9 33.0 %collective-permute-start.2 = (bf16[2,144,1280]{2,1,0:T(8,128)(2,1)}, bf16[2,144,1280]{2,1,0:T(8,128)(2,1)}, u32[]{:S(2)}, u32[]{:S(2)}) collective-permute-start(bf16[2,144,1280]{2,1,0:T(8,128)(2,1)} %get-tuple-element.123), channel_id=1, source_target_pairs={{0,3},{1,2},{2,1},{3,0},{4,7},{5,6},{6,5},{7,4},{8,11},{9,10},{10,... | collective-permute-start | bytes 2211848 | tf_op jit(solution)/shard_map/ppermute | solution.py:309
  33.7 43.6 %collective-permute-start.4 = (bf16[240,1280]{1,0:T(8,128)(2,1)}, bf16[240,1280]{1,0:T(8,128)(2,1)}, u32[]{:S(2)}, u32[]{:S(2)}) collective-permute-start(bf16[240,1280]{1,0:T(8,128)(2,1)} %pad_maximum_fusion.1), channel_id=1, source_target_pairs={{0,2},{1,3},{2,0},{3,1},{4,6},{5,7},{6,4},{7,5},{8,10},{9,11},{10,... | collective-permute-start | bytes 1843208 | tf_op jit(solution)/shard_map/ppermute | solution.py:309
  77.3 182.6 %all-gather.11.cloned.1.call-start = ((), (), s32[]{:S(2)}) async-start(), calls=%async_computation.2 | async-start | bytes 8192000 | tf_op jit(solution)/shard_map/all_gather | solution.py:333
  77.6 38.6 %collective-permute-start.6 = (bf16[2,320,1280]{2,1,0:T(8,128)(2,1)}, bf16[2,320,1280]{2,1,0:T(8,128)(2,1)}, u32[]{:S(2)}, u32[]{:S(2)}) collective-permute-start(bf16[2,320,1280]{2,1,0:T(8,128)(2,1)} %dynamic-slice_bitcast_fusion.1), channel_id=1, source_target_pairs={{0,2},{1,3},{2,0},{3,1},{4,6},{5,7},{6,4},{7,5},{8,10},{9,11},{10,... | collective-permute-start | bytes 4915208 | tf_op jit(solution)/shard_map/ppermute | solution.py:309
  116.2 143.8 %all-gather.13.cloned.1.call-start = ((), (), s32[]{:S(2)}) async-start(), calls=%async_computation.3 | async-start | bytes 4096000 | tf_op jit(solution)/shard_map/all_gather | solution.py:333
  116.7 111.9 %collective-permute-start.18 = (bf16[2,2,1280,1280]{3,2,1,0:T(8,128)(2,1)}, bf16[2,2,1280,1280]{3,2,1,0:T(8,128)(2,1)}, u32[]{:S(2)}, u32[]{:S(2)}) collective-permute-start(bf16[2,2,1280,1280]{3,2,1,0:T(8,128)(2,1)} %bitcast.106), channel_id=1, source_target_pairs={{0,1},{1,0},{2,3},{3,2},{4,5},{5,4},{6,7},{7,6},{8,9},{9,8},{10,11... | collective-permute-start | bytes 39321608 | tf_op jit(solution)/shard_map/ppermute | solution.py:309
  116.7 23.7 %collective-permute-start.7 = (bf16[4,240,1280]{2,1,0:T(8,128)(2,1)}, bf16[4,240,1280]{2,1,0:T(8,128)(2,1)}, u32[]{:S(2)}, u32[]{:S(2)}) collective-permute-start(bf16[4,240,1280]{2,1,0:T(8,128)(2,1)} %bitcast.145), channel_id=1, source_target_pairs={{0,1},{1,0},{2,3},{3,2},{4,5},{5,4},{6,7},{7,6},{8,9},{9,8},{10,11... | collective-permute-start | bytes 7372808 | tf_op jit(solution)/shard_map/ppermute | solution.py:309
  117.2 111.4 %collective-permute-start.19 = (bf16[2,1280,1280]{2,1,0:T(8,128)(2,1)}, bf16[2,1280,1280]{2,1,0:T(8,128)(2,1)}, u32[]{:S(2)}, u32[]{:S(2)}) collective-permute-start(bf16[2,1280,1280]{2,1,0:T(8,128)(2,1)} %rest_2_.1), channel_id=1, source_target_pairs={{0,1},{1,0},{2,3},{3,2},{4,5},{5,4},{6,7},{7,6},{8,9},{9,8},{10,11... | collective-permute-start | bytes 19660808 | tf_op jit(solution)/shard_map/ppermute | solution.py:309
  117.2 46.8 %collective-permute-start.8 = (bf16[320,1280]{1,0:T(8,128)(2,1)}, bf16[320,1280]{1,0:T(8,128)(2,1)}, u32[]{:S(2)}, u32[]{:S(2)}) collective-permute-start(bf16[320,1280]{1,0:T(8,128)(2,1)} %dynamic-slice_bitcast_fusion.2), channel_id=1, source_target_pairs={{0,2},{1,3},{2,0},{3,1},{4,6},{5,7},{6,4},{7,5},{8,10},{9,11},{10,... | collective-permute-start | bytes 2457608 | tf_op jit(solution)/shard_map/ppermute | solution.py:309
  164.1 141.7 %all-gather.15.cloned.1.call-start = ((), (), s32[]{:S(2)}) async-start(), calls=%async_computation.4 | async-start | bytes 3072000 | tf_op jit(solution)/shard_map/all_gather | solution.py:333
  164.1 23.8 %collective-permute-start.12 = (bf16[2,320,1280]{2,1,0:T(8,128)(2,1)}, bf16[2,320,1280]{2,1,0:T(8,128)(2,1)S(1)}, u32[]{:S(2)}, u32[]{:S(2)}) collective-permute-start(bf16[2,320,1280]{2,1,0:T(8,128)(2,1)} %bitcast.116), channel_id=1, source_target_pairs={{0,1},{1,0},{2,3},{3,2},{4,5},{5,4},{6,7},{7,6},{8,9},{9,8},{10,11... | collective-permute-start | bytes 4915208 | tf_op jit(solution)/shard_map/ppermute | solution.py:309
  164.3 4.2 collective-permute-start.9
  164.7 11.7 %collective-permute-start.10 = (bf16[2,2,80,640]{3,2,1,0:T(8,128)(2,1)}, bf16[2,2,80,640]{3,2,1,0:T(8,128)(2,1)S(1)}, u32[]{:S(2)}, u32[]{:S(2)}) collective-permute-start(bf16[2,2,80,640]{3,2,1,0:T(8,128)(2,1)} %get-tuple-element.129), channel_id=1, source_target_pairs={{0,2},{1,3},{2,0},{3,1},{4,6},{5,7},{6,4},{7,5},{8,10},{9,11},{10,... | collective-permute-start | bytes 1228808 | tf_op jit(solution)/shard_map/ppermute | solution.py:309
  168.5 19.5 %copy-start.15 = (bf16[2,2,80,640]{3,2,1,0:T(8,128)(2,1)}, bf16[2,2,80,640]{3,2,1,0:T(8,128)(2,1)S(1)}, u32[]{:S(2)}) copy-start(bf16[2,2,80,640]{3,2,1,0:T(8,128)(2,1)S(1)} %collective-permute-done.9.kv1) | copy-start | bytes 1228804
  168.5 29.8 %collective-permute-start.15 = (bf16[4,240,1280]{2,1,0:T(8,128)(2,1)}, bf16[4,240,1280]{2,1,0:T(8,128)(2,1)}, u32[]{:S(2)}, u32[]{:S(2)}) collective-permute-start(bf16[4,240,1280]{2,1,0:T(8,128)(2,1)} %bitcast.143), channel_id=1, source_target_pairs={{0,1},{1,0},{2,3},{3,2},{4,5},{5,4},{6,7},{7,6},{8,9},{9,8},{10,11... | collective-permute-start | bytes 7372808 | tf_op jit(solution)/shard_map/ppermute | solution.py:309
  176.4 11.6 %copy-start.16 = (bf16[2,2,80,640]{3,2,1,0:T(8,128)(2,1)}, bf16[2,2,80,640]{3,2,1,0:T(8,128)(2,1)S(1)}, u32[]{:S(2)}) copy-start(bf16[2,2,80,640]{3,2,1,0:T(8,128)(2,1)S(1)} %collective-permute-done.10.kv2) | copy-start | bytes 1228804
  176.4 11.5 %collective-permute-start.11 = (bf16[2,2,80,640]{3,2,1,0:T(8,128)(2,1)}, bf16[2,2,80,640]{3,2,1,0:T(8,128)(2,1)S(1)}, u32[]{:S(2)}, u32[]{:S(2)}) collective-permute-start(bf16[2,2,80,640]{3,2,1,0:T(8,128)(2,1)} %get-tuple-element.127), channel_id=1, source_target_pairs={{0,3},{1,2},{2,1},{3,0},{4,7},{5,6},{6,5},{7,4},{8,11},{9,10},{10,... | collective-permute-start | bytes 1228808 | tf_op jit(solution)/shard_map/ppermute | solution.py:309
  187.9 0.8 copy-start.17
  187.9 9.0 %collective-permute-start.13 = (bf16[2,320,1280]{2,1,0:T(8,128)(2,1)}, bf16[2,320,1280]{2,1,0:T(8,128)(2,1)}, u32[]{:S(2)}, u32[]{:S(2)}) collective-permute-start(bf16[2,320,1280]{2,1,0:T(8,128)(2,1)} %bitcast.121), channel_id=1, source_target_pairs={{0,1},{1,0},{2,3},{3,2},{4,5},{5,4},{6,7},{7,6},{8,9},{9,8},{10,11... | collective-permute-start | bytes 4915208 | tf_op jit(solution)/shard_map/ppermute | solution.py:309
  188.7 1.2 copy-start.14
  189.9 8.2 %collective-permute-start.14 = (bf16[2,320,1280]{2,1,0:T(8,128)(2,1)}, bf16[2,320,1280]{2,1,0:T(8,128)(2,1)}, u32[]{:S(2)}, u32[]{:S(2)}) collective-permute-start(bf16[2,320,1280]{2,1,0:T(8,128)(2,1)} %bitcast.126), channel_id=1, source_target_pairs={{0,1},{1,0},{2,3},{3,2},{4,5},{5,4},{6,7},{7,6},{8,9},{9,8},{10,11... | collective-permute-start | bytes 4915208 | tf_op jit(solution)/shard_map/ppermute | solution.py:309
  196.9 31.5 %collective-permute-start.16 = (bf16[240,1280]{1,0:T(8,128)(2,1)}, bf16[240,1280]{1,0:T(8,128)(2,1)}, u32[]{:S(2)}, u32[]{:S(2)}) collective-permute-start(bf16[240,1280]{1,0:T(8,128)(2,1)} %dynamic-slice_bitcast_fusion.7), channel_id=1, source_target_pairs={{0,2},{1,3},{2,0},{3,1},{4,6},{5,7},{6,4},{7,5},{8,10},{9,11},{10,... | collective-permute-start | bytes 1843208 | tf_op jit(solution)/shard_map/ppermute | solution.py:309
  198.1 30.4 %collective-permute-start.17 = (f32[2,2,1280]{2,1,0:T(2,128)}, f32[2,2,1280]{2,1,0:T(2,128)}, u32[]{:S(2)}, u32[]{:S(2)}) collective-permute-start(f32[2,2,1280]{2,1,0:T(2,128)} %rest_0_.3), channel_id=1, source_target_pairs={{0,1},{1,0},{2,3},{3,2},{4,5},{5,4},{6,7},{7,6},{8,9},{9,8},{10,11... | collective-permute-start | bytes 61448 | tf_op jit(solution)/shard_map/ppermute | solution.py:309
  198.2 61.6 %collective-permute-start.20 = (bf16[2,320,1280]{2,1,0:T(8,128)(2,1)}, bf16[2,320,1280]{2,1,0:T(8,128)(2,1)}, u32[]{:S(2)}, u32[]{:S(2)}) collective-permute-start(bf16[2,320,1280]{2,1,0:T(8,128)(2,1)} %dynamic-slice_bitcast_fusion), channel_id=1, source_target_pairs={{0,2},{1,3},{2,0},{3,1},{4,6},{5,7},{6,4},{7,5},{8,10},{9,11},{10,... | collective-permute-start | bytes 4915208 | tf_op jit(solution)/shard_map/ppermute | solution.py:309
  228.5 179.3 %all-gather.17.cloned.1.call-start = ((), (), s32[]{:S(2)}) async-start(), calls=%async_computation.5 | async-start | bytes 8192000 | tf_op jit(solution)/shard_map/all_gather | solution.py:333
  259.8 3.3 copy-start.4
  259.8 3.4 copy-start.3
  259.9 25.8 %collective-permute-start.23 = (bf16[4,2,320,1280]{3,2,1,0:T(8,128)(2,1)}, bf16[4,2,320,1280]{3,2,1,0:T(8,128)(2,1)}, u32[]{:S(2)}, u32[]{:S(2)}) collective-permute-start(bf16[4,2,320,1280]{3,2,1,0:T(8,128)(2,1)} %bitcast.136), channel_id=1, source_target_pairs={{0,1},{1,0},{2,3},{3,2},{4,5},{5,4},{6,7},{7,6},{8,9},{9,8},{10,11... | collective-permute-start | bytes 19660808 | tf_op jit(solution)/shard_map/ppermute | solution.py:309
  260.0 25.7 %collective-permute-start.24 = (bf16[1,1280,1280]{2,1,0:T(8,128)(2,1)}, bf16[1,1280,1280]{2,1,0:T(8,128)(2,1)}, u32[]{:S(2)}, u32[]{:S(2)}) collective-permute-start(bf16[1,1280,1280]{2,1,0:T(8,128)(2,1)} %bitcast.141), channel_id=1, source_target_pairs={{0,1},{1,0},{2,3},{3,2},{4,5},{5,4},{6,7},{7,6},{8,9},{9,8},{10,11... | collective-permute-start | bytes 9830408 | tf_op jit(solution)/shard_map/ppermute | solution.py:309
  260.5 6.0 %collective-permute-start.21 = (f32[2,2,1280]{2,1,0:T(2,128)}, f32[2,2,1280]{2,1,0:T(2,128)}, u32[]{:S(2)}, u32[]{:S(2)}) collective-permute-start(f32[2,2,1280]{2,1,0:T(2,128)} %rest_0_.3), channel_id=1, source_target_pairs={{0,2},{1,3},{2,0},{3,1},{4,6},{5,7},{6,4},{7,5},{8,10},{9,11},{10,... | collective-permute-start | bytes 61448 | tf_op jit(solution)/shard_map/ppermute | solution.py:309
  261.5 24.2 %collective-permute-start.22 = (f32[2,2,1280]{2,1,0:T(2,128)}, f32[2,2,1280]{2,1,0:T(2,128)}, u32[]{:S(2)}, u32[]{:S(2)}) collective-permute-start(f32[2,2,1280]{2,1,0:T(2,128)} %rest_0_.3), channel_id=1, source_target_pairs={{0,3},{1,2},{2,1},{3,0},{4,7},{5,6},{6,5},{7,4},{8,11},{9,10},{10,... | collective-permute-start | bytes 61448 | tf_op jit(solution)/shard_map/ppermute | solution.py:309
  263.3 2.7 copy-start.11
  263.3 2.7 copy-start.12
  263.3 2.6 copy-start.13
  264.9 65.4 %collective-permute-start.25 = (bf16[4,240,1280]{2,1,0:T(8,128)(2,1)}, bf16[4,240,1280]{2,1,0:T(8,128)(2,1)}, u32[]{:S(2)}, u32[]{:S(2)}) collective-permute-start(bf16[4,240,1280]{2,1,0:T(8,128)(2,1)} %pad_maximum_fusion), channel_id=1, source_target_pairs={{0,2},{1,3},{2,0},{3,1},{4,6},{5,7},{6,4},{7,5},{8,10},{9,11},{10,... | collective-permute-start | bytes 7372808 | tf_op jit(solution)/shard_map/ppermute | solution.py:309
  305.8 29.8 %collective-permute-start.26 = (bf16[4,240,1280]{2,1,0:T(8,128)(2,1)}, bf16[4,240,1280]{2,1,0:T(8,128)(2,1)}, u32[]{:S(2)}, u32[]{:S(2)}) collective-permute-start(bf16[4,240,1280]{2,1,0:T(8,128)(2,1)} %bitcast.147), channel_id=1, source_target_pairs={{0,1},{1,0},{2,3},{3,2},{4,5},{5,4},{6,7},{7,6},{8,9},{9,8},{10,11... | collective-permute-start | bytes 7372808 | tf_op jit(solution)/shard_map/ppermute | solution.py:309
  330.2 4.7 copy-start.5
  330.2 4.7 copy-start.6
  330.2 4.7 copy-start.7
  330.3 4.7 copy-start.8
  330.3 4.7 copy-start.9
  330.3 4.7 copy-start.10
  330.3 28.9 %collective-permute-start.27 = (bf16[4,240,1280]{2,1,0:T(8,128)(2,1)}, bf16[4,240,1280]{2,1,0:T(8,128)(2,1)}, u32[]{:S(2)}, u32[]{:S(2)}) collective-permute-start(bf16[4,240,1280]{2,1,0:T(8,128)(2,1)} %collective-permute-done.25.rest), channel_id=1, source_target_pairs={{0,1},{1,0},{2,3},{3,2},{4,5},{5,4},{6,7},{7,6},{8,9},{9,8},{10,11... | collective-permute-start | bytes 7372808 | tf_op jit(solution)/shard_map/ppermute | solution.py:309
  334.3 73.5 %collective-permute-start.28 = (bf16[1,1280,1280]{2,1,0:T(8,128)(2,1)}, bf16[1,1280,1280]{2,1,0:T(8,128)(2,1)}, u32[]{:S(2)}, u32[]{:S(2)}) collective-permute-start(bf16[1,1280,1280]{2,1,0:T(8,128)(2,1)} %slice.177), channel_id=1, source_target_pairs={{0,2},{1,3},{2,0},{3,1},{4,6},{5,7},{6,4},{7,5},{8,10},{9,11},{10,... | collective-permute-start | bytes 9830408 | tf_op jit(solution)/shard_map/ppermute | solution.py:309
  407.8 18.8 %collective-permute-start.29 = (bf16[4,2,320,1280]{3,2,1,0:T(8,128)(2,1)}, bf16[4,2,320,1280]{3,2,1,0:T(8,128)(2,1)}, u32[]{:S(2)}, u32[]{:S(2)}) collective-permute-start(bf16[4,2,320,1280]{3,2,1,0:T(8,128)(2,1)} %bitcast.138), channel_id=1, source_target_pairs={{0,1},{1,0},{2,3},{3,2},{4,5},{5,4},{6,7},{7,6},{8,9},{9,8},{10,11... | collective-permute-start | bytes 19660808 | tf_op jit(solution)/shard_map/ppermute | solution.py:309
  407.8 18.8 %collective-permute-start.30 = (bf16[1,1280,1280]{2,1,0:T(8,128)(2,1)}, bf16[1,1280,1280]{2,1,0:T(8,128)(2,1)}, u32[]{:S(2)}, u32[]{:S(2)}) collective-permute-start(bf16[1,1280,1280]{2,1,0:T(8,128)(2,1)} %collective-permute-done.28.rest_3_), channel_id=1, source_target_pairs={{0,1},{1,0},{2,3},{3,2},{4,5},{5,4},{6,7},{7,6},{8,9},{9,8},{10,11... | collective-permute-start | bytes 9830408 | tf_op jit(solution)/shard_map/ppermute | solution.py:309
  458.4 32.5 %collective-permute-start.31 = (bf16[2,144,1280]{2,1,0:T(8,128)(2,1)}, bf16[2,144,1280]{2,1,0:T(8,128)(2,1)}, u32[]{:S(2)}, u32[]{:S(2)}) collective-permute-start(bf16[2,144,1280]{2,1,0:T(8,128)(2,1)} %get-tuple-element.134), channel_id=1, source_target_pairs={{0,2},{1,3},{2,0},{3,1},{4,6},{5,7},{6,4},{7,5},{8,10},{9,11},{10,... | collective-permute-start | bytes 2211848 | tf_op jit(solution)/shard_map/ppermute | solution.py:309
  459.2 33.0 %collective-permute-start.32 = (bf16[2,144,1280]{2,1,0:T(8,128)(2,1)}, bf16[2,144,1280]{2,1,0:T(8,128)(2,1)}, u32[]{:S(2)}, u32[]{:S(2)}) collective-permute-start(bf16[2,144,1280]{2,1,0:T(8,128)(2,1)} %get-tuple-element.133), channel_id=1, source_target_pairs={{0,3},{1,2},{2,1},{3,0},{4,7},{5,6},{6,5},{7,4},{8,11},{9,10},{10,... | collective-permute-start | bytes 2211848 | tf_op jit(solution)/shard_map/ppermute | solution.py:309
  488.6 1.4 copy-start.2
  490.1 3.2 collective-permute-start.33
  493.4 1.6 copy-start
Sparse Core Ops, SparseCore 0:
  26.0 35.7 all-gather.6
  77.4 35.9 all-gather.8
  116.3 68.8 all-gather.10
  186.9 41.1 all-gather.12
  229.7 34.4 all-gather.14
  265.8 68.4 all-gather.16

commit v4 on v3

--- a/solution.py
+++ b/solution.py
@@ -258,7 +258,7 @@
     ff_steps(layer, a_ref, (b1_ref,), ((w1_ref, w2_ref),), w1, w2, m_scr, sems, finish)
 
 
-def ff_end_kernel(layer, h_ref, a_ref, b1, b2, b3, vec_ref, io_ref, x0, x1, wp_ref, *rest):
+def ff_end_kernel(layer, h_ref, a_ref, b2, b3, vec_ref, io_ref, x0, x1, wp_ref, *rest):
     refs, (y_ref, w1, w2, m_scr, wp, wp_sem, sems) = rest[:-7], rest[-7:]
     shards = [refs[i:i + 2] for i in range(0, len(refs), 2)]
     tok = x0.shape[1]
@@ -274,7 +274,7 @@
         for i, ref in enumerate((x0, x1)):
             y_ref[i, 0] = (y[i * tok:(i + 1) * tok] + ref[0].astype(F32)).astype(BF16)
 
-    ff_steps(layer, a_ref, (b1, b2, b3), shards, w1, w2, m_scr, sems, finish)
+    ff_steps(layer, a_ref, (b2, b3), shards, w1, w2, m_scr, sems, finish)
 
 
 def rows_spec(shape):
@@ -357,10 +357,12 @@
         kv_out[0], piece = tie(kv_out[0], far_qkv)
         full_qkv = gather(piece)
         kv_parts = [kv_out[0]] + [swap(kv_out[m], m) for m in (1, 2, 3)]
-        ff_src = [piece_of(ff1_t, 0, 2)[0], piece_of(w_ff2, 0, 1)[0]]
+        ff_src = [piece_of(ff1_t, 0, 2)[0], w_ff2[:1]]
+        qkv_src = piece_of(qkv_t, 1, 1)[0]
+        next_qkv = swap(qkv_src, 2)
         far_ff, far_second = swap(ff_src[0], 2), swap(ff_src[1], 2)
         sib_ff1, sib_ff2 = swap(ff1_t, 1), swap(w_ff2, 1)
-        x_parts = list(tie(*x_parts, *ff_src, *kv_out))[:tp_size]
+        x_parts = list(tie(*x_parts, *ff_src, qkv_src, *kv_out))[:tp_size]
 
         grid = (mine,)
         total = mine * n_tok
@@ -434,32 +436,33 @@
                 act, piece = tie(act, far_ff)
                 full_ff = gather(piece)
             else:
-                m0, rest = tie(m0, next_rest)
+                act, m0, rest, piece = tie(act, m0, full_rest, far_ff1)
+                next_ff = gather(piece)
+                rest = rest.reshape(dp_size, -1, channels)
                 rest_sib = swap(rest, 1)
             m2, m3 = self_attn(act, rem, rem_sib, layer)
             if layer == 0:
-                act, m3, piece, rest = tie(act, m3, far_second, full_rest)
-                full_second = gather(piece)
+                act, m3, rest = tie(act, m3, full_rest)
                 rest = rest.reshape(dp_size, -1, channels)
                 rest_sib = swap(rest, 1)
-                act, src_a, src_b, src_c, *src = tie(act, qkv_t, ff1_t, w_ff2, o1_t, q2_t, o2_t)
-                far_qkv = swap(piece_of(src_a, 1, 1)[0], 2)
+                act, src_b, src_c, *src = tie(act, ff1_t, w_ff2, o1_t, q2_t, o2_t)
+                next_rest = swap(jnp.concatenate([piece_of(w, 1, 1)[0] for w in src]), 2)
                 far_ff1 = swap(piece_of(src_b, 1, 2)[0], 2)
-                next_rest = swap(jnp.concatenate([w[1].reshape(dp_size, -1, channels) for w in src], axis=1), 2)
                 next_ff2 = swap(src_c[1:], 2)
             hidden, act = middle(hidden, [m0, m1, m2, m3], jnp.stack([vecs[i] for i in (6, 2, 3, 7, 4, 5)]),
                                  layer, 0, rest, rest_sib)
             if layer == 0:
-                act, piece = tie(act, far_qkv)
+                act, piece = tie(act, next_qkv)
                 full_qkv = gather(piece)
                 hidden = feed_forward(hidden, act, layer, (0, (ff1_t, w_ff2)), (1, (sib_ff1, sib_ff2)))
-                hidden, act, full, piece = tie(hidden, act, full_ff, far_ff1)
-                next_ff = gather(piece)
+                hidden, act, full = tie(hidden, act, full_ff)
                 rem = full.reshape(dp_size, 2, ff // dp_size, channels)
                 rem_sib = swap(rem, 1)
-                hidden, second = tie(hidden, full_second[None])
+                hidden, second = tie(hidden, far_second)
                 second_sib = swap(second, 1)
                 hidden = feed_forward(hidden, act, layer, (2, (rem, second)))
+                hidden, piece = tie(hidden, next_rest)
+                full_rest = gather(piece)
                 after = block_vecs[layer + 1]
                 hidden, act = call(
                     functools.partial(ff_last_kernel, layer), tiles,
@@ -468,24 +471,24 @@
                     ff_scratch(1), {0: 0},
                 )(hidden, act, bias[3], jnp.stack([vecs[8], after[0], after[1]]), rem_sib, second_sib)
 
+        hidden = feed_forward(hidden, act, layers - 1, (0, (ff1_t, w_ff2)))
         hidden, act, full, next_ff2 = tie(hidden, act, next_ff, next_ff2)
-        next_ff2_sib = swap(next_ff2, 1)
         rem = full.reshape(dp_size, 2, ff // dp_size, channels)
-        ff_weights = [sib_ff1, sib_ff2, rem, next_ff2, swap(rem, 1), next_ff2_sib]
-        hidden = feed_forward(hidden, act, layers - 1, (0, (ff1_t, w_ff2)))
+        ff_weights = [rem, next_ff2, swap(rem, 1), swap(next_ff2, 1)]
+        hidden = feed_forward(hidden, act, layers - 1, (1, (sib_ff1, sib_ff2)))
         parts = [None] * tp_size
         split = tp_size // 2
         for half in (1, 0):
             row_spec = pl.BlockSpec((1, tile, channels), lambda i, half=half: (i, half, 0))
             pair = call(
                 functools.partial(ff_end_kernel, layers - 1), grid,
-                [row_spec, row_spec] + [b_spec[layers - 1]] * 3 + [vec_spec(1, channels), vec_spec(4, channels)]
-                + [x_spec] * 2 + [any_spec] * 7,
+                [row_spec, row_spec] + [b_spec[layers - 1]] * 2 + [vec_spec(1, channels), vec_spec(4, channels)]
+                + [x_spec] * 2 + [any_spec] * 5,
                 pl.BlockSpec((split, 1, tok, channels), lambda i: (0, i, 0, 0)),
-                jax.ShapeDtypeStruct((split, mine, tok, channels), BF16), 3 * ff_flops // 2,
-                ff_scratch(3, pltpu.VMEM((channels, channels), BF16), pltpu.SemaphoreType.DMA((1,))),
+                jax.ShapeDtypeStruct((split, mine, tok, channels), BF16), 2 * ff_flops // 2,
+                ff_scratch(2, pltpu.VMEM((channels, channels), BF16), pltpu.SemaphoreType.DMA((1,))),
                 None,
-            )(hidden, act, *bias[1:], vecs[8:9], io_vecs, *x_parts[half * split:(half + 1) * split], w_proj, *ff_weights)
+            )(hidden, act, *bias[2:], vecs[8:9], io_vecs, *x_parts[half * split:(half + 1) * split], w_proj, *ff_weights)
             for i in range(split):
                 m = half * split + i
                 parts[m] = swap(pair[i], m) if m else pair[i]

time: 510 us -> 509 us (level)
  waiting for transfers between devices: 90.5 us -> 80.1 us
  starting transfers between devices: 20.1 us -> 25.3 us
    pallas_call x3 -> x4, Pallas kernels: 68.6 us -> 86.4 us  [feed_forward(): call(functools.partial(ff_kernel, layer, kinds), tiles, [t_spec, t_spec]...]
    pallas_call x2, Pallas kernels: 58.1 us -> 42.6 us  [body(): call(functools.partial(ff_end_kernel, layers - 1), grid, [row_spec, row_s...]
    ppermute x34, waiting for transfers between devices: 90.3 us -> 79.9 us  [swap(): return lax.ppermute(value, 'tp', [(i, i ^ mask) for i in range(tp_size)])]
    ppermute x34, starting transfers between devices: 19.3 us -> 24.7 us  [swap(): return lax.ppermute(value, 'tp', [(i, i ^ mask) for i in range(tp_size)])]
    unnamed x38 -> x30, local copies, waits for them, and re-layouts: 17.8 us -> 17.7 us
  transfers between devices with their start and end apart: 40 -> 40, of which waited for: 8 -> 10; matrix products, arithmetic and copies ran while one was open for 11% -> 11% of each run, Pallas kernels for 57% -> 59%
where the time goes in v4:
time: 509 us; the launch traced here: 501 us
  Pallas kernels  319 us (63%)
  waiting for transfers between devices  80.1 us (16%)
  local copies, waits for them, and re-layouts  54.3 us (11%)
  starting transfers between devices  25.3 us (5%)
  between operations  14.4 us (3%)
  matrix products  5.7 us (1%)
    pallas_call x4, Pallas kernels, self_attn(): call(functools.partial(self_kernel, layer), grid, [a_spec] + [pl.BlockSpe...  95.6 us
    pallas_call x4, Pallas kernels, feed_forward(): call(functools.partial(ff_kernel, layer, kinds), tiles, [t_spec, t_spec]...  86.4 us
    ppermute x34, waiting for transfers between devices, swap(): return lax.ppermute(value, 'tp', [(i, i ^ mask) for i in range(tp_size)])  79.9 us
    pallas_call x2, Pallas kernels, middle(): call(functools.partial(mid_kernel, ctx_len, layer, slot), grid, [a_spec]...  59.7 us
    pallas_call x2, Pallas kernels, body(): call(functools.partial(ff_end_kernel, layers - 1), grid, [row_spec, row_s...  42.6 us
    ppermute x34, starting transfers between devices, swap(): return lax.ppermute(value, 'tp', [(i, i ^ mask) for i in range(tp_size)])  24.7 us
    pallas_call x1, Pallas kernels, body(): call(functools.partial(ff_last_kernel, layer), tiles, [t_spec, t_spec, b_...  20.3 us
    unnamed x30, local copies, waits for them, and re-layouts  17.7 us
  transfers between devices with their start and end apart: 40, of which 10 were waited for; matrix products, arithmetic and copies ran while one was open for 11% of the time, Pallas kernels for 59%

profile of v4, /device:TPU:0, one launch (start us, length us, event | category | flops | bytes accessed | tf_op | source)
XLA Modules:
  0.0 501.1 jit_solution(16352221727637650912)
XLA Ops:
  6.5 2.4 dynamic-slice_bitcast_fusion.6
  8.9 3.2 collective-permute-start.3
  12.1 5.7 %convert_bitcast_fusion = bf16[2,8,77,2,5,64]{2,5,1,4,3,0:T(8,128)(2,1)S(1)} fusion(bf16[2,1024,2,5,64]{1,4,3,2,0:T(8,128)(2,1)} %param.21, bf16[8,77,1024,1,1,1]{2,0,1,5,4,3:T(8,128)(2,1)} %bitcast.142), kind=kOutput, calls=%fused_computation.2 | convolution fusion | flops 1615595520 | bytes 5459968 | tf_op jit(solution)/shard_map/blc,rcjhd->rbljhd/dot_general | solution.py:353
  18.4 2.5 copy.35
  20.9 2.6 pad_dynamic-slice_fusion
  23.5 2.6 collective-permute-done.3
  26.2 0.8 copy-done.3
  27.1 12.7 %copy.49 = bf16[2,1280,2,1280]{3,1,2,0:T(8,128)(2,1)} copy(bf16[2,1280,2,1280]{3,2,1,0:T(2,128)(2,1)} %param.23) | data formatting | bytes 26214400 | tf_op args[10]
  40.2 1.7 dynamic-slice_bitcast_fusion.2
  42.0 1.7 collective-permute-start.1
  43.8 0.9 dynamic-slice_bitcast_fusion.11
  44.7 3.9 slice.137
  48.6 0.7 slice.138
  49.9 0.9 dynamic-slice_bitcast_fusion.12
  50.8 1.0 dynamic-slice_bitcast_fusion.13
  51.8 0.8 pad_maximum_fusion
  52.6 8.5 %collective-permute-done.x1 = bf16[2,144,1280]{2,1,0:T(8,128)(2,1)} collective-permute-done((bf16[2,144,1280]{2,1,0:T(8,128)(2,1)}, bf16[2,144,1280]{2,1,0:T(8,128)(2,1)}, u32[]{:S(2)}, u32[]{:S(2)}) %collective-permute-start) | collective-permute-done | bytes 737312 | tf_op jit(solution)/shard_map/ppermute | solution.py:309
  61.1 1.7 collective-permute-start.4
  62.9 2.7 dynamic-slice_bitcast_fusion.1
  65.6 11.2 %collective-permute-done.2.x3.x1 = bf16[2,144,1280]{2,1,0:T(8,128)(2,1)} collective-permute-done((bf16[2,144,1280]{2,1,0:T(8,128)(2,1)}, bf16[2,144,1280]{2,1,0:T(8,128)(2,1)}, u32[]{:S(2)}, u32[]{:S(2)}) %collective-permute-start.2) | collective-permute-done | bytes 737312 | tf_op jit(solution)/shard_map/ppermute | solution.py:309
  76.7 14.4 %shard_map.127 = (f32[2,576,1280]{2,1,0:T(8,128)}, bf16[2,576,1280]{2,1,0:T(8,128)(2,1)}) custom-call(bf16[2,144,1280]{2,1,0:T(8,128)(2,1)} %get-tuple-element.65.x0, bf16[2,144,1280]{2,1,0:T(8,128)(2,1)} %collective-permute-done.x1, bf16[2,144,1280]{2,1,0:T(8,128)(2,1)} %collective-permute-done.1.x2.x0, bf16[2,144,1280]{2,1,0:T(8,128)(2,1)} %collective-permute-done.2.x3.x1, ...), custom_call_target="tpu_custom_call" | custom-call | flops 3774873600 | bytes 16777216 | tf_op jit(solution)/shard_map/pallas_call | solution.py:375
  91.4 1.2 collective-permute-start.6
  92.6 23.6 %shard_map.128 = (bf16[2,576,320]{2,1,0:T(8,128)(2,1)}, bf16[2,576,320]{2,1,0:T(8,128)(2,1)}) custom-call(bf16[2,576,1280]{2,1,0:T(8,128)(2,1)} %get-tuple-element.78.a_ref, bf16[2,960,1280]{2,1,0:T(8,128)(2,1)} %bitcast.111, bf16[2,960,1280]{2,1,0:T(8,128)(2,1)} %collective-permute-done.5.sib_ref), custom_call_target="tpu_custom_call" | custom-call | flops 12457082880 | bytes 16777216 | tf_op jit(solution)/shard_map/pallas_call | solution.py:383
  116.2 13.8 %collective-permute-done.6 = bf16[2,320,1280]{2,1,0:T(8,128)(2,1)} collective-permute-done((bf16[2,320,1280]{2,1,0:T(8,128)(2,1)}, bf16[2,320,1280]{2,1,0:T(8,128)(2,1)}, u32[]{:S(2)}, u32[]{:S(2)}) %collective-permute-start.6) | collective-permute-done | bytes 1638432 | tf_op jit(solution)/shard_map/ppermute | solution.py:309
  130.8 1.2 collective-permute-start.10
  132.4 2.9 collective-permute-done.7.sib_ref
  135.5 24.1 %shard_map.129 = (bf16[2,576,320]{2,1,0:T(8,128)(2,1)}, bf16[2,576,320]{2,1,0:T(8,128)(2,1)}) custom-call(bf16[2,576,1280]{2,1,0:T(8,128)(2,1)} %get-tuple-element.78.a_ref, bf16[4,240,1280]{2,1,0:T(8,128)(2,1)} %bitcast.135, bf16[4,240,1280]{2,1,0:T(8,128)(2,1)} %collective-permute-done.7.sib_ref), custom_call_target="tpu_custom_call" | custom-call | flops 12457082880 | bytes 16777216 | tf_op jit(solution)/shard_map/pallas_call | solution.py:383
  160.0 1.5 collective-permute-start.9
  161.5 10.2 %collective-permute-done.9.kv2 = bf16[2,2,80,640]{3,2,1,0:T(8,128)(2,1)S(1)} collective-permute-done((bf16[2,2,80,640]{3,2,1,0:T(8,128)(2,1)}, bf16[2,2,80,640]{3,2,1,0:T(8,128)(2,1)S(1)}, u32[]{:S(2)}, u32[]{:S(2)}) %collective-permute-start.9) | collective-permute-done | bytes 409632 | tf_op jit(solution)/shard_map/ppermute | solution.py:309
  171.7 0.8 copy-done.13
  172.5 1.6 slice_bitcast_fusion.3
  174.7 0.9 collective-permute-done.12.q2_sib
  175.6 1.5 collective-permute-start.15
  177.1 0.8 collective-permute-done.13.o2_sib
  177.9 1.5 collective-permute-start.19
  179.5 29.3 %shard_map.130 = (f32[2,576,1280]{2,1,0:T(8,128)}, bf16[2,576,1280]{2,1,0:T(8,128)(2,1)}) custom-call(f32[2,576,1280]{2,1,0:T(8,128)} %get-tuple-element.69.h_ref, bf16[2,576,320]{2,1,0:T(8,128)(2,1)} %get-tuple-element.75.o0, bf16[2,576,320]{2,1,0:T(8,128)(2,1)} %get-tuple-element.76.o1, ...), custom_call_target="tpu_custom_call", output_to_operand_aliasing={{0}: (0, {})} | custom-call | flops 15099494400 | bytes 16777216 | tf_op jit(solution)/shard_map/pallas_call | solution.py:398
  208.8 31.1 %shard_map.131.h_ref = f32[2,576,1280]{2,1,0:T(8,128)} custom-call(f32[2,576,1280]{2,1,0:T(8,128)} %get-tuple-element.85.h_ref, bf16[2,576,1280]{2,1,0:T(8,128)(2,1)} %get-tuple-element.91.a_ref, f32[2,2,1280]{2,1,0:T(2,128)} %rest_0_.3, f32[2,2,1280]{2,1,0:T(2,128)} %collective-permute-done.16.rest_1_.rest_0_, ...), custom_call_target="tpu_custom_call", output_to_operand_aliasing={{}: (0, {})} | custom-call | flops 22649241600 | bytes 16777216 | tf_op jit(solution)/shard_map/pallas_call | solution.py:421
  240.6 21.4 %collective-permute-done.19.rest_2_ = bf16[1,1280,1280]{2,1,0:T(8,128)(2,1)} collective-permute-done((bf16[1,1280,1280]{2,1,0:T(8,128)(2,1)}, bf16[1,1280,1280]{2,1,0:T(8,128)(2,1)}, u32[]{:S(2)}, u32[]{:S(2)}) %collective-permute-start.19) | collective-permute-done | bytes 3276832 | tf_op jit(solution)/shard_map/ppermute | solution.py:309
  262.0 1.5 collective-permute-start.20
  263.5 0.9 dynamic-slice_bitcast_fusion.10
  264.5 1.1 dynamic-slice_bitcast_fusion.8
  265.6 0.9 pad_maximum_fusion.1
  266.9 18.7 %shard_map.132.h_ref = f32[2,576,1280]{2,1,0:T(8,128)} custom-call(f32[2,576,1280]{2,1,0:T(8,128)} %shard_map.131.h_ref, bf16[2,576,1280]{2,1,0:T(8,128)(2,1)} %get-tuple-element.91.a_ref, f32[2,2,1280]{2,1,0:T(2,128)} %collective-permute-done.20.rest_0_.b2, bf16[4,2,320,1280]{3,2,1,0:T(8,128)(2,1)} %bitcast.130, ...), custom_call_target="tpu_custom_call", output_to_operand_aliasing={{}: (0, {})} | custom-call | flops 11324620800 | bytes 16777216 | tf_op jit(solution)/shard_map/pallas_call | solution.py:421
  285.7 1.1 collective-permute-start.22
  286.8 2.7 dynamic-slice_bitcast_fusion
  290.7 20.3 %shard_map.133 = (f32[2,576,1280]{2,1,0:T(8,128)}, bf16[2,576,1280]{2,1,0:T(8,128)(2,1)}) custom-call(f32[2,576,1280]{2,1,0:T(8,128)} %shard_map.132.h_ref, bf16[2,576,1280]{2,1,0:T(8,128)(2,1)} %get-tuple-element.91.a_ref, f32[2,2,1280]{2,1,0:T(2,128)} %collective-permute-done.22.b1_ref.b3, ...), custom_call_target="tpu_custom_call", output_to_operand_aliasing={{0}: (0, {})} | custom-call | flops 11324620800 | bytes 16777216 | tf_op jit(solution)/shard_map/pallas_call | solution.py:467
  311.0 23.8 %shard_map.134 = (bf16[2,576,320]{2,1,0:T(8,128)(2,1)}, bf16[2,576,320]{2,1,0:T(8,128)(2,1)}) custom-call(bf16[2,576,1280]{2,1,0:T(8,128)(2,1)} %get-tuple-element.109.a_ref, bf16[2,960,1280]{2,1,0:T(8,128)(2,1)} %bitcast.112, bf16[2,960,1280]{2,1,0:T(8,128)(2,1)} %collective-permute-done.5.sib_ref), custom_call_target="tpu_custom_call" | custom-call | flops 12457082880 | bytes 16777216 | tf_op jit(solution)/shard_map/pallas_call | solution.py:383
  335.5 3.9 slice.169
  339.4 1.5 collective-permute-start.28
  341.0 0.7 stack.11.vec_ref
  341.6 24.1 %shard_map.135 = (bf16[2,576,320]{2,1,0:T(8,128)(2,1)}, bf16[2,576,320]{2,1,0:T(8,128)(2,1)}) custom-call(bf16[2,576,1280]{2,1,0:T(8,128)(2,1)} %get-tuple-element.109.a_ref, bf16[4,240,1280]{2,1,0:T(8,128)(2,1)} %bitcast.139, bf16[4,240,1280]{2,1,0:T(8,128)(2,1)} %collective-permute-done.26.sib_ref), custom_call_target="tpu_custom_call" | custom-call | flops 12457082880 | bytes 16777216 | tf_op jit(solution)/shard_map/pallas_call | solution.py:383
  365.8 30.4 %shard_map.136 = (f32[2,576,1280]{2,1,0:T(8,128)}, bf16[2,576,1280]{2,1,0:T(8,128)(2,1)}) custom-call(f32[2,576,1280]{2,1,0:T(8,128)} %get-tuple-element.98.h_ref, bf16[2,576,320]{2,1,0:T(8,128)(2,1)} %get-tuple-element.107.o0, bf16[2,576,320]{2,1,0:T(8,128)(2,1)} %get-tuple-element.108.o1, ...), custom_call_target="tpu_custom_call", output_to_operand_aliasing={{0}: (0, {})} | custom-call | flops 15099494400 | bytes 16777216 | tf_op jit(solution)/shard_map/pallas_call | solution.py:398
  396.2 18.3 %shard_map.137.h_ref = f32[2,576,1280]{2,1,0:T(8,128)} custom-call(f32[2,576,1280]{2,1,0:T(8,128)} %get-tuple-element.114.h_ref, bf16[2,576,1280]{2,1,0:T(8,128)(2,1)} %get-tuple-element.119.a_ref, f32[2,2,1280]{2,1,0:T(2,128)} %rest_0_.3, bf16[2,2,1280,1280]{3,2,1,0:T(8,128)(2,1)} %bitcast.106.rest_2_.rest_1_, ...), custom_call_target="tpu_custom_call", output_to_operand_aliasing={{}: (0, {})} | custom-call | flops 11324620800 | bytes 16777216 | tf_op jit(solution)/shard_map/pallas_call | solution.py:421
  415.1 18.3 %shard_map.138.h_ref = f32[2,576,1280]{2,1,0:T(8,128)} custom-call(f32[2,576,1280]{2,1,0:T(8,128)} %shard_map.137.h_ref, bf16[2,576,1280]{2,1,0:T(8,128)(2,1)} %get-tuple-element.119.a_ref, f32[2,2,1280]{2,1,0:T(2,128)} %collective-permute-done.16.rest_1_.rest_0_, ...), custom_call_target="tpu_custom_call", output_to_operand_aliasing={{}: (0, {})} | custom-call | flops 11324620800 | bytes 16777216 | tf_op jit(solution)/shard_map/pallas_call | solution.py:421
  433.4 21.3 %shard_map.139 = bf16[2,2,144,1280]{3,2,1,0:T(8,128)(2,1)} custom-call(f32[2,576,1280]{2,1,0:T(8,128)} %shard_map.138.h_ref, bf16[2,576,1280]{2,1,0:T(8,128)(2,1)} %get-tuple-element.119.a_ref, f32[2,2,1280]{2,1,0:T(2,128)} %collective-permute-done.20.rest_0_.b2, f32[2,2,1280]{2,1,0:T(2,128)} %collective-permute-done.22.b1_ref.b3, ...), custom_call_target="tpu_custom_call" | custom-call | flops 11324620800 | bytes 16777216 | tf_op jit(solution)/shard_map/pallas_call | solution.py:483
  454.7 2.5 slice_bitcast_fusion.1
  457.7 1.0 collective-permute-start.32
  458.7 21.3 %shard_map.140 = bf16[2,2,144,1280]{3,2,1,0:T(8,128)(2,1)} custom-call(f32[2,576,1280]{2,1,0:T(8,128)} %shard_map.138.h_ref, bf16[2,576,1280]{2,1,0:T(8,128)(2,1)} %get-tuple-element.119.a_ref, f32[2,2,1280]{2,1,0:T(2,128)} %collective-permute-done.20.rest_0_.b2, f32[2,2,1280]{2,1,0:T(2,128)} %collective-permute-done.22.b1_ref.b3, ...), custom_call_target="tpu_custom_call" | custom-call | flops 11324620800 | bytes 16777216 | tf_op jit(solution)/shard_map/pallas_call | solution.py:483
  480.2 1.2 copy-done.2
  481.5 0.8 collective-permute-start.33
  482.2 1.2 bitcast_dynamic-update-slice_fusion.2
  483.4 7.5 %collective-permute-done.32 = bf16[2,144,1280]{2,1,0:T(8,128)(2,1)} collective-permute-done((bf16[2,144,1280]{2,1,0:T(8,128)(2,1)}, bf16[2,144,1280]{2,1,0:T(8,128)(2,1)}, u32[]{:S(2)}, u32[]{:S(2)}) %collective-permute-start.32) | collective-permute-done | bytes 737312 | tf_op jit(solution)/shard_map/ppermute | solution.py:309
  490.9 1.2 bitcast_dynamic-update-slice_fusion.1
  492.2 1.6 copy-done
  (94 shorter events, 8.8 us)
Async XLA Ops:
  6.5 86.0 %all-gather.7.cloned.1.call-start = ((), (), s32[]{:S(2)}) async-start(), calls=%async_computation | async-start | bytes 3072000 | tf_op jit(solution)/shard_map/all_gather | solution.py:333
  8.9 17.3 %collective-permute-start.3 = (bf16[240,1280]{1,0:T(8,128)(2,1)}, bf16[240,1280]{1,0:T(8,128)(2,1)S(1)}, u32[]{:S(2)}, u32[]{:S(2)}) collective-permute-start(bf16[240,1280]{1,0:T(8,128)(2,1)} %get-tuple-element.125), channel_id=1, source_target_pairs={{0,2},{1,3},{2,0},{3,1},{4,6},{5,7},{6,4},{7,5},{8,10},{9,11},{10,... | collective-permute-start | bytes 1843208 | tf_op jit(solution)/shard_map/ppermute | solution.py:309
  26.2 0.8 copy-start.3
  27.0 13.1 %copy-start.1 = (bf16[8,6,24,1280]{3,2,1,0:T(8,128)(2,1)S(1)}, bf16[8,6,24,1280]{3,2,1,0:T(8,128)(2,1)}, u32[]{:S(2)}) copy-start(bf16[8,6,24,1280]{3,2,1,0:T(8,128)(2,1)} %param.13) | copy-start | bytes 8847364
  27.0 132.5 %all-gather.9.cloned.1.call-start = ((), (), s32[]{:S(2)}) async-start(), calls=%async_computation.1 | async-start | bytes 3072000 | tf_op jit(solution)/shard_map/all_gather | solution.py:333
  27.1 65.5 %collective-permute-start.5 = (bf16[2,960,1280]{2,1,0:T(8,128)(2,1)}, bf16[2,960,1280]{2,1,0:T(8,128)(2,1)}, u32[]{:S(2)}, u32[]{:S(2)}) collective-permute-start(bf16[2,960,1280]{2,1,0:T(8,128)(2,1)} %bitcast.110), channel_id=1, source_target_pairs={{0,1},{1,0},{2,3},{3,2},{4,5},{5,4},{6,7},{7,6},{8,9},{9,8},{10,11... | collective-permute-start | bytes 14745608 | tf_op jit(solution)/shard_map/ppermute | solution.py:309
  39.8 169.0 %collective-permute-start.17 = (bf16[2,2,1280,1280]{3,2,1,0:T(8,128)(2,1)}, bf16[2,2,1280,1280]{3,2,1,0:T(8,128)(2,1)}, u32[]{:S(2)}, u32[]{:S(2)}) collective-permute-start(bf16[2,2,1280,1280]{3,2,1,0:T(8,128)(2,1)} %bitcast.106.rest_2_.rest_1_), channel_id=1, source_target_pairs={{0,1},{1,0},{2,3},{3,2},{4,5},{5,4},{6,7},{7,6},{8,9},{9,8},{10,11... | collective-permute-start | bytes 39321608 | tf_op jit(solution)/shard_map/ppermute | solution.py:309
  41.8 19.3 %collective-permute-start = (bf16[2,144,1280]{2,1,0:T(8,128)(2,1)}, bf16[2,144,1280]{2,1,0:T(8,128)(2,1)}, u32[]{:S(2)}, u32[]{:S(2)}) collective-permute-start(bf16[2,144,1280]{2,1,0:T(8,128)(2,1)} %get-tuple-element.129), channel_id=1, source_target_pairs={{0,1},{1,0},{2,3},{3,2},{4,5},{5,4},{6,7},{7,6},{8,9},{9,8},{10,11... | collective-permute-start | bytes 2211848 | tf_op jit(solution)/shard_map/ppermute | solution.py:309
  42.0 23.6 %collective-permute-start.1 = (bf16[2,144,1280]{2,1,0:T(8,128)(2,1)}, bf16[2,144,1280]{2,1,0:T(8,128)(2,1)}, u32[]{:S(2)}, u32[]{:S(2)}) collective-permute-start(bf16[2,144,1280]{2,1,0:T(8,128)(2,1)} %get-tuple-element.128), channel_id=1, source_target_pairs={{0,2},{1,3},{2,0},{3,1},{4,6},{5,7},{6,4},{7,5},{8,10},{9,11},{10,... | collective-permute-start | bytes 2211848 | tf_op jit(solution)/shard_map/ppermute | solution.py:309
  43.8 33.0 %collective-permute-start.2 = (bf16[2,144,1280]{2,1,0:T(8,128)(2,1)}, bf16[2,144,1280]{2,1,0:T(8,128)(2,1)}, u32[]{:S(2)}, u32[]{:S(2)}) collective-permute-start(bf16[2,144,1280]{2,1,0:T(8,128)(2,1)} %get-tuple-element.127), channel_id=1, source_target_pairs={{0,3},{1,2},{2,1},{3,0},{4,7},{5,6},{6,5},{7,4},{8,11},{9,10},{10,... | collective-permute-start | bytes 2211848 | tf_op jit(solution)/shard_map/ppermute | solution.py:309
  61.1 30.0 %collective-permute-start.4 = (bf16[240,1280]{1,0:T(8,128)(2,1)}, bf16[240,1280]{1,0:T(8,128)(2,1)}, u32[]{:S(2)}, u32[]{:S(2)}) collective-permute-start(bf16[240,1280]{1,0:T(8,128)(2,1)} %pad_maximum_fusion), channel_id=1, source_target_pairs={{0,2},{1,3},{2,0},{3,1},{4,6},{5,7},{6,4},{7,5},{8,10},{9,11},{10,... | collective-permute-start | bytes 1843208 | tf_op jit(solution)/shard_map/ppermute | solution.py:309
  91.1 148.9 %all-gather.11.cloned.1.call-start = ((), (), s32[]{:S(2)}) async-start(), calls=%async_computation.2 | async-start | bytes 8192000 | tf_op jit(solution)/shard_map/all_gather | solution.py:333
  91.4 38.6 %collective-permute-start.6 = (bf16[2,320,1280]{2,1,0:T(8,128)(2,1)}, bf16[2,320,1280]{2,1,0:T(8,128)(2,1)}, u32[]{:S(2)}, u32[]{:S(2)}) collective-permute-start(bf16[2,320,1280]{2,1,0:T(8,128)(2,1)} %dynamic-slice_bitcast_fusion.1), channel_id=1, source_target_pairs={{0,2},{1,3},{2,0},{3,1},{4,6},{5,7},{6,4},{7,5},{8,10},{9,11},{10,... | collective-permute-start | bytes 4915208 | tf_op jit(solution)/shard_map/ppermute | solution.py:309
  130.0 181.0 %all-gather.13.cloned.1.call-start = ((), (), s32[]{:S(2)}) async-start(), calls=%async_computation.3 | async-start | bytes 3072000 | tf_op jit(solution)/shard_map/all_gather | solution.py:333
  130.3 5.1 %collective-permute-start.7 = (bf16[4,240,1280]{2,1,0:T(8,128)(2,1)}, bf16[4,240,1280]{2,1,0:T(8,128)(2,1)}, u32[]{:S(2)}, u32[]{:S(2)}) collective-permute-start(bf16[4,240,1280]{2,1,0:T(8,128)(2,1)} %bitcast.134), channel_id=1, source_target_pairs={{0,1},{1,0},{2,3},{3,2},{4,5},{5,4},{6,7},{7,6},{8,9},{9,8},{10,11... | collective-permute-start | bytes 7372808 | tf_op jit(solution)/shard_map/ppermute | solution.py:309
  130.3 78.5 %collective-permute-start.18 = (bf16[2,1280,1280]{2,1,0:T(8,128)(2,1)}, bf16[2,1280,1280]{2,1,0:T(8,128)(2,1)}, u32[]{:S(2)}, u32[]{:S(2)}) collective-permute-start(bf16[2,1280,1280]{2,1,0:T(8,128)(2,1)} %rest_2_.1), channel_id=1, source_target_pairs={{0,1},{1,0},{2,3},{3,2},{4,5},{5,4},{6,7},{7,6},{8,9},{9,8},{10,11... | collective-permute-start | bytes 19660808 | tf_op jit(solution)/shard_map/ppermute | solution.py:309
  130.8 28.8 %collective-permute-start.10 = (bf16[2,2,80,640]{3,2,1,0:T(8,128)(2,1)}, bf16[2,2,80,640]{3,2,1,0:T(8,128)(2,1)}, u32[]{:S(2)}, u32[]{:S(2)}) collective-permute-start(bf16[2,2,80,640]{3,2,1,0:T(8,128)(2,1)} %get-tuple-element.131), channel_id=1, source_target_pairs={{0,3},{1,2},{2,1},{3,0},{4,7},{5,6},{6,5},{7,4},{8,11},{9,10},{10,... | collective-permute-start | bytes 1228808 | tf_op jit(solution)/shard_map/ppermute | solution.py:309
  132.0 28.0 %collective-permute-start.8 = (bf16[2,2,80,640]{3,2,1,0:T(8,128)(2,1)}, bf16[2,2,80,640]{3,2,1,0:T(8,128)(2,1)}, u32[]{:S(2)}, u32[]{:S(2)}) collective-permute-start(bf16[2,2,80,640]{3,2,1,0:T(8,128)(2,1)} %get-tuple-element.132), channel_id=1, source_target_pairs={{0,1},{1,0},{2,3},{3,2},{4,5},{5,4},{6,7},{7,6},{8,9},{9,8},{10,11... | collective-permute-start | bytes 1228808 | tf_op jit(solution)/shard_map/ppermute | solution.py:309
  135.3 36.4 %collective-permute-start.11 = (bf16[2,320,1280]{2,1,0:T(8,128)(2,1)}, bf16[2,320,1280]{2,1,0:T(8,128)(2,1)}, u32[]{:S(2)}, u32[]{:S(2)}) collective-permute-start(bf16[2,320,1280]{2,1,0:T(8,128)(2,1)} %bitcast.114), channel_id=1, source_target_pairs={{0,1},{1,0},{2,3},{3,2},{4,5},{5,4},{6,7},{7,6},{8,9},{9,8},{10,11... | collective-permute-start | bytes 4915208 | tf_op jit(solution)/shard_map/ppermute | solution.py:309
  159.6 19.9 %collective-permute-start.14 = (bf16[4,240,1280]{2,1,0:T(8,128)(2,1)}, bf16[4,240,1280]{2,1,0:T(8,128)(2,1)}, u32[]{:S(2)}, u32[]{:S(2)}) collective-permute-start(bf16[4,240,1280]{2,1,0:T(8,128)(2,1)} %bitcast.136), channel_id=1, source_target_pairs={{0,1},{1,0},{2,3},{3,2},{4,5},{5,4},{6,7},{7,6},{8,9},{9,8},{10,11... | collective-permute-start | bytes 7372808 | tf_op jit(solution)/shard_map/ppermute | solution.py:309
  160.0 11.7 %collective-permute-start.9 = (bf16[2,2,80,640]{3,2,1,0:T(8,128)(2,1)}, bf16[2,2,80,640]{3,2,1,0:T(8,128)(2,1)S(1)}, u32[]{:S(2)}, u32[]{:S(2)}) collective-permute-start(bf16[2,2,80,640]{3,2,1,0:T(8,128)(2,1)} %get-tuple-element.133), channel_id=1, source_target_pairs={{0,2},{1,3},{2,0},{3,1},{4,6},{5,7},{6,4},{7,5},{8,10},{9,11},{10,... | collective-permute-start | bytes 1228808 | tf_op jit(solution)/shard_map/ppermute | solution.py:309
  171.7 0.8 copy-start.13
  171.7 3.8 collective-permute-start.12
  172.5 5.4 %collective-permute-start.13 = (bf16[2,320,1280]{2,1,0:T(8,128)(2,1)}, bf16[2,320,1280]{2,1,0:T(8,128)(2,1)}, u32[]{:S(2)}, u32[]{:S(2)}) collective-permute-start(bf16[2,320,1280]{2,1,0:T(8,128)(2,1)} %bitcast.124), channel_id=1, source_target_pairs={{0,1},{1,0},{2,3},{3,2},{4,5},{5,4},{6,7},{7,6},{8,9},{9,8},{10,11... | collective-permute-start | bytes 4915208 | tf_op jit(solution)/shard_map/ppermute | solution.py:309
  175.6 33.2 %collective-permute-start.15 = (bf16[240,1280]{1,0:T(8,128)(2,1)}, bf16[240,1280]{1,0:T(8,128)(2,1)}, u32[]{:S(2)}, u32[]{:S(2)}) collective-permute-start(bf16[240,1280]{1,0:T(8,128)(2,1)} %get-tuple-element.126), channel_id=1, source_target_pairs={{0,2},{1,3},{2,0},{3,1},{4,6},{5,7},{6,4},{7,5},{8,10},{9,11},{10,... | collective-permute-start | bytes 1843208 | tf_op jit(solution)/shard_map/ppermute | solution.py:309
  177.9 84.1 %collective-permute-start.19 = (bf16[1,1280,1280]{2,1,0:T(8,128)(2,1)}, bf16[1,1280,1280]{2,1,0:T(8,128)(2,1)}, u32[]{:S(2)}, u32[]{:S(2)}) collective-permute-start(bf16[1,1280,1280]{2,1,0:T(8,128)(2,1)} %slice.137), channel_id=1, source_target_pairs={{0,2},{1,3},{2,0},{3,1},{4,6},{5,7},{6,4},{7,5},{8,10},{9,11},{10,... | collective-permute-start | bytes 9830408 | tf_op jit(solution)/shard_map/ppermute | solution.py:309
  179.5 29.4 %collective-permute-start.16 = (f32[2,2,1280]{2,1,0:T(2,128)}, f32[2,2,1280]{2,1,0:T(2,128)}, u32[]{:S(2)}, u32[]{:S(2)}) collective-permute-start(f32[2,2,1280]{2,1,0:T(2,128)} %rest_0_.3), channel_id=1, source_target_pairs={{0,1},{1,0},{2,3},{3,2},{4,5},{5,4},{6,7},{7,6},{8,9},{9,8},{10,11... | collective-permute-start | bytes 61448 | tf_op jit(solution)/shard_map/ppermute | solution.py:309
  240.0 50.7 %collective-permute-start.23 = (bf16[4,2,320,1280]{3,2,1,0:T(8,128)(2,1)}, bf16[4,2,320,1280]{3,2,1,0:T(8,128)(2,1)}, u32[]{:S(2)}, u32[]{:S(2)}) collective-permute-start(bf16[4,2,320,1280]{3,2,1,0:T(8,128)(2,1)} %bitcast.129), channel_id=1, source_target_pairs={{0,1},{1,0},{2,3},{3,2},{4,5},{5,4},{6,7},{7,6},{8,9},{9,8},{10,11... | collective-permute-start | bytes 19660808 | tf_op jit(solution)/shard_map/ppermute | solution.py:309
  240.6 94.3 %all-gather.15.cloned.1.call-start = ((), (), s32[]{:S(2)}) async-start(), calls=%async_computation.4 | async-start | bytes 3072000 | tf_op jit(solution)/shard_map/all_gather | solution.py:333
  262.0 28.7 %collective-permute-start.24 = (bf16[1,1280,1280]{2,1,0:T(8,128)(2,1)}, bf16[1,1280,1280]{2,1,0:T(8,128)(2,1)}, u32[]{:S(2)}, u32[]{:S(2)}) collective-permute-start(bf16[1,1280,1280]{2,1,0:T(8,128)(2,1)} %collective-permute-done.19.rest_2_), channel_id=1, source_target_pairs={{0,1},{1,0},{2,3},{3,2},{4,5},{5,4},{6,7},{7,6},{8,9},{9,8},{10,11... | collective-permute-start | bytes 9830408 | tf_op jit(solution)/shard_map/ppermute | solution.py:309
  262.0 4.9 collective-permute-start.20
  266.4 19.2 %collective-permute-start.21 = (bf16[240,1280]{1,0:T(8,128)(2,1)}, bf16[240,1280]{1,0:T(8,128)(2,1)}, u32[]{:S(2)}, u32[]{:S(2)}) collective-permute-start(bf16[240,1280]{1,0:T(8,128)(2,1)} %pad_maximum_fusion.1), channel_id=1, source_target_pairs={{0,2},{1,3},{2,0},{3,1},{4,6},{5,7},{6,4},{7,5},{8,10},{9,11},{10,... | collective-permute-start | bytes 1843208 | tf_op jit(solution)/shard_map/ppermute | solution.py:309
  285.6 4.4 copy-start.10
  285.6 4.4 copy-start.11
  285.6 4.4 copy-start.12
  285.7 128.9 %all-gather.17.cloned.1.call-start = ((), (), s32[]{:S(2)}) async-start(), calls=%async_computation.5 | async-start | bytes 8192000 | tf_op jit(solution)/shard_map/all_gather | solution.py:333
  285.7 5.0 collective-permute-start.22
  289.5 45.3 %collective-permute-start.25 = (bf16[2,320,1280]{2,1,0:T(8,128)(2,1)}, bf16[2,320,1280]{2,1,0:T(8,128)(2,1)}, u32[]{:S(2)}, u32[]{:S(2)}) collective-permute-start(bf16[2,320,1280]{2,1,0:T(8,128)(2,1)} %dynamic-slice_bitcast_fusion), channel_id=1, source_target_pairs={{0,2},{1,3},{2,0},{3,1},{4,6},{5,7},{6,4},{7,5},{8,10},{9,11},{10,... | collective-permute-start | bytes 4915208 | tf_op jit(solution)/shard_map/ppermute | solution.py:309
  334.9 6.8 %collective-permute-start.26 = (bf16[4,240,1280]{2,1,0:T(8,128)(2,1)}, bf16[4,240,1280]{2,1,0:T(8,128)(2,1)}, u32[]{:S(2)}, u32[]{:S(2)}) collective-permute-start(bf16[4,240,1280]{2,1,0:T(8,128)(2,1)} %bitcast.138), channel_id=1, source_target_pairs={{0,1},{1,0},{2,3},{3,2},{4,5},{5,4},{6,7},{7,6},{8,9},{9,8},{10,11... | collective-permute-start | bytes 7372808 | tf_op jit(solution)/shard_map/ppermute | solution.py:309
  335.2 5.7 %copy-start.4 = (f32[1,1280]{1,0:T(1,128)S(1)}, f32[1,1280]{1,0:T(1,128)}, u32[]{:S(2)}) copy-start(f32[1,1280]{1,0:T(1,128)} %get-tuple-element.140) | copy-start | bytes 15364
  335.2 5.7 %copy-start.5 = (f32[1,1280]{1,0:T(1,128)S(1)}, f32[1,1280]{1,0:T(1,128)}, u32[]{:S(2)}) copy-start(f32[1,1280]{1,0:T(1,128)} %get-tuple-element.141) | copy-start | bytes 15364
  335.2 5.7 %copy-start.6 = (f32[1,1280]{1,0:T(1,128)S(1)}, f32[1,1280]{1,0:T(1,128)}, u32[]{:S(2)}) copy-start(f32[1,1280]{1,0:T(1,128)} %get-tuple-element.142) | copy-start | bytes 15364
  335.2 5.7 %copy-start.7 = (f32[1,1280]{1,0:T(1,128)S(1)}, f32[1,1280]{1,0:T(1,128)}, u32[]{:S(2)}) copy-start(f32[1,1280]{1,0:T(1,128)} %get-tuple-element.143) | copy-start | bytes 15364
  335.2 5.7 %copy-start.8 = (f32[1,1280]{1,0:T(1,128)S(1)}, f32[1,1280]{1,0:T(1,128)}, u32[]{:S(2)}) copy-start(f32[1,1280]{1,0:T(1,128)} %get-tuple-element.144) | copy-start | bytes 15364
  335.2 5.7 %copy-start.9 = (f32[1,1280]{1,0:T(1,128)S(1)}, f32[1,1280]{1,0:T(1,128)}, u32[]{:S(2)}) copy-start(f32[1,1280]{1,0:T(1,128)} %get-tuple-element.154) | copy-start | bytes 15364
  335.2 30.5 %collective-permute-start.27 = (bf16[4,240,1280]{2,1,0:T(8,128)(2,1)}, bf16[4,240,1280]{2,1,0:T(8,128)(2,1)}, u32[]{:S(2)}, u32[]{:S(2)}) collective-permute-start(bf16[4,240,1280]{2,1,0:T(8,128)(2,1)} %bitcast.140), channel_id=1, source_target_pairs={{0,1},{1,0},{2,3},{3,2},{4,5},{5,4},{6,7},{7,6},{8,9},{9,8},{10,11... | collective-permute-start | bytes 7372808 | tf_op jit(solution)/shard_map/ppermute | solution.py:309
  339.4 75.1 %collective-permute-start.28 = (bf16[1,1280,1280]{2,1,0:T(8,128)(2,1)}, bf16[1,1280,1280]{2,1,0:T(8,128)(2,1)}, u32[]{:S(2)}, u32[]{:S(2)}) collective-permute-start(bf16[1,1280,1280]{2,1,0:T(8,128)(2,1)} %slice.169), channel_id=1, source_target_pairs={{0,2},{1,3},{2,0},{3,1},{4,6},{5,7},{6,4},{7,5},{8,10},{9,11},{10,... | collective-permute-start | bytes 9830408 | tf_op jit(solution)/shard_map/ppermute | solution.py:309
  414.5 18.8 %collective-permute-start.29 = (bf16[4,2,320,1280]{3,2,1,0:T(8,128)(2,1)}, bf16[4,2,320,1280]{3,2,1,0:T(8,128)(2,1)}, u32[]{:S(2)}, u32[]{:S(2)}) collective-permute-start(bf16[4,2,320,1280]{3,2,1,0:T(8,128)(2,1)} %bitcast.131), channel_id=1, source_target_pairs={{0,1},{1,0},{2,3},{3,2},{4,5},{5,4},{6,7},{7,6},{8,9},{9,8},{10,11... | collective-permute-start | bytes 19660808 | tf_op jit(solution)/shard_map/ppermute | solution.py:309
  414.6 18.8 %collective-permute-start.30 = (bf16[1,1280,1280]{2,1,0:T(8,128)(2,1)}, bf16[1,1280,1280]{2,1,0:T(8,128)(2,1)}, u32[]{:S(2)}, u32[]{:S(2)}) collective-permute-start(bf16[1,1280,1280]{2,1,0:T(8,128)(2,1)} %collective-permute-done.28.rest_1_), channel_id=1, source_target_pairs={{0,1},{1,0},{2,3},{3,2},{4,5},{5,4},{6,7},{7,6},{8,9},{9,8},{10,11... | collective-permute-start | bytes 9830408 | tf_op jit(solution)/shard_map/ppermute | solution.py:309
  457.3 25.0 %collective-permute-start.31 = (bf16[2,144,1280]{2,1,0:T(8,128)(2,1)}, bf16[2,144,1280]{2,1,0:T(8,128)(2,1)}, u32[]{:S(2)}, u32[]{:S(2)}) collective-permute-start(bf16[2,144,1280]{2,1,0:T(8,128)(2,1)} %get-tuple-element.138), channel_id=1, source_target_pairs={{0,2},{1,3},{2,0},{3,1},{4,6},{5,7},{6,4},{7,5},{8,10},{9,11},{10,... | collective-permute-start | bytes 2211848 | tf_op jit(solution)/shard_map/ppermute | solution.py:309
  457.7 33.2 %collective-permute-start.32 = (bf16[2,144,1280]{2,1,0:T(8,128)(2,1)}, bf16[2,144,1280]{2,1,0:T(8,128)(2,1)}, u32[]{:S(2)}, u32[]{:S(2)}) collective-permute-start(bf16[2,144,1280]{2,1,0:T(8,128)(2,1)} %get-tuple-element.137), channel_id=1, source_target_pairs={{0,3},{1,2},{2,1},{3,0},{4,7},{5,6},{6,5},{7,4},{8,11},{9,10},{10,... | collective-permute-start | bytes 2211848 | tf_op jit(solution)/shard_map/ppermute | solution.py:309
  480.0 1.4 copy-start.2
  481.5 10.6 %collective-permute-start.33 = (bf16[2,144,1280]{2,1,0:T(8,128)(2,1)S(1)}, bf16[2,144,1280]{2,1,0:T(8,128)(2,1)S(1)}, u32[]{:S(2)}, u32[]{:S(2)}) collective-permute-start(bf16[2,144,1280]{2,1,0:T(8,128)(2,1)S(1)} %get-tuple-element.135), channel_id=1, source_target_pairs={{0,1},{1,0},{2,3},{3,2},{4,5},{5,4},{6,7},{7,6},{8,9},{9,8},{10,11... | collective-permute-start | bytes 2211848 | tf_op jit(solution)/shard_map/ppermute | solution.py:309
  492.2 1.6 copy-start
Sparse Core Ops, SparseCore 0:
  27.1 35.7 all-gather.6
  91.2 35.9 all-gather.8
  130.1 69.5 all-gather.10
  240.7 34.7 all-gather.12
  285.8 35.5 all-gather.14
  335.0 69.5 all-gather.16
